TPU v7x, 32 devices: a 4x4x1 block of a 4x4x8 slice. The times are simulated.
32 devices in a mesh: dp: 1 (over z), tp: 4 (over y), ep: 8 (over x, core).
Axes of the slice: x: 4, y: 4, z: 1, core: 2. Of those that a mesh axis runs over, the one named last changes fastest.
The devices are a block of a 4x4x8 slice.
Arguments:
- hidden_in: bfloat16 [8, 1024, 4096], P(('dp', 'ep'))
- expert_ids: int32 [8, 1024, 4], P(('dp', 'ep'))
- slot_ids: int32 [8, 1024, 4], P(('dp', 'ep'))
- attn_gain: bfloat16 [4096], replicated
- w_query: bfloat16 [4096, 32, 128], P(None, 'tp')
- w_key: bfloat16 [4096, 32, 128], P(None, 'tp')
- w_value: bfloat16 [4096, 32, 128], P(None, 'tp')
- w_out: bfloat16 [32, 128, 4096], P('tp')
- ffn_gain: bfloat16 [4096], replicated
- w_gate: bfloat16 [4096, 11008], P(None, 'tp')
- w_up: bfloat16 [4096, 11008], P(None, 'tp')
- w_down: bfloat16 [11008, 4096], P('tp')
- moe_gain: bfloat16 [4096], replicated
- w_router: bfloat16 [4096, 16], replicated
- exp_gate: bfloat16 [16, 4096, 688], P('ep')
- exp_up: bfloat16 [16, 4096, 688], P('ep')
- exp_down: bfloat16 [16, 688, 4096], P('ep')
Outputs:
- output: bfloat16 [8, 1024, 4096], P(('dp', 'ep'))
All inputs are finite; a program needn't handle non-finite values.
Results may differ from a plain program's by a relative error of at most 0.00899844.
Values are sent between devices in bfloat16 or wider.
A program may use at most 768 MiB of HBM per device.

v0:
```python
import jax
import jax.numpy as jnp
from jax import lax
from jax.sharding import PartitionSpec as P

EPS = 1e-6
ROPE_BASE = 10000.0


def rms_norm(x_val, gain):
    x_f32 = x_val.astype(jnp.float32)
    inv_rms = lax.rsqrt(jnp.mean(x_f32 * x_f32, axis=-1, keepdims=True) + EPS)
    return (x_f32 * inv_rms * gain.astype(jnp.float32)).astype(jnp.bfloat16)


def rope_tables(seq_len, head_dim):
    inv_freq = ROPE_BASE ** (-jnp.arange(head_dim // 2, dtype=jnp.float32) * (2.0 / head_dim))
    angle = jnp.arange(seq_len, dtype=jnp.float32)[:, None] * inv_freq[None, :]
    return jnp.cos(angle), jnp.sin(angle)


def apply_rope(x_val, cos_tab, sin_tab):
    half_dim = x_val.shape[-1] // 2
    lower = x_val[..., :half_dim]
    upper = x_val[..., half_dim:]
    cos_b = cos_tab[:, None, :]
    sin_b = sin_tab[:, None, :]
    return jnp.concatenate([lower * cos_b - upper * sin_b, upper * cos_b + lower * sin_b], axis=-1)


def dense_branch(hidden, attn_gain, w_query, w_key, w_value, w_out, ffn_gain, w_gate, w_up, w_down):
    num_seqs, seq_len, d_model = hidden.shape
    head_dim = w_query.shape[2]
    x_norm = rms_norm(hidden, attn_gain)
    cos_tab, sin_tab = rope_tables(seq_len, head_dim)
    query = apply_rope(jnp.einsum('bsd,dhe->bshe', x_norm, w_query, preferred_element_type=jnp.float32), cos_tab, sin_tab).astype(jnp.bfloat16)
    key_proj = apply_rope(jnp.einsum('bsd,dhe->bshe', x_norm, w_key, preferred_element_type=jnp.float32), cos_tab, sin_tab).astype(jnp.bfloat16)
    value_proj = jnp.einsum('bsd,dhe->bshe', x_norm, w_value, preferred_element_type=jnp.float32).astype(jnp.bfloat16)
    scores = jnp.einsum('bqhe,bkhe->bhqk', query, key_proj, preferred_element_type=jnp.float32) * head_dim ** -0.5
    causal = jnp.arange(seq_len)[:, None] >= jnp.arange(seq_len)[None, :]
    attn_prob = jax.nn.softmax(jnp.where(causal, scores, -1e30), axis=-1).astype(jnp.bfloat16)
    context = jnp.einsum('bhqk,bkhe->bqhe', attn_prob, value_proj, preferred_element_type=jnp.float32).astype(jnp.bfloat16)
    attn_part = jnp.einsum('crif,ife->cre', context, w_out, preferred_element_type=jnp.float32)
    attn_sum = lax.psum(attn_part, 'tp')
    after_attn = (hidden.astype(jnp.float32) + attn_sum).astype(jnp.bfloat16)
    f_norm = rms_norm(after_attn, ffn_gain).reshape(num_seqs * seq_len, d_model)
    gate_pre = jnp.dot(f_norm, w_gate, preferred_element_type=jnp.float32)
    up_pre = jnp.dot(f_norm, w_up, preferred_element_type=jnp.float32)
    hidden_act = (jax.nn.silu(gate_pre) * up_pre).astype(jnp.bfloat16)
    ffn_part = jnp.dot(hidden_act, w_down, preferred_element_type=jnp.float32)
    ffn_sum = lax.psum(ffn_part, 'tp').reshape(num_seqs, seq_len, d_model)
    return after_attn.astype(jnp.float32) + ffn_sum


def expert_swiglu(x_buf, exp_gate, exp_up, exp_down):
    gate_pre = jnp.einsum('erd,edf->erf', x_buf, exp_gate, preferred_element_type=jnp.float32)
    up_pre = jnp.einsum('erd,edf->erf', x_buf, exp_up, preferred_element_type=jnp.float32)
    hidden_act = (jax.nn.silu(gate_pre) * up_pre).astype(jnp.bfloat16)
    return jnp.einsum('erf,efd->erd', hidden_act, exp_down, preferred_element_type=jnp.float32).astype(jnp.bfloat16)


def moe_branch(hidden, expert_ids, slot_ids, moe_gain, w_router, exp_gate, exp_up, exp_down):
    num_seqs, seq_len, d_model = hidden.shape
    tok_dev = num_seqs * seq_len
    top_k = expert_ids.shape[2]
    experts = w_router.shape[1]
    capacity = 3 * tok_dev * top_k // (2 * experts)
    u_norm = rms_norm(hidden, moe_gain).reshape(tok_dev, d_model)
    route_ids = expert_ids.reshape(tok_dev, top_k)
    logits = jnp.dot(u_norm, w_router, preferred_element_type=jnp.float32)
    gates = jax.nn.softmax(jnp.take_along_axis(logits, route_ids, axis=1), axis=-1)
    flat_pos = route_ids * capacity + slot_ids.reshape(tok_dev, top_k)
    token_of = jnp.broadcast_to(jnp.arange(tok_dev, dtype=jnp.int32)[:, None], (tok_dev, top_k))
    row_token = jnp.full((experts * capacity,), tok_dev, jnp.int32).at[flat_pos.reshape(-1)].set(token_of.reshape(-1))
    send_buf = jnp.take(u_norm, row_token, axis=0, mode='fill', fill_value=0).reshape(experts, capacity, d_model)
    recv_buf = lax.all_to_all(send_buf, 'ep', 0, 1, tiled=True)
    expert_out = expert_swiglu(recv_buf, exp_gate, exp_up, exp_down)
    returned = lax.all_to_all(expert_out, 'ep', 1, 0, tiled=True).reshape(experts * capacity, d_model)
    per_copy = jnp.take(returned, flat_pos, axis=0)
    moe_out = jnp.sum(gates[:, :, None] * per_copy.astype(jnp.float32), axis=1)
    return moe_out.reshape(num_seqs, seq_len, d_model)


def solution(mesh):
    tok_spec = P(('dp', 'ep'), None, None)
    col_spec = P(None, 'tp', None)
    exp_spec = P('ep', None, None)
    in_specs = (tok_spec, tok_spec, tok_spec, P(None), col_spec, col_spec, col_spec, P('tp', None, None), P(None), P(None, 'tp'), P(None, 'tp'), P('tp', None), P(None), P(None, None), exp_spec, exp_spec, exp_spec)

    def layer_local(hidden_in, expert_ids, slot_ids, attn_gain, w_query, w_key, w_value, w_out, ffn_gain, w_gate, w_up, w_down, moe_gain, w_router, exp_gate, exp_up, exp_down):
        moe_out = moe_branch(hidden_in, expert_ids, slot_ids, moe_gain, w_router, exp_gate, exp_up, exp_down)
        dense_out = dense_branch(hidden_in, attn_gain, w_query, w_key, w_value, w_out, ffn_gain, w_gate, w_up, w_down)
        return (dense_out + moe_out).astype(jnp.bfloat16)

    return jax.shard_map(layer_local, mesh=mesh, in_specs=in_specs, out_specs=tok_spec, check_vma=False)
```

profile of v0, /device:TPU:97, one launch (start us, length us, event | category | flops | bytes accessed | tf_op | source)
XLA Modules:
  0.0 2250.4 jit_solution(8682768617255085205)
XLA Ops:
  6.5 0.0 copy-start
  6.6 0.0 all-reduce.3.cloned.1.call-start
  6.6 1.4 iota_compare_fusion
  7.9 5.1 fusion.6
  13.0 0.7 convert_element_type.71
  13.7 11.9 copy.42
  25.6 12.0 copy.41
  37.6 13.0 fusion.23
  50.7 0.0 copy-done.4
  50.7 0.0 slice-start.1
  50.7 13.2 fusion.21
  63.9 1.0 fusion.46
  64.9 0.0 slice-done
  64.9 0.0 copy-start.5
  64.9 14.1 fusion.19
  79.0 3.3 fusion.38
  82.4 14.2 fusion.73
  96.5 19.5 fusion.16
  116.1 16.3 convolution_bitcast_fusion.1
  132.4 0.1 all-reduce.3.cloned.1.call-update
  132.4 0.6 copy-done.13
  133.0 0.0 copy-done.8
  133.1 0.0 copy-done.10
  133.1 0.2 copy.51
  133.3 0.3 add.150
  133.7 0.3 reshape.382
  134.0 15.5 scatter_custom_fusion
  149.6 276.8 %all-reduce.3.cloned.1.call-done = f32[1,1024,4096]{2,1,0:T(8,128)} async-done(((f32[1,1024,4096]{2,1,0:T(8,128)}), f32[1,1024,4096]{2,1,0:T(8,128)}) %all-reduce.3.cloned.1.call-update) | async-done | bytes 16777232 | tf_op jit(solution)/shard_map/psum | solution.py:44
  426.4 16.6 fusion.8
  443.0 87.4 %gather_fusion = bf16[6144,4096]{1,0:T(8,128)(2,1)} fusion(bf16[1024,4096]{1,0:T(8,128)(2,1)} %get-tuple-element.7, s32[6144]{0:T(1024)S(1)} %fusion.47), kind=kCustom, calls=%fused_computation | custom fusion | bytes 100687872 | tf_op jit(solution)/shard_map/jit(_take)/gather | solution.py:75
  530.4 33.2 %broadcast_select_fusion = bf16[16,384,4096]{2,1,0:T(8,128)(2,1)} fusion(bf16[16,384,4096]{2,1,0:T(8,128)(2,1)} %bitcast.105, pred[16,384]{1,0:T(8,128)(4,1)S(1)} %broadcast_in_dim.67), kind=kLoop, calls=%fused_computation.6 | loop fusion | flops 25165824 | bytes 100669440 | tf_op jit(solution)/shard_map/jit(_take)/select_n | solution.py:75
  563.6 558.7 %all_to_all.33 = bf16[16,384,4096]{2,1,0:T(8,128)(2,1)} all-to-all(bf16[16,384,4096]{2,1,0:T(8,128)(2,1)} %broadcast_select_fusion), channel_id=1, replica_groups=mesh['dp'=1,'tp'=4,'ep'=8] {'ep'}, dimensions={0} | all-to-all | bytes 100663296 | tf_op jit(solution)/shard_map/all_to_all | solution.py:76
  1122.3 33.2 %copy.52 = bf16[2,8,384,4096]{3,2,1,0:T(8,128)(2,1)} copy(bf16[2,8,384,4096]{3,2,0,1:T(8,128)(2,1)} %bitcast.106) | data formatting | bytes 100663296 | tf_op jit(solution)/shard_map/all_to_all | solution.py:76
  1155.6 44.3 %fusion.75 = f32[2,3072,688]{1,2,0:T(8,128)} fusion(bf16[2,3072,4096]{2,1,0:T(8,128)(2,1)} %bitcast.107, bf16[2,4096,688]{1,2,0:T(8,128)(2,1)} %param.31), kind=kOutput, calls=%fused_computation.104 | convolution fusion | flops 34628173824 | bytes 78512128 | tf_op jit(solution)/shard_map/erd,edf->erf/dot_general | solution.py:56
  1199.9 46.2 %multiply_convert_fusion = bf16[2,3072,688]{1,2,0:T(8,128)(2,1)} fusion(f32[2,3072,688]{1,2,0:T(8,128)} %fusion.75, bf16[2,3072,4096]{2,1,0:T(8,128)(2,1)} %bitcast.108, bf16[2,4096,688]{1,2,0:T(8,128)(2,1)} %param.32), kind=kOutput, calls=%fused_computation.20 | convolution fusion | flops 34653536256 | bytes 86966272 | tf_op jit(solution)/shard_map/erd,edf->erf/dot_general | solution.py:57
  1246.1 49.0 %convolution_convert_fusion = bf16[2,3072,4096]{2,1,0:T(8,128)(2,1)} fusion(bf16[2,3072,688]{1,2,0:T(8,128)(2,1)} %multiply_convert_fusion, bf16[2,688,4096]{2,1,0:T(8,128)(2,1)} %param.33), kind=kOutput, calls=%fused_computation.10 | convolution fusion | flops 34653339648 | bytes 70057984 | tf_op jit(solution)/shard_map/erf,efd->erd/dot_general | solution.py:59
  1295.1 89.2 %copy.53 = bf16[2,3072,4096]{2,0,1:T(2,128)(2,1)} copy(bf16[2,3072,4096]{2,1,0:T(8,128)(2,1)} %convolution_convert_fusion) | data formatting | bytes 100663296 | tf_op jit(solution)/shard_map/convert_element_type | solution.py:59
  1384.3 9.5 all-to-all-start.1
  1393.8 29.7 %fusion.33 = f32[1024,2752]{0,1:T(8,128)S(1)} fusion(bf16[4096,2752]{0,1:T(8,128)(2,1)} %param.26, bf16[1,1024,4096]{2,1,0:T(8,128)(2,1)} %get-tuple-element.6, f32[4096]{0:T(1024)S(1)} %convert_element_type.80, f32[1024]{0:T(1024)S(1)} %add_rsqrt_fusion), kind=kOutput, calls=%fused_computation.48 | convolution fusion | flops 23102226432 | bytes 42225664 | tf_op jit(solution)/shard_map/dot_general | solution.py:47
  1423.5 30.6 %multiply_convert_fusion.1 = bf16[1024,2752]{0,1:T(8,128)(2,1)S(1)} fusion(f32[1024,2752]{0,1:T(8,128)S(1)} %fusion.33, bf16[4096,2752]{0,1:T(8,128)(2,1)} %param.27, bf16[1,1024,4096]{2,1,0:T(8,128)(2,1)} %get-tuple-element.6, f32[4096]{0:T(1024)S(1)} %convert_element_type.80, f32[1024]{0:T(1024)S(1)} %add_rsqrt_fusion), kind=kOutput, calls=%fused_computation.34 | convolution fusion | flops 23119134720 | bytes 47861760 | tf_op jit(solution)/shard_map/dot_general | solution.py:48
  1454.1 30.3 %convolution_bitcast_fusion = f32[1,1024,4096]{2,1,0:T(8,128)} fusion(bf16[1024,2752]{0,1:T(8,128)(2,1)S(1)} %multiply_convert_fusion.1, bf16[2752,4096]{1,0:T(8,128)(2,1)} %param.28), kind=kOutput, calls=%fused_computation.35 | convolution fusion | flops 23085449216 | bytes 44957696 | tf_op jit(solution)/shard_map/dot_general | solution.py:50
  1484.4 0.1 all-reduce.5.cloned.1.call-update
  1484.5 0.7 copy-done.11
  1485.1 0.2 copy.48
  1485.4 0.2 copy.50
  1485.7 0.2 copy.55
  1485.9 0.3 reshape.366
  1486.2 0.2 copy.49
  1486.4 0.3 reshape.372
  1486.7 0.6 broadcast_clamp_fusion
  1487.3 0.8 compare_and_fusion
  1488.1 0.0 copy-done
  1488.1 5.6 fusion.74
  1493.7 33.0 %gather_fusion.2 = f32[4096]{0:T(1024)S(1)} fusion(f32[1024,16]{0,1:T(8,128)S(1)} %fusion.74, s32[4096]{0:T(1024)S(1)} %reshape.372), kind=kCustom, calls=%fused_computation.2 | custom fusion | bytes 65536 | tf_op jit(solution)/shard_map/jit(take_along_axis)/gather | solution.py:71
  1526.8 0.5 reshape.375
  1527.3 0.2 fusion.68
  1527.6 0.4 fusion.44
  1528.0 0.3 fusion.43
  1528.3 408.5 %all-to-all-done.1 = bf16[2,3072,4096]{2,0,1:T(2,128)(2,1)} async-done(((bf16[2,3072,4096]{2,0,1:T(2,128)(2,1)}), bf16[2,3072,4096]{2,0,1:T(2,128)(2,1)}, u32[]{:S(2)}, u32[]{:S(2)}) %all-to-all-start.1) | async-done | bytes 50331680 | tf_op jit(solution)/shard_map/all_to_all | solution.py:78
  1936.8 43.3 %copy.54 = bf16[2,8,384,4096]{3,2,0,1:T(8,128)(2,1)} copy(bf16[2,8,384,4096]{3,0,2,1:T(2,128)(2,1)} %bitcast.30) | data formatting | bytes 100663296 | tf_op jit(solution)/shard_map/all_to_all | solution.py:78
  1980.1 132.2 %gather_fusion.1 = bf16[4096,4096]{1,0:T(8,128)(2,1)} fusion(bf16[6144,4096]{1,0:T(8,128)(2,1)} %bitcast.104, s32[4096]{0:T(1024)S(1)} %copy-done.1), kind=kCustom, calls=%fused_computation.1 | custom fusion | bytes 67125248 | tf_op jit(solution)/shard_map/jit(_take)/gather | solution.py:79
  2112.3 48.4 %reshape.365 = bf16[1024,4,4096]{2,1,0:T(4,128)(2,1)} reshape(bf16[4096,4096]{1,0:T(8,128)(2,1)} %gather_fusion.1) | data formatting | bytes 67108864 | tf_op jit(solution)/shard_map/jit(_take)/gather | solution.py:79
  2160.8 64.5 %multiply_reduce_fusion = f32[1024,4096]{1,0:T(8,128)} fusion(bf16[1024,4,4096]{2,1,0:T(4,128)(2,1)} %reshape.365, f32[1024,4]{1,0:T(8,128)S(1)} %fusion.43, pred[1024,4]{1,0:T(8,128)(4,1)S(1)} %copy-done.7), kind=kLoop, calls=%fused_computation.5 | loop fusion | flops 62914560 | bytes 50352128 | tf_op jit(solution)/shard_map/reduce_sum | solution.py:80
  2225.3 17.8 fusion.12
  (39 shorter events, 0.2 us)
Async XLA Ops:
  6.5 1481.6 %copy-start = (bf16[4096,16]{0,1:T(8,128)(2,1)S(1)}, bf16[4096,16]{0,1:T(8,128)(2,1)}, u32[]{:S(2)}) copy-start(bf16[4096,16]{0,1:T(8,128)(2,1)} %param.30) | copy-start | bytes 393220
  6.6 419.9 %all-reduce.3.cloned.1.call-start = ((), (), s32[]{:S(2)}) async-start(), calls=%async_computation.2 | async-start | bytes 33554432 | tf_op jit(solution)/shard_map/psum | solution.py:44
  37.6 13.0 copy-start.4
  37.6 27.2 %slice-start = ((s8[8388608]{0:T(1024)(128)(4,1)}), s8[4194304]{0:T(1024)(128)(4,1)S(1)}, s32[]{:S(2)}) async-start(s8[8388608]{0:T(1024)(128)(4,1)} %bitcast.109), calls=%async_computation.4 | async-start | bytes 8388608
  50.7 14.2 slice-start.1
  64.9 14.1 copy-start.5
  82.4 14.2 copy-start.6
  132.3 0.7 copy-start.13
  132.3 0.7 copy-start.8
  132.3 0.7 copy-start.10
  1384.3 9.5 copy-start.14
  1384.3 9.5 copy-start.12
  1384.3 552.5 %all-to-all-start.1 = ((bf16[2,3072,4096]{2,0,1:T(2,128)(2,1)}), bf16[2,3072,4096]{2,0,1:T(2,128)(2,1)}, u32[]{:S(2)}, u32[]{:S(2)}) async-start(bf16[2,3072,4096]{2,0,1:T(2,128)(2,1)} %copy.53), calls=%async_computation.1 | async-start | bytes 100663296 | tf_op jit(solution)/shard_map/all_to_all | solution.py:78
  1393.8 831.5 %all-reduce.5.cloned.1.call-start = ((), (), s32[]{:S(2)}) async-start(), calls=%async_computation.3 | async-start | bytes 33554432 | tf_op jit(solution)/shard_map/psum | solution.py:51
  1484.4 0.7 copy-start.11
  1484.4 0.9 copy-start.9
  1485.4 1.9 copy-start.2
  1493.7 33.6 %copy-start.3 = (s32[1,1024,4]{2,1,0:T(8,128)S(1)}, s32[1,1024,4]{2,1,0:T(8,128)}, u32[]{:S(2)}) copy-start(s32[1,1024,4]{2,1,0:T(8,128)} %copy-done.2) | copy-start | bytes 49156
  1936.8 43.3 %copy-start.1 = (s32[4096]{0:T(1024)S(1)}, s32[4096]{0:T(1024)}, u32[]{:S(2)}) copy-start(s32[4096]{0:T(1024)} %broadcast_clamp_fusion) | copy-start | bytes 49156
  2112.3 48.4 %copy-start.7 = (pred[1024,4]{1,0:T(8,128)(4,1)S(1)}, pred[1024,4]{1,0:T(8,128)(4,1)}, u32[]{:S(2)}) copy-start(pred[1024,4]{1,0:T(8,128)(4,1)} %compare_and_fusion) | copy-start | bytes 12292
Sparse Core Ops, SparseCore 0:
  132.5 293.8 all-reduce.2
  1484.6 289.6 all-reduce.4
where the time goes:
time: 2260 us; the launch traced here: 2250 us
  waiting for transfers between devices  685 us (30%)
  blocking collectives  559 us (25%)
  local copies, waits for them, and re-layouts  511 us (23%)
  matrix products  326 us (14%)
  other arithmetic  146 us (6%)
    all_to_all x1, blocking collectives, moe_branch(): recv_buf = lax.all_to_all(send_buf, 'ep', 0, 1, tiled=True)  559 us
    all_to_all x1, waiting for transfers between devices, moe_branch(): lax.all_to_all(expert_out, 'ep', 1, 0, tiled=True)  408 us
    psum x1, waiting for transfers between devices, dense_branch(): attn_sum = lax.psum(attn_part, 'tp')  277 us
    gather x2, local copies, waits for them, and re-layouts, moe_branch(): per_copy = jnp.take(returned, flat_pos, axis=0)  181 us
    convert_element_type x1, local copies, waits for them, and re-layouts, expert_swiglu(): jnp.einsum('erf,efd->erd', hidden_act, exp_down, preferred_element_type=j...  89.2 us
    gather x1, local copies, waits for them, and re-layouts, moe_branch(): jnp.take(u_norm, row_token, axis=0, mode='fill', fill_value=0)  87.4 us
    reduce_sum x1, other arithmetic, moe_branch(): moe_out = jnp.sum(gates[:, :, None] * per_copy.astype(jnp.float32), axis=1)  64.5 us
    dot_general x1, matrix products, expert_swiglu(): jnp.einsum('erf,efd->erd', hidden_act, exp_down, preferred_element_type=j...  49 us
  transfers between devices with their start and end apart: 3, of which 2 were waited for; matrix products, arithmetic and copies ran while one was open for 19% of the time, Pallas kernels for 0%

commit v1 on v0

v1 whole, which is shorter than its diff:
```python
import jax
import jax.numpy as jnp
from jax import lax
from jax.sharding import PartitionSpec as P

EPS = 1e-6
ROPE_BASE = 10000.0
F32 = jnp.float32
BF16 = jnp.bfloat16


def rms_norm(x_val, gain):
    x_f32 = x_val.astype(F32)
    inv_rms = lax.rsqrt(jnp.mean(x_f32 * x_f32, axis=-1, keepdims=True) + EPS)
    return (x_f32 * inv_rms * gain.astype(F32)).astype(BF16)


def rope_tables(seq_len, head_dim):
    inv_freq = ROPE_BASE ** (-jnp.arange(head_dim // 2, dtype=F32) * (2.0 / head_dim))
    angle = jnp.arange(seq_len, dtype=F32)[:, None] * inv_freq[None, :]
    return jnp.cos(angle), jnp.sin(angle)


def apply_rope(x_val, cos_tab, sin_tab):
    half_dim = x_val.shape[-1] // 2
    lower = x_val[..., :half_dim]
    upper = x_val[..., half_dim:]
    cos_b = cos_tab[:, None, :]
    sin_b = sin_tab[:, None, :]
    return jnp.concatenate([lower * cos_b - upper * sin_b, upper * cos_b + lower * sin_b], axis=-1)


def attention(hidden, attn_gain, w_query, w_key, w_value):
    num_seqs, seq_len, d_model = hidden.shape
    head_dim = w_query.shape[2]
    x_norm = rms_norm(hidden, attn_gain)
    cos_tab, sin_tab = rope_tables(seq_len, head_dim)
    query = apply_rope(jnp.einsum('bsd,dhe->bshe', x_norm, w_query, preferred_element_type=F32), cos_tab, sin_tab).astype(BF16)
    key_proj = apply_rope(jnp.einsum('bsd,dhe->bshe', x_norm, w_key, preferred_element_type=F32), cos_tab, sin_tab).astype(BF16)
    value_proj = jnp.einsum('bsd,dhe->bshe', x_norm, w_value, preferred_element_type=F32).astype(BF16)
    scores = jnp.einsum('bqhe,bkhe->bhqk', query, key_proj, preferred_element_type=F32) * head_dim ** -0.5
    causal = jnp.arange(seq_len)[:, None] >= jnp.arange(seq_len)[None, :]
    attn_prob = jax.nn.softmax(jnp.where(causal, scores, -1e30), axis=-1).astype(BF16)
    context = jnp.einsum('bhqk,bkhe->bqhe', attn_prob, value_proj, preferred_element_type=F32).astype(BF16)
    return context


def moe_partial(tokens, ids, moe_gain, w_router, exp_gate, exp_up, exp_down):
    experts = w_router.shape[1]
    local = exp_gate.shape[0]
    u_norm = rms_norm(tokens, moe_gain)
    logits = jnp.dot(u_norm, w_router, preferred_element_type=F32)
    hot = ids[:, :, None] == jnp.arange(experts, dtype=jnp.int32)[None, None, :]
    picked = jnp.sum(jnp.where(hot, logits[:, None, :], 0.0), axis=-1)
    gates = jax.nn.softmax(picked, axis=-1)
    first = lax.axis_index('ep') * local
    total = None
    for k in range(local):
        mine = ids == first + k
        weight = jnp.sum(jnp.where(mine, gates, 0.0), axis=1, keepdims=True)
        chosen = jnp.any(mine, axis=1, keepdims=True)
        gate_pre = jnp.dot(u_norm, exp_gate[k], preferred_element_type=F32)
        up_pre = jnp.dot(u_norm, exp_up[k], preferred_element_type=F32)
        act = (jax.nn.silu(gate_pre) * up_pre).astype(BF16)
        y_out = jnp.dot(act, exp_down[k], preferred_element_type=F32).astype(BF16)
        term = jnp.where(chosen, weight * y_out.astype(F32), 0.0)
        total = term if total is None else total + term
    return total


def solution(mesh):
    tok_spec = P(('dp', 'ep'), None, None)
    col_spec = P(None, 'tp', None)
    exp_spec = P('ep', None, None)
    in_specs = (tok_spec, tok_spec, tok_spec, P(None), col_spec, col_spec, col_spec, P('tp', None, None), P(None), P(None, 'tp'), P(None, 'tp'), P('tp', None), P(None), P(None, None), exp_spec, exp_spec, exp_spec)
    tp = mesh.shape['tp']
    ep = mesh.shape['ep']

    def layer_local(hidden_in, expert_ids, slot_ids, attn_gain, w_query, w_key, w_value, w_out, ffn_gain, w_gate, w_up, w_down, moe_gain, w_router, exp_gate, exp_up, exp_down):
        num_seqs, seq_len, d_model = hidden_in.shape
        tokens = num_seqs * seq_len
        top_k = expert_ids.shape[2]
        heads, head_dim = w_out.shape[0], w_out.shape[1]
        quarter = tokens // tp
        t_idx = lax.axis_index('tp')
        e_idx = lax.axis_index('ep')
        flat = hidden_in.reshape(tokens, d_model)
        own = lax.dynamic_slice_in_dim(flat, t_idx * quarter, quarter, 0)
        own_ids = lax.dynamic_slice_in_dim(expert_ids.reshape(tokens, top_k), t_idx * quarter, quarter, 0)
        gathered = lax.all_gather(own, 'ep', axis=0, tiled=True)
        gathered_ids = lax.all_gather(own_ids, 'ep', axis=0, tiled=True)
        per_ep = heads // ep
        rows = lax.dynamic_slice_in_dim(w_out, e_idx * per_ep, per_ep, 0).reshape(per_ep * head_dim, d_model)
        cols = lax.all_to_all(rows, 'tp', 1, 0, tiled=True)
        w_out_cols = lax.all_gather(cols, 'ep', axis=0, tiled=True)

        context = attention(hidden_in, attn_gain, w_query, w_key, w_value)
        ctx_all = lax.all_gather(context, 'tp', axis=0, tiled=False)
        ctx_all = ctx_all.reshape(tp, tokens, ep, per_ep * head_dim)
        w_cols = w_out_cols.reshape(ep, tp, per_ep * head_dim, d_model // tp)
        o_cols = jnp.einsum('tsef,etfd->sd', ctx_all, w_cols, preferred_element_type=F32)
        width = d_model // tp
        x_cols = lax.dynamic_slice_in_dim(flat, t_idx * width, width, 1)
        a_cols = (x_cols.astype(F32) + o_cols).astype(BF16)
        after_attn = lax.all_gather(a_cols, 'tp', axis=1, tiled=True)

        part = moe_partial(gathered, gathered_ids, moe_gain, w_router, exp_gate, exp_up, exp_down)
        moe_own = lax.psum_scatter(part, 'ep', scatter_dimension=0, tiled=True)

        f_norm = rms_norm(after_attn, ffn_gain)
        gate_pre = jnp.dot(f_norm, w_gate, preferred_element_type=F32)
        up_pre = jnp.dot(f_norm, w_up, preferred_element_type=F32)
        act = (jax.nn.silu(gate_pre) * up_pre).astype(BF16)
        ffn_part = jnp.dot(act, w_down, preferred_element_type=F32)
        ffn_own = lax.psum_scatter(ffn_part, 'tp', scatter_dimension=0, tiled=True)
        a_own = lax.dynamic_slice_in_dim(after_attn, t_idx * quarter, quarter, 0)
        out_own = ((a_own.astype(F32) + ffn_own) + moe_own).astype(BF16)
        return lax.all_gather(out_own, 'tp', axis=0, tiled=True).reshape(hidden_in.shape)

    return jax.shard_map(layer_local, mesh=mesh, in_specs=in_specs, out_specs=tok_spec, check_vma=False)
```

time: 2260 us -> 891 us (0.39)
  blocking collectives: 559 us -> 43.9 us
  local copies, waits for them, and re-layouts: 511 us -> 46.8 us
  waiting for transfers between devices: 685 us -> 441 us
  other arithmetic: 146 us -> 36.9 us
  matrix products: 326 us -> 299 us
    all_to_all x1, blocking collectives: 559 us -> 25 us  [layer_local(): cols = lax.all_to_all(rows, 'tp', 1, 0, tiled=True)]
    all_to_all x1 -> x0, waiting for transfers between devices: 408 us -> none  [moe_branch(): lax.all_to_all(expert_out, 'ep', 1, 0, tiled=True)]
    gather x7 -> x0, local copies, waits for them, and re-layouts: 302 us -> none  [the longest x2 181 us: moe_branch(): per_copy = jnp.take(returned, flat_pos, axis=0)]
    psum x2 -> x0, waiting for transfers between devices: 277 us -> none  [the longest x1 277 us: dense_branch(): attn_sum = lax.psum(attn_part, 'tp')]
    all_gather x0 -> x5, waiting for transfers between devices: none -> 270 us  [the longest x1 80.9 us: layer_local(): lax.all_gather(out_own, 'tp', axis=0, tiled=True).reshape(hidden_in.shape)]
    reduce_scatter x0 -> x2, waiting for transfers between devices: none -> 171 us  [the longest x1 171 us: layer_local(): moe_own = lax.psum_scatter(part, 'ep', scatter_dimension=0, tiled=True)]
    convert_element_type x1, local copies, waits for them, and re-layouts: 89.2 us -> 2.89 us  [attention(): jnp.einsum('bhqk,bkhe->bqhe', attn_prob, value_proj, preferred_element_ty...]
    all_to_all x2 -> x1, local copies, waits for them, and re-layouts: 76.6 us -> 1.32 us  [layer_local(): cols = lax.all_to_all(rows, 'tp', 1, 0, tiled=True)]
  transfers between devices with their start and end apart: 3 -> 7, of which waited for: 2 -> 5; matrix products, arithmetic and copies ran while one was open for 19% -> 27% of each run, Pallas kernels for 0% -> 0%
where the time goes in v1:
time: 891 us; the launch traced here: 882 us
  waiting for transfers between devices  441 us (49%)
  matrix products  299 us (34%)
  local copies, waits for them, and re-layouts  46.8 us (5%)
  blocking collectives  43.9 us (5%)
  other arithmetic  36.9 us (4%)
  between operations  14.1 us (2%)
    reduce_scatter x1, waiting for transfers between devices, layer_local(): moe_own = lax.psum_scatter(part, 'ep', scatter_dimension=0, tiled=True)  171 us
    all_gather x1, waiting for transfers between devices, layer_local(): lax.all_gather(out_own, 'tp', axis=0, tiled=True).reshape(hidden_in.shape)  80.9 us
    all_gather x1, waiting for transfers between devices, layer_local(): after_attn = lax.all_gather(a_cols, 'tp', axis=1, tiled=True)  77.2 us
    all_gather x1, waiting for transfers between devices, layer_local(): ctx_all = lax.all_gather(context, 'tp', axis=0, tiled=False)  62.7 us
    all_gather x1, waiting for transfers between devices, layer_local(): w_out_cols = lax.all_gather(cols, 'ep', axis=0, tiled=True)  48.8 us
    dot_general x2, matrix products, moe_partial(): y_out = jnp.dot(act, exp_down[k], preferred_element_type=F32).astype(BF16)  46.6 us
    dot_general x2, matrix products, moe_partial(): gate_pre = jnp.dot(u_norm, exp_gate[k], preferred_element_type=F32)  37.9 us
    unnamed x28, local copies, waits for them, and re-layouts  37.4 us
  transfers between devices with their start and end apart: 7, of which 5 were waited for; matrix products, arithmetic and copies ran while one was open for 27% of the time, Pallas kernels for 0%

profile of v1, /device:TPU:97, one launch (start us, length us, event | category | flops | bytes accessed | tf_op | source)
XLA Modules:
  0.0 882.2 jit_solution(12321308835595956677)
XLA Ops:
  6.6 0.0 all-gather.15.cloned.1.call-start
  6.6 1.4 iota_compare_fusion
  7.9 12.1 %copy.60 = bf16[4096,8,128]{0,2,1:T(8,128)(2,1)} copy(bf16[4096,8,128]{2,1,0:T(8,128)(2,1)} %param.20) | data formatting | bytes 16777216 | tf_op args[4]
  20.0 5.1 fusion.5
  25.1 1.8 fusion.68
  26.9 11.9 %copy.61 = bf16[4096,8,128]{0,2,1:T(8,128)(2,1)} copy(bf16[4096,8,128]{2,1,0:T(8,128)(2,1)} %param.21) | data formatting | bytes 16777216 | tf_op args[5]
  38.7 13.0 %fusion.17 = f32[1024,1024]{0,1:S(1)} fusion(bf16[4096,1024]{0,1:T(8,128)(2,1)} %bitcast.91, bf16[1,1024,4096]{2,1,0:T(8,128)(2,1)} %param.17, f32[4096]{0:T(1024)S(1)} %convert_element_type.91, f32[1024]{0:T(1024)S(1)} %add_rsqrt_fusion.2), kind=kOutput, calls=%fused_computation.28 | convolution fusion | flops 8606711808 | bytes 20992000
  51.7 0.0 slice-start.1
  51.8 13.2 %fusion.19 = f32[1024,1024]{0,1} fusion(bf16[4096,1024]{0,1:T(8,128)(2,1)S(1)} %bitcast.93, bf16[1,1024,4096]{2,1,0:T(8,128)(2,1)} %param.17, f32[4096]{0:T(1024)S(1)} %convert_element_type.91, f32[1024]{0:T(1024)S(1)} %add_rsqrt_fusion.2), kind=kOutput, calls=%fused_computation.30 | convolution fusion | flops 8606711808 | bytes 20992000
  65.0 14.1 %fusion.15 = bf16[1024,8,128]{2,0,1:T(8,128)(2,1)} fusion(bf16[4096,8,128]{2,1,0:T(8,128)(2,1)} %param.22, bf16[1,1024,4096]{2,1,0:T(8,128)(2,1)S(1)} %bitcast.90, f32[4096]{0:T(1024)S(1)} %convert_element_type.91, f32[1024]{0:T(1024)S(1)} %add_rsqrt_fusion.2), kind=kOutput, calls=%fused_computation.26 | convolution fusion | flops 8606711808 | bytes 18894848 | tf_op jit(solution)/shard_map/bsd,dhe->bshe/dot_general | solution.py:40
  79.1 3.3 fusion.62
  82.4 14.0 %fusion.91 = f32[8,1024]{1,0:T(8,128)S(1)} fusion(pred[1024,1024]{0,1:T(8,128)(4,1)} %iota_compare_fusion, bf16[1024,8,64]{0,2,1:T(8,128)(2,1)} %get-tuple-element.15, bf16[1024,8,64]{0,2,1:T(8,128)(2,1)} %get-tuple-element.16, bf16[1024,8,64]{0,2,1:T(8,128)(2,1)} %get-tuple-element.12, bf16[1024,8,64]{0,2,1:T(8,128)(2,1)S(1)} %get-tuple-element.11), kind=kOutput, calls=%fused_computation.102 | convolution fusion | flops 2189427712 | bytes 5275648 | tf_op jit(solution)/shard_map/sub | solution.py:43
  96.4 18.7 %convert_bitcast_fusion = bf16[1,1024,8,128]{1,3,2,0:T(8,128)(2,1)S(1)} fusion(f32[8,1024]{1,0:T(8,128)S(1)} %fusion.91, pred[1024,1024]{0,1:T(8,128)(4,1)} %iota_compare_fusion, bf16[1024,8,128]{2,0,1:T(8,128)(2,1)} %fusion.15, bf16[1024,8,64]{0,2,1:T(8,128)(2,1)} %get-tuple-element.15, bf16[1024,8,64]{0,2,1:T(8,128)(2,1)} %get-tuple-element.16, ...), kind=kOutput, calls=%fused_computation.62 | convolution fusion | flops 4346356736 | bytes 9469952 | tf_op jit(solution)/shard_map/bhqk,bkhe->bqhe/dot_general | solution.py:44
  115.1 2.9 copy.66
  118.0 0.1 all-gather.15.cloned.1.call-update
  118.1 0.1 all-gather.9.cloned.1.call-start
  118.2 1.3 constant_dynamic-slice_fusion.2
  119.5 0.7 copy.75
  120.1 25.0 %all_to_all.19 = bf16[128,4,1024]{0,2,1:T(8,128)(2,1)S(1)} all-to-all(bf16[128,4,1024]{0,2,1:T(8,128)(2,1)S(1)} %bitcast.97), channel_id=1, replica_groups=mesh['dp'=1,'tp'=4,'ep'=8] {'tp'}, dimensions={1} | all-to-all | bytes 2097152 | tf_op jit(solution)/shard_map/all_to_all | solution.py:94
  145.2 1.3 copy.68
  146.5 0.1 all-gather.9.cloned.1.call-update
  146.6 0.1 all-gather.11.cloned.1.call-start
  146.6 62.7 %all-gather.15.cloned.1.call-done = bf16[4,1024,8,128]{3,2,1,0:T(8,128)(2,1)} async-done(((bf16[1,1024,8,128]{3,2,1,0:T(8,128)(2,1)}), bf16[4,1024,8,128]{3,2,1,0:T(8,128)(2,1)}) %all-gather.15.cloned.1.call-update) | async-done | bytes 8388624 | tf_op jit(solution)/shard_map/all_gather | solution.py:98
  209.3 48.8 %all-gather.9.cloned.1.call-done = bf16[4096,1024]{1,0:T(8,128)(2,1)} async-done(((bf16[512,1024]{1,0:T(8,128)(2,1)}), bf16[4096,1024]{1,0:T(8,128)(2,1)}) %all-gather.9.cloned.1.call-update) | async-done | bytes 8388624 | tf_op jit(solution)/shard_map/all_gather | solution.py:95
  258.1 15.4 %fusion.41 = bf16[1024,1024]{1,0:T(8,128)(2,1)} fusion(bf16[8,4,128,1024]{3,2,1,0:T(8,128)(2,1)} %bitcast.100, bf16[4,1024,8,128]{3,2,1,0:T(8,128)(2,1)} %all-gather.15.cloned.1.call-done, bf16[1,1024,4096]{2,1,0:T(8,128)(2,1)} %param.17, s32[]{:T(128)S(6)} %select_n.34), kind=kOutput, calls=%fused_computation.55 | convolution fusion | flops 8593080320 | bytes 20971524 | tf_op jit(solution)/shard_map/tsef,etfd->sd/dot_general | solution.py:101
  273.6 0.1 all-gather.11.cloned.1.call-update
  273.6 0.1 all-gather.17.cloned.1.call-start
  273.7 3.1 constant_dynamic-slice_fusion
  276.8 0.1 all-gather.17.cloned.1.call-update
  276.9 0.1 reduce-scatter.3.cloned.1.call-start
  277.0 77.2 %all-gather.11.cloned.1.call-done = bf16[1024,4096]{1,0:T(8,128)(2,1)} async-done(((bf16[1024,1024]{1,0:T(8,128)(2,1)}), bf16[1024,4096]{1,0:T(8,128)(2,1)}) %all-gather.11.cloned.1.call-update) | async-done | bytes 8388624 | tf_op jit(solution)/shard_map/all_gather | solution.py:105
  354.2 5.2 fusion.8
  359.4 0.5 copy-done.3
  360.0 29.0 %fusion.53 = f32[1024,2752]{0,1:T(8,128)} fusion(bf16[4096,2752]{0,1:T(8,128)(2,1)} %param.25, bf16[1024,4096]{1,0:T(8,128)(2,1)S(1)} %copy-done.3, f32[4096]{0:T(1024)S(1)} %convert_element_type.101, f32[1024]{0:T(1024)S(1)} %add_rsqrt_fusion.1), kind=kOutput, calls=%fused_computation.59 | convolution fusion | flops 23102226432 | bytes 42225664 | tf_op jit(solution)/shard_map/dot_general | solution.py:111
  389.0 29.2 %multiply_convert_fusion = bf16[1024,2752]{0,1:T(8,128)(2,1)S(1)} fusion(f32[1024,2752]{0,1:T(8,128)} %fusion.53, bf16[4096,2752]{0,1:T(8,128)(2,1)} %param.26, bf16[1024,4096]{1,0:T(8,128)(2,1)S(1)} %copy-done.3, f32[4096]{0:T(1024)S(1)} %convert_element_type.101, f32[1024]{0:T(1024)S(1)} %add_rsqrt_fusion.1), kind=kOutput, calls=%fused_computation.25 | convolution fusion | flops 23119134720 | bytes 47861760 | tf_op jit(solution)/shard_map/dot_general | solution.py:112
  418.2 30.3 %fusion.92 = f32[1024,4096]{1,0:T(8,128)} fusion(bf16[1024,2752]{0,1:T(8,128)(2,1)S(1)} %multiply_convert_fusion, bf16[2752,4096]{1,0:T(8,128)(2,1)} %param.27), kind=kOutput, calls=%fused_computation.103 | convolution fusion | flops 23085449216 | bytes 44957696 | tf_op jit(solution)/shard_map/dot_general | solution.py:114
  448.5 0.1 reduce-scatter.3.cloned.1.call-update
  448.5 0.1 reduce-scatter.5.cloned.1.call-start
  448.6 0.6 copy-done.9
  449.2 0.7 constant_dynamic-slice_fusion.1
  449.9 18.9 %all-gather.1 = s32[1,2048,4]{1,2,0:T(4,128)S(1)} all-gather(s32[1,256,4]{1,2,0:T(4,128)S(1)} %constant_dynamic-slice_fusion.1), channel_id=3, replica_groups=mesh['dp'=1,'tp'=4,'ep'=8] {'ep'}, dimensions={1}, use_global_device_ids=true | all-gather | bytes 36864 | tf_op jit(solution)/shard_map/all_gather | solution.py:91
  468.7 0.1 fusion.90
  468.8 0.0 all-gather.17.cloned.1.call-done
  468.8 8.1 fusion.1
  476.9 2.6 copy-done.2
  479.5 5.3 fusion.3
  484.9 4.4 fusion.93
  489.3 1.3 copy-done.1
  490.6 0.1 select_reduce_fusion
  490.8 0.1 select_reduce_fusion.2
  490.8 16.3 %fusion.31 = f32[2048,688]{0,1:T(8,128)S(1)} fusion(bf16[2048,4096]{1,0:T(8,128)(2,1)} %copy-done.1, bf16[2,4096,688]{1,2,0:T(8,128)(2,1)} %param.31), kind=kOutput, calls=%fused_computation.42 | convolution fusion | flops 11542724608 | bytes 28049408 | tf_op jit(solution)/shard_map/dot_general | solution.py:63
  507.2 19.0 %multiply_convert_fusion.2 = bf16[2048,688]{0,1:T(8,128)(2,1)} fusion(f32[2048,688]{0,1:T(8,128)S(1)} %fusion.31, bf16[2048,4096]{1,0:T(8,128)(2,1)} %copy-done.1, bf16[2,4096,688]{1,2,0:T(8,128)(2,1)} %param.30), kind=kOutput, calls=%fused_computation.51 | convolution fusion | flops 11551178752 | bytes 30867456 | tf_op jit(solution)/shard_map/dot_general | solution.py:62
  526.2 19.4 %fusion.29 = bf16[2048,4096]{1,0:T(8,128)(2,1)} fusion(bf16[2048,688]{0,1:T(8,128)(2,1)} %multiply_convert_fusion.2, bf16[2,688,4096]{2,1,0:T(8,128)(2,1)} %param.32), kind=kOutput, calls=%fused_computation.40 | convolution fusion | flops 11542724608 | bytes 25231360 | tf_op jit(solution)/shard_map/dot_general | solution.py:65
  545.6 16.5 %fusion.25 = f32[2048,688]{0,1:T(8,128)S(1)} fusion(bf16[2048,4096]{1,0:T(8,128)(2,1)} %copy-done.1, bf16[2,4096,688]{1,2,0:T(8,128)(2,1)} %param.31), kind=kOutput, calls=%fused_computation.36 | convolution fusion | flops 11542724608 | bytes 28049408 | tf_op jit(solution)/shard_map/dot_general | solution.py:63
  562.1 18.9 %multiply_convert_fusion.1 = bf16[2048,688]{0,1:T(8,128)(2,1)} fusion(f32[2048,688]{0,1:T(8,128)S(1)} %fusion.25, bf16[2048,4096]{1,0:T(8,128)(2,1)} %copy-done.1, bf16[2,4096,688]{1,2,0:T(8,128)(2,1)} %param.30), kind=kOutput, calls=%fused_computation.47 | convolution fusion | flops 11551178752 | bytes 30867456 | tf_op jit(solution)/shard_map/dot_general | solution.py:62
  581.0 27.2 %select_add_fusion = f32[2048,4096]{1,0:T(8,128)} fusion(f32[2048]{0:T(1024)S(1)} %get-tuple-element.6, bf16[2048,4096]{1,0:T(8,128)(2,1)} %fusion.29, f32[2048]{0:T(1024)S(1)} %get-tuple-element.5, pred[2048]{0:T(1024)(128)(4,1)S(1)} %get-tuple-element.9, pred[2048]{0:T(1024)(128)(4,1)S(1)} %get-tuple-element.17, ...), kind=kOutput, calls=%fused_computation.6 | convolution fusion | flops 11609833472 | bytes 58806272 | tf_op jit(solution)/shard_map/dot_general | solution.py:65
  608.2 0.1 reduce-scatter.5.cloned.1.call-update
  608.2 0.1 all-gather.13.cloned.1.call-start
  608.3 0.0 reduce-scatter.3.cloned.1.call-done
  608.3 171.4 %reduce-scatter.5.cloned.1.call-done = f32[256,4096]{1,0:T(8,128)} async-done(((f32[2048,4096]{1,0:T(8,128)}), f32[256,4096]{1,0:T(8,128)}) %reduce-scatter.5.cloned.1.call-update) | async-done | bytes 4194320 | tf_op jit(solution)/shard_map/reduce_scatter | solution.py:108
  779.8 6.3 add_convert_fusion
  786.1 0.1 all-gather.13.cloned.1.call-update
  786.2 80.9 %all-gather.13.cloned.1.call-done = bf16[1024,4096]{1,0:T(8,128)(2,1)} async-done(((bf16[256,4096]{1,0:T(8,128)(2,1)}), bf16[1024,4096]{1,0:T(8,128)(2,1)}) %all-gather.13.cloned.1.call-update) | async-done | bytes 8388624 | tf_op jit(solution)/shard_map/all_gather | solution.py:118
  867.0 7.9 copy.83
  (29 shorter events, 0.1 us)
Async XLA Ops:
  6.5 478.3 %copy-start = (bf16[4096,16]{0,1:T(8,128)(2,1)S(1)}, bf16[4096,16]{0,1:T(8,128)(2,1)}, u32[]{:S(2)}) copy-start(bf16[4096,16]{0,1:T(8,128)(2,1)} %param.29) | copy-start | bytes 393220
  6.6 202.8 %all-gather.15.cloned.1.call-start = ((), (), s32[]{:S(2)}) async-start(), calls=%async_computation.8 | async-start | bytes 10485760 | tf_op jit(solution)/shard_map/all_gather | solution.py:98
  7.9 12.1 %copy-start.7 = (bf16[4096]{0:T(1024)(128)(2,1)S(1)}, bf16[4096]{0:T(1024)(128)(2,1)}, u32[]{:S(2)}) copy-start(bf16[4096]{0:T(1024)(128)(2,1)} %param.19) | copy-start | bytes 24580
  38.7 13.0 %copy-start.4 = (bf16[4096,8,128]{0,2,1:T(8,128)(2,1)S(1)}, bf16[4096,8,128]{0,2,1:T(8,128)(2,1)}, u32[]{:S(2)}) copy-start(bf16[4096,8,128]{0,2,1:T(8,128)(2,1)} %copy.61) | copy-start | bytes 25165828
  38.7 26.2 %slice-start = ((s8[8388608]{0:T(1024)(128)(4,1)}), s8[4194304]{0:T(1024)(128)(4,1)S(1)}, s32[]{:S(2)}) async-start(s8[8388608]{0:T(1024)(128)(4,1)} %bitcast.89), calls=%async_computation.10 | async-start | bytes 8388608
  51.7 13.2 %slice-start.1 = ((s8[8388608]{0:T(1024)(128)(4,1)}), s8[4194304]{0:T(1024)(128)(4,1)S(1)}, s32[]{:S(2)}) async-start(s8[8388608]{0:T(1024)(128)(4,1)} %bitcast.89), calls=%async_computation.11 | async-start | bytes 8388608
  65.0 14.1 %copy-start.5 = (f32[1024,1024]{0,1:S(1)}, f32[1024,1024]{0,1}, u32[]{:S(2)}) copy-start(f32[1024,1024]{0,1} %fusion.19) | copy-start | bytes 12582916
  65.0 14.1 %copy-start.6 = (f32[1024,64]{0,1:T(8,128)S(1)}, f32[1024,64]{0,1:T(8,128)}, u32[]{:S(2)}) copy-start(f32[1024,64]{0,1:T(8,128)} %get-tuple-element.20) | copy-start | bytes 786436
  118.1 140.0 %all-gather.9.cloned.1.call-start = ((), (), s32[]{:S(2)}) async-start(), calls=%async_computation.3 | async-start | bytes 9437184 | tf_op jit(solution)/shard_map/all_gather | solution.py:95
  146.6 207.6 %all-gather.11.cloned.1.call-start = ((), (), s32[]{:S(2)}) async-start(), calls=%async_computation.4 | async-start | bytes 10485760 | tf_op jit(solution)/shard_map/all_gather | solution.py:105
  273.6 3.4 copy-start.8
  273.6 195.2 %all-gather.17.cloned.1.call-start = ((), (), s32[]{:S(2)}) async-start(), calls=%async_computation.9 | async-start | bytes 18874368 | tf_op jit(solution)/shard_map/all_gather | solution.py:90
  276.9 331.4 %reduce-scatter.3.cloned.1.call-start = ((), (), s32[]{:S(2)}) async-start(), calls=%async_computation.5 | async-start | bytes 20971520 | tf_op jit(solution)/shard_map/reduce_scatter | solution.py:115
  354.2 5.8 copy-start.3
  448.5 0.7 copy-start.9
  448.5 331.2 %reduce-scatter.5.cloned.1.call-start = ((), (), s32[]{:S(2)}) async-start(), calls=%async_computation.6 | async-start | bytes 37748736 | tf_op jit(solution)/shard_map/reduce_scatter | solution.py:108
  468.8 10.7 %copy-start.2 = (bf16[1,2048,4096]{2,1,0:T(8,128)(2,1)S(1)}, bf16[1,2048,4096]{2,1,0:T(8,128)(2,1)}, u32[]{:S(2)}) copy-start(bf16[1,2048,4096]{2,1,0:T(8,128)(2,1)} %all-gather.17.cloned.1.call-done) | copy-start | bytes 50331652
  484.9 5.7 copy-start.1
  608.2 258.8 %all-gather.13.cloned.1.call-start = ((), (), s32[]{:S(2)}) async-start(), calls=%async_computation.7 | async-start | bytes 10485760 | tf_op jit(solution)/shard_map/all_gather | solution.py:118
Sparse Core Ops, SparseCore 0:
  118.2 91.0 all-gather.14
  210.9 47.1 all-gather.8
  273.7 80.4 all-gather.10
  355.7 84.1 all-gather.16
  448.7 146.3 reduce-scatter.2
  608.4 171.3 reduce-scatter.4
  786.3 80.7 all-gather.12

commit v2 on v1

--- a/solution.py
+++ b/solution.py
@@ -1,12 +1,326 @@
+import functools
 import jax
 import jax.numpy as jnp
 from jax import lax
+from jax.experimental import pallas as pl
+from jax.experimental.pallas import tpu as pltpu
 from jax.sharding import PartitionSpec as P
 
+F32 = jnp.float32
+BF16 = jnp.bfloat16
 EPS = 1e-6
 ROPE_BASE = 10000.0
-F32 = jnp.float32
-BF16 = jnp.bfloat16
+MESH = pl.DeviceIdType.MESH
+NT = (((1,), (1,)), ((), ()))
+
+
+def rcopy(src, dst, ssem, rsem, dev):
+    return pltpu.make_async_remote_copy(src_ref=src, dst_ref=dst, send_sem=ssem, recv_sem=rsem, device_id=dev, device_id_type=MESH)
+
+
+def entry_barrier(neighbours):
+    barrier = pltpu.get_barrier_semaphore()
+    for dev in neighbours:
+        pl.semaphore_signal(barrier, inc=1, device_id=dev, device_id_type=MESH)
+    pl.semaphore_wait(barrier, len(neighbours))
+
+
+def norm_rows(src, dst, gain, rows, step):
+    def one(r, carry):
+        sl = pl.ds(pl.multiple_of(r * step, step), step)
+        x = src[sl, :].astype(F32)
+        inv = lax.rsqrt(jnp.mean(x * x, axis=-1, keepdims=True) + EPS)
+        dst[sl, :] = (x * inv * gain[...].astype(F32)).astype(BF16)
+        return carry
+    lax.fori_loop(0, rows // step, one, 0)
+
+
+def ffn_body(fb, a_ref, wg, wu, wd, gain, m_ref, out_ref,
+             a_buf, n2, h, wbuf, dbuf, p1, p2, yrecv, xrecv, mbuf,
+             asem, wsem, dsem, msem, osem, ys, yr, xs, xr, gs, gr, fs, fr):
+    t = lax.axis_index('tp')
+    e = lax.axis_index('ep')
+    big = lax.rem(e, 2)
+    xc = e // 2
+    q = a_buf.shape[1]
+    d_model = a_buf.shape[2]
+    f_loc = wg.shape[0]
+    cw = d_model // 8
+    hw = cw // 2
+    nf = f_loc // fb
+    tail = f_loc - nf * fb
+    yright, yleft = {'tp': lax.rem(t + 1, 4)}, {'tp': lax.rem(t + 3, 4)}
+    xright, xleft = {'ep': lax.rem(xc + 1, 4) * 2 + big}, {'ep': lax.rem(xc + 3, 4) * 2 + big}
+
+    def cols(cb):
+        return pl.ds(pl.multiple_of(cb * cw, cw), cw)
+
+    def chunk(c):
+        return lax.rem(c + 8, 4)
+
+    def rows(c):
+        return pl.ds(pl.multiple_of(chunk(c) * q, q), q)
+
+    def a_load(c, slot):
+        return pltpu.make_async_copy(a_ref.at[rows(c)], a_buf.at[slot], asem.at[slot])
+
+    def w_load(i, slot, size):
+        sl = pl.ds(pl.multiple_of(i * fb, fb), size)
+        return (pltpu.make_async_copy(wg.at[sl], wbuf.at[slot, 0, pl.ds(0, size)], wsem.at[slot, 0]),
+                pltpu.make_async_copy(wu.at[sl], wbuf.at[slot, 1, pl.ds(0, size)], wsem.at[slot, 1]))
+
+    def w_start(i):
+        slot = lax.rem(i, 2)
+
+        @pl.when(i < nf)
+        def _():
+            for c in w_load(i, slot, fb):
+                c.start()
+
+        @pl.when(i == nf)
+        def _():
+            for c in w_load(nf, slot, tail):
+                c.start()
+
+    def col_of(j):
+        return lax.rem(j, 2) * 4 + j // 2
+
+    def d_load(jj):
+        slot = lax.rem(jj, 2)
+        start = pl.multiple_of(col_of(jj // 2) * cw + slot * hw, hw)
+        return pltpu.make_async_copy(wd.at[:, pl.ds(start, hw)], dbuf.at[slot], dsem.at[slot])
+
+    def m_load(k):
+        s, j = k // 8 + 1, lax.rem(k, 8)
+        side = lax.rem(j, 2)
+        c = lax.rem(xc + (2 * side - 1) * (1 + s) + 8, 4)
+        slot = lax.rem(k, 2)
+        return pltpu.make_async_copy(m_ref.at[c, :, cols(col_of(j))], mbuf.at[slot], msem.at[slot])
+
+    def send(buf, ssem, rsem, src, right, left, side, step, i):
+        @pl.when(side == 0)
+        def _():
+            rcopy(src, buf.at[0, step, i], ssem.at[0, step, i], rsem.at[0, step, i], right).start()
+
+        @pl.when(side == 1)
+        def _():
+            rcopy(src, buf.at[1, step, i], ssem.at[1, step, i], rsem.at[1, step, i], left).start()
+
+    def ysend(src, side, step, i):
+        send(yrecv, ys, yr, src, yright, yleft, side, step, i)
+
+    def xsend(src, side, step, i):
+        send(xrecv, xs, xr, src, xright, xleft, side, step, i)
+
+    def arrived(buf, ssem, rsem, side, step, i, dev):
+        rcopy(buf.at[side, step, i], buf.at[side, step, i], ssem.at[side, step, i], rsem.at[side, step, i], dev).wait_recv()
+
+    def sent(buf, ssem, rsem, side, step, i, dev):
+        rcopy(buf.at[side, step, i], buf.at[side, step, i], ssem.at[side, step, i], rsem.at[side, step, i], dev).wait_send()
+
+    def xserve(k):
+        s, j = k // 8, lax.rem(k, 8)
+        side, i = lax.rem(j, 2), j // 2
+        m_load(k + 1).start()
+        m_load(k).wait()
+        arrived(xrecv, xs, xr, side, s, i, xright)
+        xrecv[side, s, i] = xrecv[side, s, i] + mbuf[lax.rem(k, 2)]
+        xsend(xrecv.at[side, s, i], side, s + 1, i)
+
+    def gate_up(serve):
+        def block(i, size):
+            slot = lax.rem(i, 2)
+            for c in w_load(i, slot, size):
+                c.wait()
+            g = lax.dot_general(n2[...], wbuf[slot, 0, pl.ds(0, size)], NT, preferred_element_type=F32)
+            u = lax.dot_general(n2[...], wbuf[slot, 1, pl.ds(0, size)], NT, preferred_element_type=F32)
+            h[:, pl.ds(pl.multiple_of(i * fb, fb), size)] = (jax.nn.silu(g) * u).astype(BF16)
+
+        def one(i, carry):
+            block(i, fb)
+            w_start(i + 2)
+            serve(i)
+            return carry
+        lax.fori_loop(0, nf, one, 0)
+        block(nf, tail)
+
+    def down(use):
+        def one(jj, carry):
+            sub = lax.rem(jj, 2)
+            d_load(jj).wait()
+            r = jnp.dot(h[...], dbuf[sub], preferred_element_type=F32)
+
+            @pl.when(jj + 2 < 16)
+            def _():
+                d_load(jj + 2).start()
+            use(jj // 2, sub, pl.ds(pl.multiple_of(sub * hw, hw), hw), r)
+            return carry
+        lax.fori_loop(0, 16, one, 0)
+
+    a_load(t - 1, 0).start()
+    a_load(t + 1, 1).start()
+    w_start(0)
+    w_start(1)
+    entry_barrier((yright, yleft, xright, xleft))
+
+    def x_first(i, carry):
+        xsend(m_ref.at[chunk(xc - 1), :, cols(i)], 0, 0, i)
+        xsend(m_ref.at[chunk(xc + 1), :, cols(4 + i)], 1, 0, i)
+        return carry
+    lax.fori_loop(0, 4, x_first, 0)
+    d_load(0).start()
+    d_load(1).start()
+    m_load(0).start()
+
+    for slot in range(2):
+        a_load(t, slot).wait()
+        norm_rows(a_buf.at[slot], n2.at[pl.ds(slot * q, q)], gain, q, 16)
+    a_load(t + 2, 0).start()
+    a_load(t, 1).start()
+    gate_up(lambda i: None)
+    w_start(0)
+    w_start(1)
+
+    def use1(j, sub, part, r):
+        p1[col_of(j), :, part] = r
+        side, i = lax.rem(j, 2), j // 2
+
+        @pl.when(sub == 1)
+        def _():
+            ysend(p1.at[col_of(j), pl.ds(pl.multiple_of(side * q, q), q)], side, 0, i)
+    down(use1)
+    d_load(0).start()
+    d_load(1).start()
+
+    for slot in range(2):
+        a_load(t, slot).wait()
+        norm_rows(a_buf.at[slot], n2.at[pl.ds(slot * q, q)], gain, q, 16)
+
+    def serve2(i):
+        @pl.when(i < 8)
+        def _():
+            xserve(i)
+    gate_up(serve2)
+    for k in range(min(nf, 8), 8):
+        xserve(k)
+
+    def use2(j, sub, part, r):
+        side, i = lax.rem(j, 2), j // 2
+        p2[col_of(j), :, part] = r[q:]
+
+        @pl.when(sub == 0)
+        def _():
+            arrived(yrecv, ys, yr, side, 0, i, yright)
+        yrecv[side, 0, i, :, part] = yrecv[side, 0, i, :, part] + r[:q]
+
+        @pl.when(sub == 1)
+        def _():
+            ysend(yrecv.at[side, 0, i], side, 1, i)
+    down(use2)
+
+    def third(j, carry):
+        side, i = lax.rem(j, 2), j // 2
+        xserve(8 + j)
+        arrived(yrecv, ys, yr, side, 1, i, yright)
+        yrecv[side, 1, i] = yrecv[side, 1, i] + p1[col_of(j), pl.ds(pl.multiple_of((1 - side) * q, q), q)]
+        ysend(yrecv.at[side, 1, i], side, 2, i)
+        return carry
+    lax.fori_loop(0, 8, third, 0)
+
+    def out_local(cb):
+        return pltpu.make_async_copy(n2.at[pl.ds(0, q), cols(cb)], out_ref.at[rows(t), cols(cb)], osem.at[cb])
+
+    def gather(cb, side, dev):
+        return rcopy(n2.at[pl.ds(0, q), cols(cb)], out_ref.at[rows(t), cols(cb)], gs.at[side, cb], gr.at[side, cb], dev)
+
+    def last(j, carry):
+        side, i = lax.rem(j, 2), j // 2
+        cb = col_of(j)
+        k = 16 + j
+
+        @pl.when(j + 1 < 8)
+        def _():
+            m_load(k + 1).start()
+        m_load(k).wait()
+        arrived(xrecv, xs, xr, side, 2, i, xright)
+        arrived(yrecv, ys, yr, side, 2, i, yright)
+        b_val = a_buf[1, :, cols(cb)].astype(F32) + (yrecv[side, 2, i] + p2[cb])
+        n2[pl.ds(0, q), cols(cb)] = (b_val + (xrecv[side, 2, i] + mbuf[lax.rem(k, 2)])).astype(BF16)
+        out_local(cb).start()
+        gather(cb, 0, yright).start()
+        gather(cb, 1, yleft).start()
+        return carry
+    lax.fori_loop(0, 8, last, 0)
+
+    half = q // 2
+
+    def half_rows(c, which):
+        return pl.ds(pl.multiple_of(chunk(c) * q + which * half, half), half)
+
+    def forward(c, which, cb, dev):
+        ref = out_ref.at[half_rows(c, which), cols(cb)]
+        return rcopy(ref, ref, fs.at[which, cb], fr.at[which, cb], dev)
+
+    def pass_on(j, carry):
+        cb = col_of(j)
+        gather(cb, 0, yright).wait_recv()
+        forward(t - 1, 0, cb, yright).start()
+        gather(cb, 1, yleft).wait_recv()
+        forward(t + 1, 1, cb, yleft).start()
+        return carry
+    lax.fori_loop(0, 8, pass_on, 0)
+
+    def finish(j, carry):
+        cb = col_of(j)
+        out_local(cb).wait()
+        for which in range(2):
+            gather(cb, which, yright).wait_send()
+            forward(t, which, cb, yright).wait_send()
+            forward(t, which, cb, yright).wait_recv()
+        return carry
+    lax.fori_loop(0, 8, finish, 0)
+
+    def drain(k, carry):
+        step, j = k // 8, lax.rem(k, 8)
+        sent(yrecv, ys, yr, lax.rem(j, 2), step, j // 2, yright)
+        sent(xrecv, xs, xr, lax.rem(j, 2), step, j // 2, yright)
+        return carry
+    lax.fori_loop(0, 24, drain, 0)
+
+
+def ffn_call(after_attn, wg_t, wu_t, w_down, gain, m_part, fb=256):
+    tokens, d_model = after_attn.shape
+    f_loc = wg_t.shape[0]
+    q = tokens // 4
+    cw = d_model // 8
+    hbm = pl.BlockSpec(memory_space=pl.ANY)
+    vmem = pl.BlockSpec(memory_space=pltpu.VMEM)
+    dma = pltpu.SemaphoreType.DMA
+    flops = 2 * tokens * d_model * f_loc * 3
+    return pl.pallas_call(
+        functools.partial(ffn_body, fb),
+        out_shape=jax.ShapeDtypeStruct((tokens, d_model), BF16),
+        in_specs=[hbm, hbm, hbm, hbm, vmem, hbm],
+        out_specs=hbm,
+        scratch_shapes=[
+            pltpu.VMEM((2, q, d_model), BF16),
+            pltpu.VMEM((2 * q, d_model), BF16),
+            pltpu.VMEM((2 * q, f_loc), BF16),
+            pltpu.VMEM((2, 2, fb, d_model), BF16),
+            pltpu.VMEM((2, f_loc, cw // 2), BF16),
+            pltpu.VMEM((8, 2 * q, cw), F32),
+            pltpu.VMEM((8, q, cw), F32),
+            pltpu.VMEM((2, 3, 4, q, cw), F32),
+            pltpu.VMEM((2, 3, 4, q, cw), F32),
+            pltpu.VMEM((2, q, cw), F32),
+            dma((2,)), dma((2, 2)), dma((2,)), dma((2,)), dma((8,)),
+            dma((2, 3, 4)), dma((2, 3, 4)), dma((2, 3, 4)), dma((2, 3, 4)),
+            dma((2, 8)), dma((2, 8)), dma((2, 8)), dma((2, 8)),
+        ],
+        compiler_params=pltpu.CompilerParams(collective_id=2, has_side_effects=True, vmem_limit_bytes=67043328),
+        cost_estimate=pl.CostEstimate(flops=flops, bytes_accessed=4 * tokens * d_model + 12 * f_loc * d_model, transcendentals=tokens * f_loc),
+        name='ffn_ring',
+    )(after_attn, wg_t, wu_t, w_down, gain, m_part)
 
 
 def rms_norm(x_val, gain):
@@ -45,18 +359,17 @@
     return context
 
 
-def moe_partial(tokens, ids, moe_gain, w_router, exp_gate, exp_up, exp_down):
+def moe_partial(tokens, ids, first, moe_gain, w_router, exp_gate, exp_up, exp_down):
     experts = w_router.shape[1]
-    local = exp_gate.shape[0]
+    local = len(exp_gate)
     u_norm = rms_norm(tokens, moe_gain)
     logits = jnp.dot(u_norm, w_router, preferred_element_type=F32)
     hot = ids[:, :, None] == jnp.arange(experts, dtype=jnp.int32)[None, None, :]
     picked = jnp.sum(jnp.where(hot, logits[:, None, :], 0.0), axis=-1)
     gates = jax.nn.softmax(picked, axis=-1)
-    first = lax.axis_index('ep') * local
     total = None
     for k in range(local):
-        mine = ids == first + k
+        mine = ids == first[k]
         weight = jnp.sum(jnp.where(mine, gates, 0.0), axis=1, keepdims=True)
         chosen = jnp.any(mine, axis=1, keepdims=True)
         gate_pre = jnp.dot(u_norm, exp_gate[k], preferred_element_type=F32)
@@ -85,10 +398,15 @@
         t_idx = lax.axis_index('tp')
         e_idx = lax.axis_index('ep')
         flat = hidden_in.reshape(tokens, d_model)
+        core = lax.rem(e_idx, 2)
         own = lax.dynamic_slice_in_dim(flat, t_idx * quarter, quarter, 0)
         own_ids = lax.dynamic_slice_in_dim(expert_ids.reshape(tokens, top_k), t_idx * quarter, quarter, 0)
-        gathered = lax.all_gather(own, 'ep', axis=0, tiled=True)
-        gathered_ids = lax.all_gather(own_ids, 'ep', axis=0, tiled=True)
+        gathered = lax.all_gather(own, 'ep', axis=0, tiled=False).reshape(ep // 2, 2, quarter, d_model)
+        gathered = lax.dynamic_index_in_dim(gathered, core, 1, keepdims=False).reshape(ep // 2 * quarter, d_model)
+        gathered_ids = lax.all_gather(own_ids, 'ep', axis=0, tiled=False).reshape(ep // 2, 2, quarter, top_k)
+        gathered_ids = lax.dynamic_index_in_dim(gathered_ids, core, 1, keepdims=False).reshape(ep // 2 * quarter, top_k)
+        swap = [(k, k + 1 - 2 * (k % 2)) for k in range(ep)]
+        other = [lax.ppermute(w, 'ep', swap) for w in (exp_gate, exp_up, exp_down)]
         per_ep = heads // ep
         rows = lax.dynamic_slice_in_dim(w_out, e_idx * per_ep, per_ep, 0).reshape(per_ep * head_dim, d_model)
         cols = lax.all_to_all(rows, 'tp', 1, 0, tiled=True)
@@ -104,17 +422,12 @@
         a_cols = (x_cols.astype(F32) + o_cols).astype(BF16)
         after_attn = lax.all_gather(a_cols, 'tp', axis=1, tiled=True)
 
-        part = moe_partial(gathered, gathered_ids, moe_gain, w_router, exp_gate, exp_up, exp_down)
-        moe_own = lax.psum_scatter(part, 'ep', scatter_dimension=0, tiled=True)
-
-        f_norm = rms_norm(after_attn, ffn_gain)
-        gate_pre = jnp.dot(f_norm, w_gate, preferred_element_type=F32)
-        up_pre = jnp.dot(f_norm, w_up, preferred_element_type=F32)
-        act = (jax.nn.silu(gate_pre) * up_pre).astype(BF16)
-        ffn_part = jnp.dot(act, w_down, preferred_element_type=F32)
-        ffn_own = lax.psum_scatter(ffn_part, 'tp', scatter_dimension=0, tiled=True)
-        a_own = lax.dynamic_slice_in_dim(after_attn, t_idx * quarter, quarter, 0)
-        out_own = ((a_own.astype(F32) + ffn_own) + moe_own).astype(BF16)
-        return lax.all_gather(out_own, 'tp', axis=0, tiled=True).reshape(hidden_in.shape)
+        local = exp_gate.shape[0]
+        other_e = e_idx + 1 - 2 * core
+        first = [e_idx * local + k for k in range(local)] + [other_e * local + k for k in range(local)]
+        weights = [[w[k] for k in range(local)] + [v[k] for k in range(local)] for w, v in zip((exp_gate, exp_up, exp_down), other)]
+        part = moe_partial(gathered, gathered_ids, first, moe_gain, w_router, *weights)
+        out = ffn_call(after_attn, w_gate.T, w_up.T, w_down, ffn_gain.reshape(1, d_model), part.reshape(ep // 2, quarter, d_model))
+        return out.reshape(hidden_in.shape)
 
     return jax.shard_map(layer_local, mesh=mesh, in_specs=in_specs, out_specs=tok_spec, check_vma=False)

time: 891 us -> 777 us (0.87)
  waiting for transfers between devices: 441 us -> 109 us
  Pallas kernels: 0 us -> 249 us
  matrix products: 299 us -> 221 us
  blocking collectives: 43.9 us -> 86.3 us
    pallas_call x0 -> x1, Pallas kernels: none -> 249 us  [ffn_call(): pl.pallas_call(functools.partial(ffn_body, fb), out_shape=jax.ShapeDtypeS...]
    reduce_scatter x2 -> x0, waiting for transfers between devices: 171 us -> none  [the longest x1 171 us: layer_local(): moe_own = lax.psum_scatter(part, 'ep', scatter_dimension=0, tiled=True)]
    dot_general x3 -> x0, matrix products: 88.5 us -> none  [the longest x1 30.3 us: layer_local(): ffn_part = jnp.dot(act, w_down, preferred_element_type=F32)]
    all_gather x1, waiting for transfers between devices: 77.2 us -> 0.01 us  [layer_local(): after_attn = lax.all_gather(a_cols, 'tp', axis=1, tiled=True)]
    all_gather x1, waiting for transfers between devices: 62.7 us -> 0.02 us  [layer_local(): ctx_all = lax.all_gather(context, 'tp', axis=0, tiled=False)]
    all_gather x1, blocking collectives: 18.9 us -> 61.3 us  [layer_local(): lax.all_gather(own_ids, 'ep', axis=0, tiled=False)]
    convert_element_type x4, other arithmetic: 5.36 us -> 21.1 us  [rms_norm(): return (x_f32 * inv_rms * gain.astype(F32)).astype(BF16)]
    dot_general x2 -> x4, matrix products: 46.6 us -> 61.4 us  [moe_partial(): y_out = jnp.dot(act, exp_down[k], preferred_element_type=F32).astype(BF16)]
  transfers between devices with their start and end apart: 7 -> 7, of which waited for: 5 -> 2; matrix products, arithmetic and copies ran while one was open for 27% -> 24% of each run, Pallas kernels for 0% -> 0%
where the time goes in v2:
time: 777 us; the launch traced here: 767 us
  Pallas kernels  249 us (32%)
  matrix products  221 us (28%)
  waiting for transfers between devices  109 us (14%)
  blocking collectives  86.3 us (11%)
  local copies, waits for them, and re-layouts  44.1 us (6%)
  other arithmetic  37 us (5%)
  between operations  13.9 us (2%)
    pallas_call x1, Pallas kernels, ffn_call(): pl.pallas_call(functools.partial(ffn_body, fb), out_shape=jax.ShapeDtypeS...  249 us
    all_gather x1, waiting for transfers between devices, layer_local(): lax.all_gather(own, 'ep', axis=0, tiled=False)  69.1 us
    dot_general x4, matrix products, moe_partial(): y_out = jnp.dot(act, exp_down[k], preferred_element_type=F32).astype(BF16)  61.4 us
    all_gather x1, blocking collectives, layer_local(): lax.all_gather(own_ids, 'ep', axis=0, tiled=False)  61.3 us
    all_gather x1, waiting for transfers between devices, layer_local(): w_out_cols = lax.all_gather(cols, 'ep', axis=0, tiled=True)  40.1 us
    dot_general x4, matrix products, moe_partial(): up_pre = jnp.dot(u_norm, exp_up[k], preferred_element_type=F32)  36.1 us
    unnamed x35, local copies, waits for them, and re-layouts  34.1 us
    dot_general x4, matrix products, moe_partial(): gate_pre = jnp.dot(u_norm, exp_gate[k], preferred_element_type=F32)  29.1 us
  transfers between devices with their start and end apart: 7, of which 2 were waited for; matrix products, arithmetic and copies ran while one was open for 24% of the time, Pallas kernels for 0%

profile of v2, /device:TPU:97, one launch (start us, length us, event | category | flops | bytes accessed | tf_op | source)
XLA Modules:
  0.0 767.0 jit_solution(8141453511889079969)
XLA Ops:
  6.6 1.3 iota_compare_fusion
  7.9 5.1 fusion.2
  13.0 1.8 fusion.69
  14.7 12.0 %copy.59 = bf16[4096,8,128]{0,2,1:T(8,128)(2,1)} copy(bf16[4096,8,128]{2,1,0:T(8,128)(2,1)} %param.20) | data formatting | bytes 16777216 | tf_op args[4]
  26.8 15.0 %fusion.11 = bf16[1024,8,128]{2,0,1:T(8,128)(2,1)} fusion(bf16[4096,8,128]{2,1,0:T(8,128)(2,1)} %param.22, bf16[1,1024,4096]{2,1,0:T(8,128)(2,1)} %param.17, f32[4096]{0:T(1024)S(1)} %convert_element_type.117, f32[1024]{0:T(1024)S(1)} %add_rsqrt_fusion.1), kind=kOutput, calls=%fused_computation.20 | convolution fusion | flops 8606711808 | bytes 18894848 | tf_op jit(solution)/shard_map/bsd,dhe->bshe/dot_general | solution.py:354
  41.8 13.1 %fusion.13 = f32[1024,1024]{0,1} fusion(bf16[4096,1024]{0,1:T(8,128)(2,1)S(1)} %bitcast.136, bf16[1,1024,4096]{2,1,0:T(8,128)(2,1)} %param.17, f32[4096]{0:T(1024)S(1)} %convert_element_type.117, f32[1024]{0:T(1024)S(1)} %add_rsqrt_fusion.1), kind=kOutput, calls=%fused_computation.22 | convolution fusion | flops 8606711808 | bytes 20992000
  54.9 12.0 %copy.60 = bf16[4096,8,128]{0,2,1:T(8,128)(2,1)} copy(bf16[4096,8,128]{2,1,0:T(8,128)(2,1)} %param.21) | data formatting | bytes 16777216 | tf_op args[5]
  67.0 13.1 %fusion.15 = f32[1024,1024]{0,1:S(1)} fusion(bf16[4096,1024]{0,1:T(8,128)(2,1)} %bitcast.135, bf16[1,1024,4096]{2,1,0:T(8,128)(2,1)} %param.17, f32[4096]{0:T(1024)S(1)} %convert_element_type.117, f32[1024]{0:T(1024)S(1)} %add_rsqrt_fusion.1), kind=kOutput, calls=%fused_computation.24 | convolution fusion | flops 8606711808 | bytes 20992000
  80.1 2.4 fusion.63
  82.5 1.0 copy-done.3
  83.5 0.4 copy-done.4
  83.9 13.7 %fusion.95 = f32[8,1024]{1,0:T(8,128)S(1)} fusion(pred[1024,1024]{0,1:T(8,128)(4,1)} %iota_compare_fusion, bf16[1024,8,64]{0,2,1:T(8,128)(2,1)S(1)} %get-tuple-element.22, bf16[1024,8,64]{0,2,1:T(8,128)(2,1)} %get-tuple-element.23, bf16[1024,8,64]{0,2,1:T(8,128)(2,1)S(1)} %get-tuple-element.19, bf16[1024,8,64]{0,2,1:T(8,128)(2,1)S(1)} %get-tuple-element.18), kind=kOutput, calls=%fused_computation.118 | convolution fusion | flops 2189427712 | bytes 5275648 | tf_op jit(solution)/shard_map/sub | solution.py:357
  97.6 18.7 %convert_bitcast_fusion = bf16[1,1024,8,128]{1,3,2,0:T(8,128)(2,1)S(1)} fusion(f32[8,1024]{1,0:T(8,128)S(1)} %fusion.95, pred[1024,1024]{0,1:T(8,128)(4,1)} %iota_compare_fusion, bf16[1024,8,128]{2,0,1:T(8,128)(2,1)} %fusion.11, bf16[1024,8,64]{0,2,1:T(8,128)(2,1)} %copy-done.4, bf16[1024,8,64]{0,2,1:T(8,128)(2,1)} %get-tuple-element.23, ...), kind=kOutput, calls=%fused_computation.68 | convolution fusion | flops 4346356736 | bytes 9469952 | tf_op jit(solution)/shard_map/bhqk,bkhe->bqhe/dot_general | solution.py:358
  116.3 2.9 copy.65
  119.2 0.1 all-gather.12.cloned.1.call-update
  119.3 0.0 copy-start.8
  119.3 0.0 copy-start.9
  119.3 0.1 all-gather.6.cloned.1.call-start
  119.4 1.3 constant_dynamic-slice_fusion.3
  120.7 0.7 copy.74
  121.3 25.0 %all_to_all.19 = bf16[128,4,1024]{0,2,1:T(8,128)(2,1)S(1)} all-to-all(bf16[128,4,1024]{0,2,1:T(8,128)(2,1)S(1)} %bitcast.140), channel_id=1, replica_groups=mesh['dp'=1,'tp'=4,'ep'=8] {'tp'}, dimensions={1} | all-to-all | bytes 2097152 | tf_op jit(solution)/shard_map/all_to_all | solution.py:412
  146.3 1.4 copy.67
  147.7 0.1 all-gather.6.cloned.1.call-update
  147.8 0.1 all-gather.10.cloned.1.call-start
  147.9 3.1 constant_dynamic-slice_fusion
  151.0 0.1 all-gather.10.cloned.1.call-update
  151.1 0.1 all-gather.8.cloned.1.call-start
  151.1 4.8 collective-permute-start
  155.9 0.1 collective-permute-start.1
  156.0 0.4 collective-permute-start.2
  156.4 0.6 reshape.400.gain
  157.0 0.7 constant_dynamic-slice_fusion.2
  157.7 61.3 %all_gather.24 = s32[8,256,4]{1,2,0:T(4,128)S(1)} all-gather(s32[1,256,4]{1,2,0:T(4,128)S(1)} %constant_dynamic-slice_fusion.2), channel_id=1, replica_groups=mesh['dp'=1,'tp'=4,'ep'=8] {'ep'}, dimensions={0}, use_global_device_ids=true | all-gather | bytes 36864 | tf_op jit(solution)/shard_map/all_gather | solution.py:406
  219.1 0.1 fusion.92
  219.2 0.0 all-gather.12.cloned.1.call-done
  219.2 40.1 %all-gather.6.cloned.1.call-done = bf16[4096,1024]{1,0:T(8,128)(2,1)} async-done(((bf16[512,1024]{1,0:T(8,128)(2,1)}), bf16[4096,1024]{1,0:T(8,128)(2,1)}) %all-gather.6.cloned.1.call-update) | async-done | bytes 8388624 | tf_op jit(solution)/shard_map/all_gather | solution.py:413
  259.3 15.4 %fusion.43 = bf16[1024,1024]{1,0:T(8,128)(2,1)} fusion(bf16[8,4,128,1024]{3,2,1,0:T(8,128)(2,1)} %bitcast.158, bf16[4,1024,8,128]{3,2,1,0:T(8,128)(2,1)} %all-gather.12.cloned.1.call-done, bf16[1,1024,4096]{2,1,0:T(8,128)(2,1)} %param.17, s32[]{:T(128)S(6)} %select_n.55), kind=kOutput, calls=%fused_computation.59 | convolution fusion | flops 8593080320 | bytes 20971524 | tf_op jit(solution)/shard_map/tsef,etfd->sd/dot_general | solution.py:419
  274.7 0.1 all-gather.8.cloned.1.call-update
  274.8 69.1 %all-gather.10.cloned.1.call-done = bf16[8,256,4096]{2,1,0:T(8,128)(2,1)} async-done(((bf16[1,256,4096]{2,1,0:T(8,128)(2,1)}), bf16[8,256,4096]{2,1,0:T(8,128)(2,1)}) %all-gather.10.cloned.1.call-update) | async-done | bytes 16777232 | tf_op jit(solution)/shard_map/all_gather | solution.py:404
  343.8 5.1 multiply_reduce_fusion
  348.9 0.0 copy-start.6
  348.9 10.5 %fusion.6 = bf16[1024,4096]{1,0:T(8,128)(2,1)} fusion(f32[4096]{0:T(1024)S(1)} %convert_element_type.128, f32[1024]{0:T(1024)S(1)} %bitcast.145, bf16[4,2,256,4096]{3,2,1,0:T(8,128)(2,1)} %bitcast.124, s32[]{:T(128)S(6)} %select_n.59), kind=kLoop, calls=%fused_computation.12 | loop fusion | flops 16777216 | bytes 16797700 | tf_op jit(solution)/shard_map/convert_element_type | solution.py:329
  359.5 5.6 fusion.96
  365.1 0.1 select_reduce_fusion
  365.3 10.5 %multiply_convert_fusion = bf16[4,1,256,4096]{3,2,1,0:T(8,128)(2,1)} fusion(f32[4096]{0:T(1024)S(1)} %convert_element_type.128, f32[4,256]{1,0:T(4,128)S(1)} %get-tuple-element.28, bf16[4,2,256,4096]{3,2,1,0:T(8,128)(2,1)} %bitcast.125, s32[]{:T(128)S(6)} %select_n.59), kind=kLoop, calls=%fused_computation.14 | loop fusion | flops 16777216 | bytes 16797700 | tf_op jit(solution)/shard_map/convert_element_type | solution.py:329
  375.8 10.5 %fusion.27 = f32[1024,688]{0,1:T(8,128)S(1)} fusion(bf16[1024,4096]{1,0:T(8,128)(2,1)} %bitcast.126, bf16[2,4096,688]{1,2,0:T(8,128)(2,1)} %param.31), kind=kOutput, calls=%fused_computation.42 | convolution fusion | flops 5771362304 | bytes 16842752 | tf_op jit(solution)/shard_map/dot_general | solution.py:376
  386.3 0.0 slice-start.2
  386.3 8.3 %fusion.33 = f32[1024,688]{0,1:T(8,128)S(1)} fusion(bf16[1024,4096]{1,0:T(8,128)(2,1)S(1)} %bitcast.127, bf16[2,4096,688]{1,2,0:T(8,128)(2,1)} %param.31), kind=kOutput, calls=%fused_computation.48 | convolution fusion | flops 5771362304 | bytes 16842752 | tf_op jit(solution)/shard_map/dot_general | solution.py:376
  394.7 6.4 multiply_convert_fusion.4
  401.1 12.0 %fusion.31 = bf16[1024,4096]{1,0:T(8,128)(2,1)} fusion(bf16[1024,688]{0,1:T(8,128)(2,1)S(1)} %multiply_convert_fusion.4, bf16[2,688,4096]{2,1,0:T(8,128)(2,1)} %param.32), kind=kOutput, calls=%fused_computation.46 | convolution fusion | flops 5771362304 | bytes 15433728 | tf_op jit(solution)/shard_map/dot_general | solution.py:378
  413.1 0.0 collective-permute-done
  413.1 8.1 %fusion.21 = f32[1024,688]{0,1:T(8,128)S(1)} fusion(bf16[1024,4096]{1,0:T(8,128)(2,1)S(1)} %bitcast.129, bf16[2,4096,688]{1,2,0:T(8,128)(2,1)} %collective-permute-done), kind=kOutput, calls=%fused_computation.33 | convolution fusion | flops 5771362304 | bytes 16842752 | tf_op jit(solution)/shard_map/dot_general | solution.py:375
  421.3 6.4 multiply_convert_fusion.3
  427.7 0.1 select_reduce_fusion.4
  427.8 11.7 %fusion.25 = bf16[1024,4096]{1,0:T(8,128)(2,1)} fusion(bf16[1024,688]{0,1:T(8,128)(2,1)S(1)} %multiply_convert_fusion.3, bf16[2,688,4096]{2,1,0:T(8,128)(2,1)} %param.32), kind=kOutput, calls=%fused_computation.40 | convolution fusion | flops 5771362304 | bytes 15433728 | tf_op jit(solution)/shard_map/dot_general | solution.py:378
  439.5 8.1 %fusion.24 = f32[1024,688]{0,1:T(8,128)S(1)} fusion(bf16[1024,4096]{1,0:T(8,128)(2,1)S(1)} %bitcast.131, bf16[2,4096,688]{1,2,0:T(8,128)(2,1)} %collective-permute-done), kind=kOutput, calls=%fused_computation.39 | convolution fusion | flops 5771362304 | bytes 16842752 | tf_op jit(solution)/shard_map/dot_general | solution.py:375
  447.7 0.0 collective-permute-done.1
  447.7 9.2 %fusion.20 = f32[1024,688]{0,1:T(8,128)} fusion(bf16[1024,4096]{1,0:T(8,128)(2,1)S(1)} %bitcast.132, bf16[2,4096,688]{1,2,0:T(8,128)(2,1)} %collective-permute-done.1), kind=kOutput, calls=%fused_computation.31 | convolution fusion | flops 5771362304 | bytes 16842752 | tf_op jit(solution)/shard_map/dot_general | solution.py:376
  456.9 8.1 %fusion.23 = f32[1024,688]{0,1:T(8,128)S(1)} fusion(bf16[1024,4096]{1,0:T(8,128)(2,1)S(1)} %bitcast.133, bf16[2,4096,688]{1,2,0:T(8,128)(2,1)} %collective-permute-done.1), kind=kOutput, calls=%fused_computation.37 | convolution fusion | flops 5771362304 | bytes 16842752 | tf_op jit(solution)/shard_map/dot_general | solution.py:376
  465.0 0.0 collective-permute-done.2
  465.0 12.1 %fusion.22 = bf16[1024,4096]{1,0:T(8,128)(2,1)} fusion(bf16[2,688,4096]{2,1,0:T(8,128)(2,1)} %collective-permute-done.2, f32[1024,688]{0,1:T(8,128)S(1)} %fusion.23, f32[1024,688]{0,1:T(8,128)S(1)} %fusion.24), kind=kOutput, calls=%fused_computation.35 | convolution fusion | flops 5775589376 | bytes 19660800 | tf_op jit(solution)/shard_map/dot_general | solution.py:378
  477.2 25.5 %select_add_fusion = f32[1024,4096]{1,0:T(8,128)} fusion(f32[1024]{0:T(1024)S(1)} %bitcast.151, bf16[1024,4096]{1,0:T(8,128)(2,1)} %fusion.22, f32[1024]{0:T(1024)S(1)} %bitcast.152, bf16[1024,4096]{1,0:T(8,128)(2,1)} %fusion.25, f32[1024]{0:T(1024)S(1)} %bitcast.153, bf16[1024,4096]{1,0:T(8,128)(2,1)} %fusion.31, f32[1024]{0:T(1024)S(1)} %bitcast.150, ...), kind=kOutput, calls=%fused_computation.13 | convolution fusion | flops 5842698240 | bytes 53235712 | tf_op jit(solution)/shard_map/dot_general | solution.py:378
  502.7 249.5 %ffn_ring.1 = bf16[1024,4096]{1,0:T(8,128)(2,1)} custom-call(bf16[1024,4096]{1,0:T(8,128)(2,1)} %all-gather.8.cloned.1.call-done.a_ref, bf16[2752,4096]{1,0:T(8,128)(2,1)} %bitcast.154, bf16[2752,4096]{1,0:T(8,128)(2,1)} %bitcast.155, bf16[2752,4096]{1,0:T(8,128)(2,1)} %wd.1, bf16[1,4096]{1,0:T(2,128)(2,1)} %reshape.400.gain, f32[4,256,4096]{2,1,0:T(8,128)} %bitcast.159), custom_call_target="tpu_custom_call" | custom-call | flops 69256347648 | bytes 152043520 | tf_op jit(solution)/shard_map/ffn_ring/pallas_call | solution.py:300
  752.2 7.9 %copy.87 = bf16[1,1024,4096]{2,1,0:T(8,128)(2,1)} copy(bf16[1,1024,4096]{2,1,0:T(8,128)(2,1)} %bitcast.134) | data formatting | bytes 16777216
  (42 shorter events, 0.2 us)
Async XLA Ops:
  6.5 6.4 copy-start.7
  6.5 212.7 %all-gather.12.cloned.1.call-start = ((), (), s32[]{:S(2)}) async-start(), calls=%async_computation.4 | async-start | bytes 10485760 | tf_op jit(solution)/shard_map/all_gather | solution.py:416
  26.8 15.0 %copy-start.1 = (bf16[4096,8,128]{0,2,1:T(8,128)(2,1)S(1)}, bf16[4096,8,128]{0,2,1:T(8,128)(2,1)}, u32[]{:S(2)}) copy-start(bf16[4096,8,128]{0,2,1:T(8,128)(2,1)} %copy.59) | copy-start | bytes 25165828
  67.0 13.2 %copy-start.2 = (f32[1024,1024]{0,1:S(1)}, f32[1024,1024]{0,1}, u32[]{:S(2)}) copy-start(f32[1024,1024]{0,1} %fusion.13) | copy-start | bytes 12582916
  67.0 13.2 %copy-start.5 = (f32[1024,64]{0,1:T(8,128)S(1)}, f32[1024,64]{0,1:T(8,128)}, u32[]{:S(2)}) copy-start(f32[1024,64]{0,1:T(8,128)} %get-tuple-element.31) | copy-start | bytes 786436
  82.5 1.0 copy-start.3
  82.5 1.4 copy-start.4
  119.3 37.2 %copy-start.8 = (bf16[4096]{0:T(1024)(128)(2,1)S(1)}, bf16[4096]{0:T(1024)(128)(2,1)}, u32[]{:S(2)}) copy-start(bf16[4096]{0:T(1024)(128)(2,1)} %param.28) | copy-start | bytes 24580
  119.3 37.2 %copy-start.9 = (bf16[4096]{0:T(1024)(128)(2,1)S(1)}, bf16[4096]{0:T(1024)(128)(2,1)}, u32[]{:S(2)}) copy-start(bf16[4096]{0:T(1024)(128)(2,1)} %param.24) | copy-start | bytes 24580
  119.3 140.0 %all-gather.6.cloned.1.call-start = ((), (), s32[]{:S(2)}) async-start(), calls=%async_computation.1 | async-start | bytes 9437184 | tf_op jit(solution)/shard_map/all_gather | solution.py:413
  147.8 196.0 %all-gather.10.cloned.1.call-start = ((), (), s32[]{:S(2)}) async-start(), calls=%async_computation.3 | async-start | bytes 18874368 | tf_op jit(solution)/shard_map/all_gather | solution.py:404
  151.1 351.6 %all-gather.8.cloned.1.call-start = ((), (), s32[]{:S(2)}) async-start(), calls=%async_computation.2 | async-start | bytes 10485760 | tf_op jit(solution)/shard_map/all_gather | solution.py:423
  151.1 262.0 %collective-permute-start = (bf16[2,4096,688]{1,2,0:T(8,128)(2,1)}, bf16[2,4096,688]{1,2,0:T(8,128)(2,1)}, u32[]{:S(2)}, u32[]{:S(2)}) collective-permute-start(bf16[2,4096,688]{1,2,0:T(8,128)(2,1)} %param.30), channel_id=1, source_target_pairs={{0,1},{1,0},{2,3},{3,2},{4,5},{5,4},{6,7},{7,6},{8,9},{9,8},{10,11... | collective-permute-start | bytes 33816584 | tf_op jit(solution)/shard_map/ppermute | solution.py:409
  155.9 291.8 %collective-permute-start.1 = (bf16[2,4096,688]{1,2,0:T(8,128)(2,1)}, bf16[2,4096,688]{1,2,0:T(8,128)(2,1)}, u32[]{:S(2)}, u32[]{:S(2)}) collective-permute-start(bf16[2,4096,688]{1,2,0:T(8,128)(2,1)} %param.31), channel_id=1, source_target_pairs={{0,1},{1,0},{2,3},{3,2},{4,5},{5,4},{6,7},{7,6},{8,9},{9,8},{10,11... | collective-permute-start | bytes 33816584 | tf_op jit(solution)/shard_map/ppermute | solution.py:409
  156.0 309.0 %collective-permute-start.2 = (bf16[2,688,4096]{2,1,0:T(8,128)(2,1)}, bf16[2,688,4096]{2,1,0:T(8,128)(2,1)}, u32[]{:S(2)}, u32[]{:S(2)}) collective-permute-start(bf16[2,688,4096]{2,1,0:T(8,128)(2,1)} %param.32), channel_id=1, source_target_pairs={{0,1},{1,0},{2,3},{3,2},{4,5},{5,4},{6,7},{7,6},{8,9},{9,8},{10,11... | collective-permute-start | bytes 33816584 | tf_op jit(solution)/shard_map/ppermute | solution.py:409
  348.9 10.6 %copy-start.6 = (bf16[4096,16]{0,1:T(8,128)(2,1)S(1)}, bf16[4096,16]{0,1:T(8,128)(2,1)}, u32[]{:S(2)}) copy-start(bf16[4096,16]{0,1:T(8,128)(2,1)} %param.29) | copy-start | bytes 393220
  375.8 10.5 %copy-start = (bf16[4,1,256,4096]{3,2,1,0:T(8,128)(2,1)S(1)}, bf16[4,1,256,4096]{3,2,1,0:T(8,128)(2,1)}, u32[]{:S(2)}) copy-start(bf16[4,1,256,4096]{3,2,1,0:T(8,128)(2,1)} %multiply_convert_fusion) | copy-start | bytes 25165828
  375.8 18.8 %slice-start = ((s8[11272192]{0:T(1024)(128)(4,1)}), s8[4194304]{0:T(1024)(128)(4,1)S(1)}, s32[]{:S(2)}) async-start(s8[11272192]{0:T(1024)(128)(4,1)} %bitcast.156), calls=%async_computation.5 | async-start | bytes 8388608
  375.8 18.8 %slice-start.1 = ((s8[11272192]{0:T(1024)(128)(4,1)}), s8[4194304]{0:T(1024)(128)(4,1)S(1)}, s32[]{:S(2)}) async-start(s8[11272192]{0:T(1024)(128)(4,1)} %bitcast.156), calls=%async_computation.6 | async-start | bytes 8388608
  386.3 8.3 %slice-start.2 = ((s8[11272192]{0:T(1024)(128)(4,1)}), s8[2883584]{0:T(1024)(128)(4,1)S(1)}, s32[]{:S(2)}) async-start(s8[11272192]{0:T(1024)(128)(4,1)} %bitcast.156), calls=%async_computation.7 | async-start | bytes 5767168
Sparse Core Ops, SparseCore 0:
  119.4 91.0 all-gather.11
  212.1 47.1 all-gather.5
  261.0 82.8 all-gather.9
  345.3 80.7 all-gather.7

commit v3 on v2

v3 whole, which is shorter than its diff:
```python
import functools

import jax
import jax.numpy as jnp
from jax import lax
from jax.experimental import pallas as pl
from jax.experimental.pallas import tpu as pltpu
from jax.sharding import PartitionSpec as P

F32 = jnp.float32
BF16 = jnp.bfloat16
EPS = 1e-6
ROPE_BASE = 10000.0
VMEM_LIMIT = 67043328
MESH = pl.DeviceIdType.MESH
NT = (((1,), (1,)), ((), ()))


RING = 4
SIDES = (0, 1)


def odd(k):
    return lax.rem(k, 2)


def turn(side):
    return 1 - 2 * side


def loop(count, body):
    def step(k, carry):
        body(k)
        return carry
    lax.fori_loop(0, count, step, 0)


def window(index, size):
    return pl.ds(pl.multiple_of(index * size, size), size)


def rcopy(src, dst, ssem, rsem, dev):
    return pltpu.make_async_remote_copy(src_ref=src, dst_ref=dst, send_sem=ssem, recv_sem=rsem, device_id=dev, device_id_type=MESH)


def entry_barrier(neighbours):
    barrier = pltpu.get_barrier_semaphore()
    for dev in neighbours:
        pl.semaphore_signal(barrier, inc=1, device_id=dev, device_id_type=MESH)
    pl.semaphore_wait(barrier, len(neighbours))


def norm_rows(src, dst, gain, rows, step):
    def one(r):
        sl = window(r, step)
        x = src[sl, :].astype(F32)
        inv = lax.rsqrt(jnp.mean(x * x, axis=-1, keepdims=True) + EPS)
        dst[sl, :] = (x * inv * gain[...].astype(F32)).astype(BF16)
    loop(rows // step, one)


def ffn_body(fb, a_ref, wg, wu, wd, gain, m_ref, out_ref,
             a_buf, n2, h, wbuf, dbuf, p1, p2, yrecv, xrecv, mbuf,
             asem, wsem, dsem, msem, osem, ys, yr, xs, xr, gs, gr, fs, fr):
    t = lax.axis_index('tp')
    e = lax.axis_index('ep')
    big = odd(e)
    xc = e // 2
    q = a_buf.shape[1]
    d_model = a_buf.shape[2]
    f_loc = wg.shape[0]
    cw = d_model // 8
    hw = cw // 2
    nf = f_loc // fb
    tail = f_loc - nf * fb
    yright, yleft = {'tp': lax.rem(t + 1, RING)}, {'tp': lax.rem(t + 3, RING)}
    xright, xleft = {'ep': lax.rem(xc + 1, RING) * 2 + big}, {'ep': lax.rem(xc + 3, RING) * 2 + big}

    def cols(cb):
        return window(cb, cw)

    def chunk(c):
        return lax.rem(c + 8, RING)

    def rows(c):
        return window(chunk(c), q)

    def a_load(c, slot):
        return pltpu.make_async_copy(a_ref.at[rows(c)], a_buf.at[slot], asem.at[slot])

    def w_load(i, slot, size):
        sl = pl.ds(pl.multiple_of(i * fb, fb), size)
        return (pltpu.make_async_copy(wg.at[sl], wbuf.at[slot, 0, pl.ds(0, size)], wsem.at[slot, 0]),
                pltpu.make_async_copy(wu.at[sl], wbuf.at[slot, 1, pl.ds(0, size)], wsem.at[slot, 1]))

    def w_start(i):
        slot = odd(i)

        @pl.when(i < nf)
        def _():
            for c in w_load(i, slot, fb):
                c.start()

        @pl.when(i == nf)
        def _():
            for c in w_load(nf, slot, tail):
                c.start()

    def col_of(j):
        return odd(j) * 4 + j // 2

    def d_load(jj):
        slot = odd(jj)
        start = pl.multiple_of(col_of(jj // 2) * cw + slot * hw, hw)
        return pltpu.make_async_copy(wd.at[:, pl.ds(start, hw)], dbuf.at[slot], dsem.at[slot])

    def m_load(k):
        s, j = k // 8 + 1, lax.rem(k, 8)
        side = odd(j)
        c = lax.rem(xc + (2 * side - 1) * (1 + s) + 8, RING)
        slot = odd(k)
        return pltpu.make_async_copy(m_ref.at[c, :, cols(col_of(j))], mbuf.at[slot], msem.at[slot])

    def send(buf, ssem, rsem, src, right, left, side, step, i):
        @pl.when(side == 0)
        def _():
            rcopy(src, buf.at[0, step, i], ssem.at[0, step, i], rsem.at[0, step, i], right).start()

        @pl.when(side == 1)
        def _():
            rcopy(src, buf.at[1, step, i], ssem.at[1, step, i], rsem.at[1, step, i], left).start()

    def ysend(src, side, step, i):
        send(yrecv, ys, yr, src, yright, yleft, side, step, i)

    def xsend(src, side, step, i):
        send(xrecv, xs, xr, src, xright, xleft, side, step, i)

    def arrived(buf, ssem, rsem, side, step, i, dev):
        rcopy(buf.at[side, step, i], buf.at[side, step, i], ssem.at[side, step, i], rsem.at[side, step, i], dev).wait_recv()

    def sent(buf, ssem, rsem, side, step, i, dev):
        rcopy(buf.at[side, step, i], buf.at[side, step, i], ssem.at[side, step, i], rsem.at[side, step, i], dev).wait_send()

    def xserve(k):
        s, j = k // 8, lax.rem(k, 8)
        side, i = odd(j), j // 2
        m_load(k + 1).start()
        m_load(k).wait()
        arrived(xrecv, xs, xr, side, s, i, xright)
        xrecv[side, s, i] = xrecv[side, s, i] + mbuf[odd(k)]
        xsend(xrecv.at[side, s, i], side, s + 1, i)

    def gate_up(serve):
        def block(i, size):
            slot = odd(i)
            for c in w_load(i, slot, size):
                c.wait()
            g = lax.dot_general(n2[...], wbuf[slot, 0, pl.ds(0, size)], NT, preferred_element_type=F32)
            u = lax.dot_general(n2[...], wbuf[slot, 1, pl.ds(0, size)], NT, preferred_element_type=F32)
            h[:, pl.ds(pl.multiple_of(i * fb, fb), size)] = (jax.nn.silu(g) * u).astype(BF16)

        def one(i):
            block(i, fb)
            w_start(i + 2)
            serve(i)
        loop(nf, one)
        block(nf, tail)

    def down(use):
        def one(jj):
            sub = odd(jj)
            d_load(jj).wait()
            r = jnp.dot(h[...], dbuf[sub], preferred_element_type=F32)

            @pl.when(jj + 2 < 16)
            def _():
                d_load(jj + 2).start()
            use(jj // 2, sub, window(sub, hw), r)
        loop(16, one)

    a_load(t - 1, 0).start()
    a_load(t + 1, 1).start()
    w_start(0)
    w_start(1)
    entry_barrier((yright, yleft, xright, xleft))

    def x_first(i):
        xsend(m_ref.at[chunk(xc - 1), :, cols(i)], 0, 0, i)
        xsend(m_ref.at[chunk(xc + 1), :, cols(4 + i)], 1, 0, i)
    loop(4, x_first)
    d_load(0).start()
    d_load(1).start()
    m_load(0).start()

    for slot in SIDES:
        a_load(t, slot).wait()
        norm_rows(a_buf.at[slot], n2.at[pl.ds(slot * q, q)], gain, q, 16)
    a_load(t + 2, 0).start()
    a_load(t, 1).start()
    gate_up(lambda i: None)
    w_start(0)
    w_start(1)

    def use1(j, sub, part, r):
        p1[col_of(j), :, part] = r
        side, i = odd(j), j // 2

        @pl.when(sub == 1)
        def _():
            ysend(p1.at[col_of(j), window(side, q)], side, 0, i)
    down(use1)
    d_load(0).start()
    d_load(1).start()

    for slot in SIDES:
        a_load(t, slot).wait()
        norm_rows(a_buf.at[slot], n2.at[pl.ds(slot * q, q)], gain, q, 16)

    def serve2(i):
        @pl.when(i < 8)
        def _():
            xserve(i)
    gate_up(serve2)
    for k in range(min(nf, 8), 8):
        xserve(k)

    def use2(j, sub, part, r):
        side, i = odd(j), j // 2
        p2[col_of(j), :, part] = r[q:]

        @pl.when(sub == 0)
        def _():
            arrived(yrecv, ys, yr, side, 0, i, yright)
        yrecv[side, 0, i, :, part] = yrecv[side, 0, i, :, part] + r[:q]

        @pl.when(sub == 1)
        def _():
            ysend(yrecv.at[side, 0, i], side, 1, i)
    down(use2)

    def third(j):
        side, i = odd(j), j // 2
        xserve(8 + j)
        arrived(yrecv, ys, yr, side, 1, i, yright)
        yrecv[side, 1, i] = yrecv[side, 1, i] + p1[col_of(j), window((1 - side), q)]
        ysend(yrecv.at[side, 1, i], side, 2, i)
    loop(8, third)

    def out_local(cb):
        return pltpu.make_async_copy(n2.at[pl.ds(0, q), cols(cb)], out_ref.at[rows(t), cols(cb)], osem.at[cb])

    def gather(cb, side, dev):
        return rcopy(n2.at[pl.ds(0, q), cols(cb)], out_ref.at[rows(t), cols(cb)], gs.at[side, cb], gr.at[side, cb], dev)

    def last(j):
        side, i = odd(j), j // 2
        cb = col_of(j)
        k = 16 + j

        @pl.when(j + 1 < 8)
        def _():
            m_load(k + 1).start()
        m_load(k).wait()
        arrived(xrecv, xs, xr, side, 2, i, xright)
        arrived(yrecv, ys, yr, side, 2, i, yright)
        b_val = a_buf[1, :, cols(cb)].astype(F32) + (yrecv[side, 2, i] + p2[cb])
        n2[pl.ds(0, q), cols(cb)] = (b_val + (xrecv[side, 2, i] + mbuf[odd(k)])).astype(BF16)
        out_local(cb).start()
        gather(cb, 0, yright).start()
        gather(cb, 1, yleft).start()
    loop(8, last)

    half = q // 2

    def half_rows(c, which):
        return pl.ds(pl.multiple_of(chunk(c) * q + which * half, half), half)

    def forward(c, which, cb, dev):
        ref = out_ref.at[half_rows(c, which), cols(cb)]
        return rcopy(ref, ref, fs.at[which, cb], fr.at[which, cb], dev)

    def pass_on(j):
        cb = col_of(j)
        gather(cb, 0, yright).wait_recv()
        forward(t - 1, 0, cb, yright).start()
        gather(cb, 1, yleft).wait_recv()
        forward(t + 1, 1, cb, yleft).start()
    loop(8, pass_on)

    def finish(j):
        cb = col_of(j)
        out_local(cb).wait()
        for which in SIDES:
            gather(cb, which, yright).wait_send()
            forward(t, which, cb, yright).wait_send()
            forward(t, which, cb, yright).wait_recv()
    loop(8, finish)

    def drain(k):
        step, j = k // 8, lax.rem(k, 8)
        sent(yrecv, ys, yr, odd(j), step, j // 2, yright)
        sent(xrecv, xs, xr, odd(j), step, j // 2, yright)
    loop(24, drain)


def ffn_call(after_attn, wg_t, wu_t, w_down, gain, m_part, fb=256):
    tokens, d_model = after_attn.shape
    f_loc = wg_t.shape[0]
    q = tokens // 4
    cw = d_model // 8
    hbm = pl.BlockSpec(memory_space=pl.ANY)
    vmem = pl.BlockSpec(memory_space=pltpu.VMEM)
    dma = pltpu.SemaphoreType.DMA
    flops = 2 * tokens * d_model * f_loc * 3
    return pl.pallas_call(
        functools.partial(ffn_body, fb),
        out_shape=jax.ShapeDtypeStruct((tokens, d_model), BF16),
        in_specs=[hbm, hbm, hbm, hbm, vmem, hbm],
        out_specs=hbm,
        scratch_shapes=[
            pltpu.VMEM((2, q, d_model), BF16),
            pltpu.VMEM((2 * q, d_model), BF16),
            pltpu.VMEM((2 * q, f_loc), BF16),
            pltpu.VMEM((2, 2, fb, d_model), BF16),
            pltpu.VMEM((2, f_loc, cw // 2), BF16),
            pltpu.VMEM((8, 2 * q, cw), F32),
            pltpu.VMEM((8, q, cw), F32),
            pltpu.VMEM((2, 3, RING, q, cw), F32),
            pltpu.VMEM((2, 3, RING, q, cw), F32),
            pltpu.VMEM((2, q, cw), F32),
            dma((2,)), dma((2, 2)), dma((2,)), dma((2,)), dma((8,)),
        ] + [dma((2, 3, RING))] * RING + [dma((2, 8))] * RING,
        compiler_params=pltpu.CompilerParams(collective_id=2, has_side_effects=True, vmem_limit_bytes=VMEM_LIMIT),
        cost_estimate=pl.CostEstimate(flops=flops, bytes_accessed=4 * tokens * d_model + 12 * f_loc * d_model, transcendentals=tokens * f_loc),
        name='ffn_ring',
    )(after_attn, wg_t, wu_t, w_down, gain, m_part)


def attn_body(x_ref, wq, wk, wv, wo, eg, eu, ed, gain, cosf, sinf, ids, moe_gain, router,
              ctx_all, hid_all, gates_all, w_cols, og, ou, od,
              xv, xn, raw, wide, wb, qb, kb, vb, ctxb, ub, gbuf,
              lsem, rawsem, cls, cs, cr, cfs, cfr, hs, hr, hfs, hfr, gs, gr, was, war, wxs, wxr, wfs, wfr, wds, wdr, es, er):
    t = lax.axis_index('tp')
    e = lax.axis_index('ep')
    core = odd(e)
    xc = e // 2
    tokens, d_model = xv.shape
    heads, hd = wq.shape[1], wq.shape[2]
    q = tokens // 4
    kblk = raw.shape[1]
    nk = d_model // kblk
    width = d_model // 4
    pair = 2 * hd
    pairs = heads // 2

    def y_dev(k):
        return {'tp': lax.rem(t + k + 4, RING)}

    def x_id(k):
        return lax.rem(xc + k + 4, RING) * 2 + core

    def x_dev(k):
        return {'ep': x_id(k)}
    partner = {'ep': xc * 2 + 1 - core}

    own_rows = window(t, q)
    rots = (x_ref, xv)
    load_x = [pltpu.make_async_copy(x_ref.at[pl.ds(k * q, q)], xv.at[pl.ds(k * q, q)], lsem.at[k]) for k in range(RING)]
    for c in load_x:
        c.start()
    mats = (wq, wk, wv)

    def raw_load(m, k):
        sl = window(k, kblk)
        return pltpu.make_async_copy(mats[m].at[sl], raw.at[odd(k)], rawsem.at[odd(k)])
    raw_load(0, 0).start()
    raw_load(0, 1).start()
    entry_barrier((y_dev(1), y_dev(-1), y_dev(2), x_dev(1), x_dev(-1), x_dev(2), partner))

    head_rows = window(e, hd)

    def col_block(c):
        return window(c, width)
    w_own = pltpu.make_async_copy(wo.at[head_rows, col_block(t)], w_cols.at[e, t], lsem.at[4])
    w_own.start()
    swap = [rcopy(wo.at[head_rows, col_block(lax.rem(t + k, RING))], w_cols.at[e, t], was.at[k - 1], war.at[k - 1], y_dev(k)) for k in (1, 2, 3)]
    for c in swap:
        c.start()
    hid = [rcopy(x_ref.at[own_rows], hid_all.at[xc], hs.at[k], hr.at[k], x_dev(1 - 2 * k)) for k in SIDES]
    for c in hid:
        c.start()
    exp = [rcopy(src, dst, es.at[k], er.at[k], partner) for k, (src, dst) in enumerate(((eg, og), (eu, ou), (ed, od)))]
    for c in exp:
        c.start()

    for k in range(RING):
        load_x[k].wait()
        norm_rows(xv.at[pl.ds(k * q, q)], xn.at[pl.ds(k * q, q)], gain, q, 16)
    hid_own = pltpu.make_async_copy(xv.at[own_rows], hid_all.at[xc], lsem.at[5])
    hid_own.start()

    norm_rows(xv.at[own_rows], ub, moe_gain, q, 16)
    logits = jnp.dot(ub[...], router[...], preferred_element_type=F32)
    lane = lax.broadcasted_iota(jnp.int32, logits.shape, 1)
    own_ids = ids[own_rows, :]
    chosen = lane == own_ids[:, 0:1]
    for j in range(1, ids.shape[1]):
        chosen = jnp.logical_or(chosen, lane == own_ids[:, j:j + 1])
    top = jnp.max(jnp.where(chosen, logits, -jnp.inf), axis=-1, keepdims=True)
    p = jnp.where(chosen, jnp.exp(jnp.where(chosen, logits - top, 0.0)), 0.0)
    gbuf[...] = p / jnp.sum(p, axis=-1, keepdims=True)
    gate_own = pltpu.make_async_copy(gbuf, gates_all.at[xc], lsem.at[6])
    gate_own.start()
    gate_out = [rcopy(gbuf, gates_all.at[xc], gs.at[k - 1], gr.at[k - 1], x_dev(k)) for k in (1, 2, 3)]
    for c in gate_out:
        c.start()

    for m in range(3):
        def one(k, m=m):
            slot = odd(k)
            raw_load(m, k).wait()
            wide[...] = raw[slot].astype(F32).reshape(kblk * heads, hd)

            @pl.when(k + 2 < nk)
            def _():
                raw_load(m, k + 2).start()
            rows = window(k, kblk)
            for h in range(heads):
                wb[m, rows, h * hd:(h + 1) * hd] = wide[pl.ds(h, kblk, stride=heads), :].astype(BF16)
        loop(nk, one)
        if m < 2:
            raw_load(m + 1, 0).start()
            raw_load(m + 1, 1).start()

    w_own.wait()
    for c in swap:
        c.wait_recv()
    wx = [rcopy(w_cols.at[e], w_cols.at[e], wxs.at[k], wxr.at[k], x_dev(1 - 2 * k)) for k in SIDES]
    for c in wx:
        c.start()

    def w_core(k):
        return rcopy(w_cols.at[x_id(k)], w_cols.at[x_id(k)], wds.at[k], wdr.at[k], partner)
    w_core(0).start()

    def ctx_cols(g):
        return window(g, pair)

    def ctx_local(g):
        return pltpu.make_async_copy(ctxb.at[g], ctx_all.at[t, :, ctx_cols(g)], cls.at[g])

    def ctx_send(g, side):
        return rcopy(ctxb.at[g], ctx_all.at[t, :, ctx_cols(g)], cs.at[side, g], cr.at[side, g], y_dev(turn(side)))

    def ctx_forward(g, side):
        src = lax.rem(t + 3 + 2 * side, RING)
        ref = ctx_all.at[src, pl.ds(side * (tokens // 2), tokens // 2), ctx_cols(g)]
        return rcopy(ref, ref, cfs.at[side, g], cfr.at[side, g], y_dev(turn(side)))

    def pass_on(g):
        for side in SIDES:
            ctx_send(g, side).wait_recv()
            ctx_forward(g, side).start()

    scale = hd ** -0.5
    tri = lax.broadcasted_iota(jnp.int32, (q, q), 0) >= lax.broadcasted_iota(jnp.int32, (q, q), 1)

    def heads_of(g):
        cols = ctx_cols(g)
        for m, dst in ((0, qb), (1, kb), (2, vb)):
            r = jnp.dot(xn[...], wb[m, :, cols], preferred_element_type=F32)
            if m == 2:
                dst[...] = r.astype(BF16)
            else:
                for h in SIDES:
                    part = r[:, h * hd:(h + 1) * hd]
                    turned = part * cosf[...] + pltpu.roll(part, hd // 2, 1) * sinf[...]
                    dst[:, h * hd:(h + 1) * hd] = turned.astype(BF16)
        for h in SIDES:
            hc = slice(h * hd, (h + 1) * hd)
            for b in range(RING):
                s = lax.dot_general(qb[b * q:(b + 1) * q, hc], kb[0:(b + 1) * q, hc], NT, preferred_element_type=F32) * scale
                diag = jnp.where(tri, s[:, b * q:], -1e30)
                s = diag if b == 0 else jnp.concatenate([s[:, :b * q], diag], axis=1)
                w = jnp.exp(s - jnp.max(s, axis=-1, keepdims=True))
                prob = (w * (1.0 / jnp.sum(w, axis=-1, keepdims=True))).astype(BF16)
                ctxb[g, b * q:(b + 1) * q, hc] = jnp.dot(prob, vb[0:(b + 1) * q, hc], preferred_element_type=F32).astype(BF16)
        ctx_local(g).start()
        ctx_send(g, 0).start()
        ctx_send(g, 1).start()

        @pl.when(g >= 2)
        def _():
            pass_on(g - 2)
    loop(pairs, heads_of)

    def hid_forward(side):
        ref = hid_all.at[lax.rem(xc + 3 + 2 * side, RING), pl.ds(side * (q // 2), q // 2)]
        return rcopy(ref, ref, hfs.at[side], hfr.at[side], x_dev(turn(side)))

    def w_forward(side):
        ref = w_cols.at[x_id(2 * side - 1), pl.ds(2 * side, 2)]
        return rcopy(ref, ref, wfs.at[side], wfr.at[side], x_dev(turn(side)))
    for side in SIDES:
        hid[side].wait_recv()
        hid_forward(side).start()
    pass_on(pairs - 2)
    for side in SIDES:
        wx[side].wait_recv()
        w_forward(side).start()
    w_core(1).start()
    w_core(3).start()
    pass_on(pairs - 1)
    for side in SIDES:
        w_forward(side).wait_recv()
    w_core(2).start()

    for side in SIDES:
        hid_forward(side).wait()
        hid[side].wait_send()
        wx[side].wait_send()
        w_forward(side).wait_send()
        for g in range(pairs):
            ctx_send(g, side).wait_send()
            ctx_forward(g, side).wait()
    for c in swap:
        c.wait_send()
    for c in gate_out:
        c.wait()
    for c in exp:
        c.wait()
    for k in range(RING):
        w_core(k).wait()
    for g in range(pairs):
        ctx_local(g).wait()
    hid_own.wait()
    gate_own.wait()


def attn_call(x, wq, wk, wv, wo, eg, eu, ed, gain, cosf, sinf, ids, moe_gain, router):
    tokens, d_model = x.shape
    heads, hd = wq.shape[1], wq.shape[2]
    q = tokens // 4
    kblk = min(256, d_model)
    experts = router.shape[1]
    hbm = pl.BlockSpec(memory_space=pl.ANY)
    vmem = pl.BlockSpec(memory_space=pltpu.VMEM)
    dma = pltpu.SemaphoreType.DMA
    two, three = dma((2,)), dma((3,))
    sds = jax.ShapeDtypeStruct
    pairs = heads // 2
    return pl.pallas_call(
        attn_body,
        out_shape=(sds((4, tokens, heads * hd), BF16), sds((4, q, d_model), BF16), sds((4, q, experts), F32),
                   sds((8, 4, hd, d_model // 4), BF16), sds(eg.shape, BF16), sds(eu.shape, BF16), sds(ed.shape, BF16)),
        in_specs=[hbm] * 8 + [vmem] * 6,
        out_specs=(hbm,) * 7,
        scratch_shapes=[
            pltpu.VMEM((tokens, d_model), BF16), pltpu.VMEM((tokens, d_model), BF16),
            pltpu.VMEM((2, kblk, heads, hd), BF16), pltpu.VMEM((kblk * heads, hd), F32),
            pltpu.VMEM((3, d_model, heads * hd), BF16),
            pltpu.VMEM((tokens, 2 * hd), BF16), pltpu.VMEM((tokens, 2 * hd), BF16), pltpu.VMEM((tokens, 2 * hd), BF16),
            pltpu.VMEM((pairs, tokens, 2 * hd), BF16), pltpu.VMEM((q, d_model), BF16), pltpu.VMEM((q, experts), F32),
            dma((7,)), two, dma((pairs,)),
        ] + [dma((2, pairs))] * RING + [two] * RING + [three] * RING + [two] * RING + [dma((RING,))] * 2 + [three] * 2,
        compiler_params=pltpu.CompilerParams(collective_id=0, has_side_effects=True, vmem_limit_bytes=VMEM_LIMIT),
        cost_estimate=pl.CostEstimate(flops=2 * tokens * d_model * heads * hd * 3, bytes_accessed=6 * d_model * heads * hd, transcendentals=heads * tokens * tokens),
        name='attn_gather',
    )(x, wq, wk, wv, wo, eg, eu, ed, gain, cosf, sinf, ids, moe_gain, router)


def moe_body(ctx_all, w_cols, x_ref, hid_all, gates_all, eg, eu, ed, og, ou, od, moe_gain, a_full, m_part,
             wcv, cbuf, xbuf, abuf, u, mv, h, wbuf, dbuf, gbuf,
             lsem, csem, xsem, als, as_, ar, fs, fr, hsem, wsem, dsem, msem):
    t = lax.axis_index('tp')
    e = lax.axis_index('ep')
    core = odd(e)
    tokens, d_model = x_ref.shape
    q = tokens // 4
    width = d_model // 4
    local, fe = eg.shape[0], eg.shape[1]
    fb = wbuf.shape[2]
    nfull = fe // fb
    tail = fe - nfull * fb
    sizes = [fb] * nfull + [tail]
    nb = len(sizes)
    cw = dbuf.shape[2]
    nn = d_model // cw

    def y_dev(k):
        return {'tp': lax.rem(t + k + 4, RING)}
    my_cols = window(t, width)

    def rows(c):
        return window(c, q)

    hk = wcv.shape[1]
    load_w = [pltpu.make_async_copy(w_cols.at[:, k], wcv.at[k], lsem.at[k]) for k in range(RING)]
    load_g = pltpu.make_async_copy(gates_all, gbuf, lsem.at[4])

    def ctx_load(c, slot):
        wide = cbuf.shape[2] // 4
        return [pltpu.make_async_copy(ctx_all.at[k, rows(c)], cbuf.at[slot, :, pl.ds(k * wide, wide)], csem.at[slot, k]) for k in range(RING)]

    def x_load(c, slot):
        return pltpu.make_async_copy(x_ref.at[rows(c), my_cols], xbuf.at[slot], xsem.at[slot])

    def hid_load(k):
        return pltpu.make_async_copy(hid_all.at[k], u.at[pl.ds(k * q, q)], hsem.at[k])

    def w_load(k, b, slot, from_own):
        g_ref, u_ref = (eg, eu) if from_own else (og, ou)
        kk = k if from_own else k - local
        sl = pl.ds(b * fb, sizes[b])
        return (pltpu.make_async_copy(g_ref.at[kk, sl], wbuf.at[slot, 0, pl.ds(0, sizes[b])], wsem.at[slot, 0]),
                pltpu.make_async_copy(u_ref.at[kk, sl], wbuf.at[slot, 1, pl.ds(0, sizes[b])], wsem.at[slot, 1]))

    def w_start(k, b):
        slot = odd(k * nb + b)

        @pl.when(k < local)
        def _():
            for c in w_load(k, b, slot, True):
                c.start()

        @pl.when(jnp.logical_and(k >= local, k < 2 * local))
        def _():
            for c in w_load(k, b, slot, False):
                c.start()

    def d_load(k, n, from_own):
        ref = ed if from_own else od
        kk = k if from_own else k - local
        slot = odd(n)
        return pltpu.make_async_copy(ref.at[kk, :, window(n, cw)], dbuf.at[slot], dsem.at[slot])

    def d_start(k, n):
        @pl.when(k < local)
        def _():
            d_load(k, n, True).start()

        @pl.when(jnp.logical_and(k >= local, k < 2 * local))
        def _():
            d_load(k, n, False).start()

    for c in ctx_load(0, 0):
        c.start()
    for c in load_w:
        c.start()
    x_load(0, 0).start()
    entry_barrier((y_dev(1), y_dev(-1)))
    load_g.start()
    for k in range(RING):
        hid_load(k).start()
    for b in SIDES:
        w_start(jnp.int32(0), b)
        d_start(jnp.int32(0), jnp.int32(b))
    for c in load_w:
        c.wait()

    def a_local(c):
        return pltpu.make_async_copy(abuf.at[c], a_full.at[rows(c), my_cols], als.at[c])

    def a_send(c, side):
        return rcopy(abuf.at[c], a_full.at[rows(c), my_cols], as_.at[side, c], ar.at[side, c], y_dev(turn(side)))

    def a_forward(c, side):
        src = lax.rem(t + 3 + 2 * side, RING)
        ref = a_full.at[pl.ds(pl.multiple_of(c * q + side * (q // 2), q // 2), q // 2), window(src, width)]
        return rcopy(ref, ref, fs.at[side, c], fr.at[side, c], y_dev(turn(side)))

    def o_chunk(c):
        slot = odd(c)

        @pl.when(c + 1 < 4)
        def _():
            for d in ctx_load(c + 1, 1 - slot):
                d.start()
            x_load(c + 1, 1 - slot).start()
        for d in ctx_load(c, slot):
            d.wait()
        x_load(c, slot).wait()
        o = jnp.dot(cbuf[slot], wcv[...].reshape(4 * hk * wcv.shape[2], width), preferred_element_type=F32)
        abuf[c] = (xbuf[slot].astype(F32) + o).astype(BF16)
        a_local(c).start()
        a_send(c, 0).start()
        a_send(c, 1).start()
    loop(4, o_chunk)

    for k in range(RING):
        hid_load(k).wait()
        norm_rows(u.at[pl.ds(k * q, q)], u.at[pl.ds(k * q, q)], moe_gain, q, 16)
    load_g.wait()

    def pass_on(c):
        for side in SIDES:
            a_send(c, side).wait_recv()
            a_forward(c, side).start()

    def m_out(n):
        cols = window(n, cw)
        return pltpu.make_async_copy(mv.at[n], m_part.at[:, cols], msem.at[n])

    def expert(k):
        which = jnp.where(k < local, e * local + k, (xc2 + 1 - core) * local + k - local)
        gate_all = gbuf[...].reshape(tokens, gbuf.shape[2])
        lane = lax.broadcasted_iota(jnp.int32, gate_all.shape, 1)
        weight = jnp.sum(jnp.where(lane == which, gate_all, 0.0), axis=1, keepdims=True)
        for b, size in enumerate(sizes):
            slot = odd(k * nb + b)
            for c in w_load(0, b, slot, True):
                c.wait()
            g = lax.dot_general(u[...], wbuf[slot, 0, 0:size], NT, preferred_element_type=F32)
            v = lax.dot_general(u[...], wbuf[slot, 1, 0:size], NT, preferred_element_type=F32)
            h[:, b * fb:b * fb + size] = (jax.nn.silu(g) * v).astype(BF16)
            nxt = b + 2
            w_start(k + nxt // nb, nxt % nb)

        def block(n):
            d_load(0, n, True).wait()
            y = jnp.dot(h[...], dbuf[odd(n)], preferred_element_type=F32).astype(BF16)
            term = jnp.where(weight > 0.0, weight * y.astype(F32), 0.0)

            @pl.when(n + 2 < nn)
            def _():
                d_start(k, n + 2)

            @pl.when(n + 2 >= nn)
            def _():
                d_start(k + 1, n + 2 - nn)

            @pl.when(k == 0)
            def _():
                mv[n] = term

            @pl.when(k > 0)
            def _():
                mv[n] = mv[n] + term

            @pl.when(k == 2 * local - 1)
            def _():
                m_out(n).start()
        loop(nn, block)

        @pl.when(k >= 0)
        def _():
            pass_on(k)
    xc2 = e - core
    loop(2 * local, expert)

    for c in range(RING):
        a_local(c).wait()
        for side in SIDES:
            a_send(c, side).wait_send()
            a_forward(c, side).wait()

    def finish(n):
        m_out(n).wait()
    loop(nn, finish)


def moe_call(ctx_all, w_cols, x, hid_all, gates_all, eg, eu, ed, og, ou, od, moe_gain, fb=256, cw=512):
    tokens, d_model = x.shape
    q = tokens // 4
    width = d_model // 4
    hd = w_cols.shape[2]
    local, fe = eg.shape[0], eg.shape[1]
    assert 2 * local == 4
    hbm = pl.BlockSpec(memory_space=pl.ANY)
    vmem = pl.BlockSpec(memory_space=pltpu.VMEM)
    dma = pltpu.SemaphoreType.DMA
    sds = jax.ShapeDtypeStruct
    nn = d_model // cw
    return pl.pallas_call(
        moe_body,
        out_shape=(sds((tokens, d_model), BF16), sds((tokens, d_model), F32)),
        in_specs=[hbm] * 11 + [vmem],
        out_specs=(hbm, hbm),
        scratch_shapes=[
            pltpu.VMEM((4, 8, hd, width), BF16), pltpu.VMEM((2, q, 4 * 8 * hd), BF16), pltpu.VMEM((2, q, width), BF16),
            pltpu.VMEM((4, q, width), BF16), pltpu.VMEM((tokens, d_model), BF16),
            pltpu.VMEM((nn, tokens, cw), F32), pltpu.VMEM((tokens, fe), BF16), pltpu.VMEM((2, 2, fb, d_model), BF16),
            pltpu.VMEM((2, fe, cw), BF16), pltpu.VMEM(gates_all.shape, F32),
            dma((5,)), dma((2, RING)), dma((2,)), dma((RING,)),
        ] + [dma((2, RING))] * RING + [dma((RING,)), dma((2, 2)), dma((2,)), dma((nn,))],
        compiler_params=pltpu.CompilerParams(collective_id=1, has_side_effects=True, vmem_limit_bytes=VMEM_LIMIT),
        cost_estimate=pl.CostEstimate(flops=2 * tokens * d_model * fe * 3 * 4, bytes_accessed=24 * fe * d_model, transcendentals=4 * tokens * fe),
        name='moe_gather',
    )(ctx_all, w_cols, x, hid_all, gates_all, eg, eu, ed, og, ou, od, moe_gain)


def rope_tables(seq_len, head_dim):
    inv_freq = ROPE_BASE ** (-jnp.arange(head_dim // 2, dtype=F32) * (2.0 / head_dim))
    angle = jnp.arange(seq_len, dtype=F32)[:, None] * inv_freq[None, :]
    return jnp.cos(angle), jnp.sin(angle)


def solution(mesh, fb=256, cw=512):
    tok_spec = P(('dp', 'ep'), None, None)
    col_spec = P(None, 'tp', None)
    exp_spec = P('ep', None, None)
    in_specs = (tok_spec, tok_spec, tok_spec, P(None), col_spec, col_spec, col_spec, P('tp', None, None), P(None), P(None, 'tp'), P(None, 'tp'), P('tp', None), P(None), P(None, None), exp_spec, exp_spec, exp_spec)

    def layer_local(hidden_in, expert_ids, slot_ids, attn_gain, w_query, w_key, w_value, w_out, ffn_gain, w_gate, w_up, w_down, moe_gain, w_router, exp_gate, exp_up, exp_down):
        num_seqs, seq_len, d_model = hidden_in.shape
        tokens = num_seqs * seq_len
        heads, head_dim = w_out.shape[0], w_out.shape[1]
        x = hidden_in.reshape(tokens, d_model)
        ids = expert_ids.reshape(tokens, expert_ids.shape[2])
        cos_tab, sin_tab = rope_tables(seq_len, head_dim)
        cosf = jnp.concatenate([cos_tab, cos_tab], axis=1)
        sinf = jnp.concatenate([-sin_tab, sin_tab], axis=1)
        eg, eu = jnp.swapaxes(exp_gate, 1, 2), jnp.swapaxes(exp_up, 1, 2)
        row = lambda g: g.reshape(1, d_model)
        ctx_all, hid_all, gates_all, w_cols, og, ou, od = attn_call(
            x, w_query, w_key, w_value, w_out.reshape(heads * head_dim, d_model), eg, eu, exp_down,
            row(attn_gain), cosf, sinf, ids, row(moe_gain), w_router)
        after_attn, m_part = moe_call(ctx_all, w_cols, x, hid_all, gates_all, eg, eu, exp_down, og, ou, od, row(moe_gain), fb=fb, cw=cw)
        out = ffn_call(after_attn, w_gate.T, w_up.T, w_down, row(ffn_gain), m_part.reshape(4, tokens // 4, d_model), fb=fb)
        return out.reshape(hidden_in.shape)

    return jax.shard_map(layer_local, mesh=mesh, in_specs=in_specs, out_specs=tok_spec, check_vma=False)
```

time: 777 us -> 540 us (0.69)
  Pallas kernels: 249 us -> 516 us
  matrix products: 221 us -> 0 us
  waiting for transfers between devices: 109 us -> 0 us
  blocking collectives: 86.3 us -> 0 us
  other arithmetic: 37 us -> 3.35 us
  local copies, waits for them, and re-layouts: 44.1 us -> 15.8 us
  between operations: 13.9 us -> 0.47 us
    pallas_call x0 -> x2, Pallas kernels: none -> 269 us  [the longest x1 139 us: attn_call(): pl.pallas_call(attn_body, out_shape=(sds((4, tokens, heads * hd), BF16),...]
    dot_general x16 -> x0, matrix products: 181 us -> none  [the longest x4 61.4 us: moe_partial(): y_out = jnp.dot(act, exp_down[k], preferred_element_type=F32).astype(BF16)]
    all_gather x4 -> x0, waiting for transfers between devices: 109 us -> none  [the longest x1 69.1 us: layer_local(): lax.all_gather(own, 'ep', axis=0, tiled=False)]
    all_gather x1 -> x0, blocking collectives: 61.3 us -> none  [layer_local(): lax.all_gather(own_ids, 'ep', axis=0, tiled=False)]
    unnamed x2 -> x0, matrix products: 26.2 us -> none
    all_to_all x1 -> x0, blocking collectives: 25 us -> none  [layer_local(): cols = lax.all_to_all(rows, 'tp', 1, 0, tiled=True)]
    unnamed x35 -> x3, local copies, waits for them, and re-layouts: 34.1 us -> 11.9 us
    convert_element_type x4 -> x0, other arithmetic: 21.1 us -> none  [rms_norm(): return (x_f32 * inv_rms * gain.astype(F32)).astype(BF16)]
  transfers between devices with their start and end apart: 7 -> 0, of which waited for: 2 -> 0; matrix products, arithmetic and copies ran while one was open for 24% -> 0% of each run, Pallas kernels for 0% -> 0%
where the time goes in v3:
time: 540 us; the launch traced here: 536 us
  Pallas kernels  516 us (96%)
  local copies, waits for them, and re-layouts  15.8 us (3%)
    pallas_call x1, Pallas kernels, ffn_call(): pl.pallas_call(functools.partial(ffn_body, fb), out_shape=jax.ShapeDtypeS...  248 us
    pallas_call x1, Pallas kernels, attn_call(): pl.pallas_call(attn_body, out_shape=(sds((4, tokens, heads * hd), BF16),...  139 us
    pallas_call x1, Pallas kernels, moe_call(): pl.pallas_call(moe_body, out_shape=(sds((tokens, d_model), BF16), sds((to...  129 us
    unnamed x3, local copies, waits for them, and re-layouts  11.9 us

profile of v3, /device:TPU:97, one launch (start us, length us, event | category | flops | bytes accessed | tf_op | source)
XLA Modules:
  0.0 535.9 jit_solution(3029529301180102356)
XLA Ops:
  0.0 2.0 fusion.2
  2.0 1.4 pad_maximum_fusion
  3.4 1.3 reshape.35.moe_gain
  4.7 2.2 copy.18.router
  6.9 1.8 copy.17
  8.6 1.3 reshape.33.gain
  9.9 139.1 %attn_gather.1 = (bf16[4,1024,1024]{2,1,0:T(8,128)(2,1)}, bf16[4,256,4096]{2,1,0:T(8,128)(2,1)}, f32[4,256,16]{2,1,0:T(8,128)}, bf16[8,4,128,1024]{3,2,1,0:T(8,1...) custom-call(bf16[1024,4096]{1,0:T(8,128)(2,1)} %bitcast.18, ...), custom_call_target="tpu_custom_call" | custom-call | flops 25769803776 | bytes 25165824 | tf_op jit(solution)/shard_map/attn_gather/pallas_call | solution.py:553
  149.0 129.5 %moe_gather.1 = (bf16[1024,4096]{1,0:T(8,128)(2,1)}, f32[1024,4096]{1,0:T(8,128)}) custom-call(bf16[4,1024,1024]{2,1,0:T(8,128)(2,1)} %get-tuple-element.14.ctx_all, bf16[8,4,128,1024]{3,2,1,0:T(8,128)(2,1)} %get-tuple-element.15.w_cols, bf16[1024,4096]{1,0:T(8,128)(2,1)} %bitcast.19, bf16[4,256,4096]{2,1,0:T(8,128)(2,1)} %get-tuple-element.16.hid_all, ...), custom_call_target="tpu_custom_call" | custom-call | flops 69256347648 | bytes 67633152 | tf_op jit(solution)/shard_map/moe_gather/pallas_call | solution.py:775
  278.5 1.3 reshape.36.gain
  279.8 247.7 %ffn_ring.1 = bf16[1024,4096]{1,0:T(8,128)(2,1)} custom-call(bf16[1024,4096]{1,0:T(8,128)(2,1)} %get-tuple-element.21.a_ref, bf16[2752,4096]{1,0:T(8,128)(2,1)} %bitcast.11, bf16[2752,4096]{1,0:T(8,128)(2,1)} %bitcast.12, bf16[2752,4096]{1,0:T(8,128)(2,1)} %wd.1, bf16[1,4096]{1,0:T(2,128)(2,1)} %reshape.36.gain, f32[4,256,4096]{2,1,0:T(8,128)} %bitcast.20), custom_call_target="tpu_custom_call" | custom-call | flops 69256347648 | bytes 152043520 | tf_op jit(solution)/shard_map/ffn_ring/pallas_call | solution.py:316
  527.5 7.9 %copy.20 = bf16[1,1024,4096]{2,1,0:T(8,128)(2,1)} copy(bf16[1,1024,4096]{2,1,0:T(8,128)(2,1)} %bitcast.9) | data formatting | bytes 16777216
  (1 shorter events, 0.0 us)

commit v4 on v2

v4 whole, which is shorter than its diff:
```python
import functools

import jax
import jax.numpy as jnp
import numpy as np
from jax import lax
from jax.experimental import pallas as pl
from jax.experimental.pallas import tpu as pltpu
from jax.sharding import PartitionSpec as P

F32 = jnp.float32
BF16 = jnp.bfloat16
EPS = 1e-6
ROPE_BASE = 10000.0
VMEM_LIMIT = 67043328
MESH = pl.DeviceIdType.MESH
NT = (((1,), (1,)), ((), ()))


RING = 4
SIDES = (0, 1)


def odd(k):
    return lax.rem(k, 2)


def turn(side):
    return 1 - 2 * side


def loop(count, body):
    def step(k, carry):
        body(k)
        return carry
    lax.fori_loop(0, count, step, 0)


def window(index, size):
    return pl.ds(pl.multiple_of(index * size, size), size)


def rcopy(src, dst, ssem, rsem, dev):
    return pltpu.make_async_remote_copy(src_ref=src, dst_ref=dst, send_sem=ssem, recv_sem=rsem, device_id=dev, device_id_type=MESH)


def entry_barrier(neighbours):
    barrier = pltpu.get_barrier_semaphore()
    for dev in neighbours:
        pl.semaphore_signal(barrier, inc=1, device_id=dev, device_id_type=MESH)
    pl.semaphore_wait(barrier, len(neighbours))


def norm_rows(src, dst, gain, rows, step):
    def one(r):
        sl = window(r, step)
        x = src[sl, :].astype(F32)
        inv = lax.rsqrt(jnp.mean(x * x, axis=-1, keepdims=True) + EPS)
        dst[sl, :] = (x * inv * gain[...].astype(F32).reshape(1, -1)).astype(BF16)
    loop(rows // step, one)


def ffn_body(fb, a_ref, wg, wu, wd, gain, m_ref, out_ref,
             a_buf, n2, h, wbuf, dbuf, p1, p2, yrecv, xrecv, mbuf,
             asem, wsem, dsem, msem, osem, ys, yr, xs, xr, gs, gr, fs, fr):
    t = lax.axis_index('tp')
    e = lax.axis_index('ep')
    big = odd(e)
    xc = e // 2
    q = a_buf.shape[1]
    d_model = a_buf.shape[2]
    f_loc = wg.shape[0]
    cw = d_model // 8
    hw = cw // 2
    nf = f_loc // fb
    tail = f_loc - nf * fb
    yright, yleft = {'tp': lax.rem(t + 1, RING)}, {'tp': lax.rem(t + 3, RING)}
    xright, xleft = {'ep': lax.rem(xc + 1, RING) * 2 + big}, {'ep': lax.rem(xc + 3, RING) * 2 + big}

    def cols(cb):
        return window(cb, cw)

    def chunk(c):
        return lax.rem(c + 8, RING)

    def rows(c):
        return window(chunk(c), q)

    def a_load(c, slot):
        return pltpu.make_async_copy(a_ref.at[rows(c)], a_buf.at[slot], asem.at[slot])

    def w_load(i, slot, size):
        sl = pl.ds(pl.multiple_of(i * fb, fb), size)
        return (pltpu.make_async_copy(wg.at[sl], wbuf.at[slot, 0, pl.ds(0, size)], wsem.at[slot, 0]),
                pltpu.make_async_copy(wu.at[sl], wbuf.at[slot, 1, pl.ds(0, size)], wsem.at[slot, 1]))

    def w_start(i):
        slot = odd(i)

        @pl.when(i < nf)
        def _():
            for c in w_load(i, slot, fb):
                c.start()

        @pl.when(i == nf)
        def _():
            for c in w_load(nf, slot, tail):
                c.start()

    def col_of(j):
        return odd(j) * 4 + j // 2

    def d_load(jj):
        slot = odd(jj)
        start = pl.multiple_of(col_of(jj // 2) * cw + slot * hw, hw)
        return pltpu.make_async_copy(wd.at[:, pl.ds(start, hw)], dbuf.at[slot], dsem.at[slot])

    def m_load(k):
        s, j = k // 8 + 1, lax.rem(k, 8)
        side = odd(j)
        c = lax.rem(xc + (2 * side - 1) * (1 + s) + 8, RING)
        slot = odd(k)
        return pltpu.make_async_copy(m_ref.at[c, :, cols(col_of(j))], mbuf.at[slot], msem.at[slot])

    def send(buf, ssem, rsem, src, right, left, side, step, i):
        @pl.when(side == 0)
        def _():
            rcopy(src, buf.at[0, step, i], ssem.at[0, step, i], rsem.at[0, step, i], right).start()

        @pl.when(side == 1)
        def _():
            rcopy(src, buf.at[1, step, i], ssem.at[1, step, i], rsem.at[1, step, i], left).start()

    def ysend(src, side, step, i):
        send(yrecv, ys, yr, src, yright, yleft, side, step, i)

    def xsend(src, side, step, i):
        send(xrecv, xs, xr, src, xright, xleft, side, step, i)

    def arrived(buf, ssem, rsem, side, step, i, dev):
        rcopy(buf.at[side, step, i], buf.at[side, step, i], ssem.at[side, step, i], rsem.at[side, step, i], dev).wait_recv()

    def sent(buf, ssem, rsem, side, step, i, dev):
        rcopy(buf.at[side, step, i], buf.at[side, step, i], ssem.at[side, step, i], rsem.at[side, step, i], dev).wait_send()

    def xserve(k):
        s, j = k // 8, lax.rem(k, 8)
        side, i = odd(j), j // 2
        m_load(k + 1).start()
        m_load(k).wait()
        arrived(xrecv, xs, xr, side, s, i, xright)
        xrecv[side, s, i] = xrecv[side, s, i] + mbuf[odd(k)]
        xsend(xrecv.at[side, s, i], side, s + 1, i)

    def gate_up(serve):
        def block(i, size):
            slot = odd(i)
            for c in w_load(i, slot, size):
                c.wait()
            g = lax.dot_general(n2[...], wbuf[slot, 0, pl.ds(0, size)], NT, preferred_element_type=F32)
            u = lax.dot_general(n2[...], wbuf[slot, 1, pl.ds(0, size)], NT, preferred_element_type=F32)
            h[:, pl.ds(pl.multiple_of(i * fb, fb), size)] = (jax.nn.silu(g) * u).astype(BF16)

        def one(i):
            block(i, fb)
            w_start(i + 2)
            serve(i)
        loop(nf, one)
        block(nf, tail)

    def down(use):
        def one(jj):
            sub = odd(jj)
            d_load(jj).wait()
            r = jnp.dot(h[...], dbuf[sub], preferred_element_type=F32)

            @pl.when(jj + 2 < 16)
            def _():
                d_load(jj + 2).start()
            use(jj // 2, sub, window(sub, hw), r)
        loop(16, one)

    a_load(t - 1, 0).start()
    a_load(t + 1, 1).start()
    w_start(0)
    w_start(1)
    entry_barrier((yright, yleft, xright, xleft))

    def x_first(i):
        xsend(m_ref.at[chunk(xc - 1), :, cols(i)], 0, 0, i)
        xsend(m_ref.at[chunk(xc + 1), :, cols(4 + i)], 1, 0, i)
    loop(4, x_first)
    d_load(0).start()
    d_load(1).start()
    m_load(0).start()

    for slot in SIDES:
        a_load(t, slot).wait()
        norm_rows(a_buf.at[slot], n2.at[pl.ds(slot * q, q)], gain, q, 16)
    a_load(t + 2, 0).start()
    a_load(t, 1).start()
    gate_up(lambda i: None)
    w_start(0)
    w_start(1)

    def use1(j, sub, part, r):
        p1[col_of(j), :, part] = r
        side, i = odd(j), j // 2

        @pl.when(sub == 1)
        def _():
            ysend(p1.at[col_of(j), window(side, q)], side, 0, i)
    down(use1)
    d_load(0).start()
    d_load(1).start()

    for slot in SIDES:
        a_load(t, slot).wait()
        norm_rows(a_buf.at[slot], n2.at[pl.ds(slot * q, q)], gain, q, 16)

    def serve2(i):
        @pl.when(i < 8)
        def _():
            xserve(i)
    gate_up(serve2)
    for k in range(min(nf, 8), 8):
        xserve(k)

    def use2(j, sub, part, r):
        side, i = odd(j), j // 2
        p2[col_of(j), :, part] = r[q:]

        @pl.when(sub == 0)
        def _():
            arrived(yrecv, ys, yr, side, 0, i, yright)
        yrecv[side, 0, i, :, part] = yrecv[side, 0, i, :, part] + r[:q]

        @pl.when(sub == 1)
        def _():
            ysend(yrecv.at[side, 0, i], side, 1, i)
    down(use2)

    def third(j):
        side, i = odd(j), j // 2
        xserve(8 + j)
        arrived(yrecv, ys, yr, side, 1, i, yright)
        yrecv[side, 1, i] = yrecv[side, 1, i] + p1[col_of(j), window((1 - side), q)]
        ysend(yrecv.at[side, 1, i], side, 2, i)
    loop(8, third)

    def out_local(cb):
        return pltpu.make_async_copy(n2.at[pl.ds(0, q), cols(cb)], out_ref.at[rows(t), cols(cb)], osem.at[cb])

    def gather(cb, side, dev):
        return rcopy(n2.at[pl.ds(0, q), cols(cb)], out_ref.at[rows(t), cols(cb)], gs.at[side, cb], gr.at[side, cb], dev)

    def last(j):
        side, i = odd(j), j // 2
        cb = col_of(j)
        k = 16 + j

        @pl.when(j + 1 < 8)
        def _():
            m_load(k + 1).start()
        m_load(k).wait()
        arrived(xrecv, xs, xr, side, 2, i, xright)
        arrived(yrecv, ys, yr, side, 2, i, yright)
        b_val = a_buf[1, :, cols(cb)].astype(F32) + (yrecv[side, 2, i] + p2[cb])
        n2[pl.ds(0, q), cols(cb)] = (b_val + (xrecv[side, 2, i] + mbuf[odd(k)])).astype(BF16)
        out_local(cb).start()
        gather(cb, 0, yright).start()
        gather(cb, 1, yleft).start()
    loop(8, last)

    half = q // 2

    def half_rows(c, which):
        return pl.ds(pl.multiple_of(chunk(c) * q + which * half, half), half)

    def forward(c, which, cb, dev):
        ref = out_ref.at[half_rows(c, which), cols(cb)]
        return rcopy(ref, ref, fs.at[which, cb], fr.at[which, cb], dev)

    def pass_on(j):
        cb = col_of(j)
        gather(cb, 0, yright).wait_recv()
        forward(t - 1, 0, cb, yright).start()
        gather(cb, 1, yleft).wait_recv()
        forward(t + 1, 1, cb, yleft).start()
    loop(8, pass_on)

    def finish(j):
        cb = col_of(j)
        out_local(cb).wait()
        for which in SIDES:
            gather(cb, which, yright).wait_send()
            forward(t, which, cb, yright).wait_send()
            forward(t, which, cb, yright).wait_recv()
    loop(8, finish)

    def drain(k):
        step, j = k // 8, lax.rem(k, 8)
        sent(yrecv, ys, yr, odd(j), step, j // 2, yright)
        sent(xrecv, xs, xr, odd(j), step, j // 2, yright)
    loop(24, drain)


def ffn_call(after_attn, wg_t, wu_t, w_down, gain, m_part):
    tokens, d_model = after_attn.shape
    f_loc = wg_t.shape[0]
    fb = 256 if f_loc > 512 else 128
    q = tokens // 4
    cw = d_model // 8
    hbm = pl.BlockSpec(memory_space=pl.ANY)
    vmem = pl.BlockSpec(memory_space=pltpu.VMEM)
    dma = pltpu.SemaphoreType.DMA
    flops = 2 * tokens * d_model * f_loc * 3
    return pl.pallas_call(
        functools.partial(ffn_body, fb),
        out_shape=jax.ShapeDtypeStruct((tokens, d_model), BF16),
        in_specs=[hbm, hbm, hbm, hbm, vmem, hbm],
        out_specs=hbm,
        scratch_shapes=[
            pltpu.VMEM((2, q, d_model), BF16),
            pltpu.VMEM((2 * q, d_model), BF16),
            pltpu.VMEM((2 * q, f_loc), BF16),
            pltpu.VMEM((2, 2, fb, d_model), BF16),
            pltpu.VMEM((2, f_loc, cw // 2), BF16),
            pltpu.VMEM((8, 2 * q, cw), F32),
            pltpu.VMEM((8, q, cw), F32),
            pltpu.VMEM((2, 3, RING, q, cw), F32),
            pltpu.VMEM((2, 3, RING, q, cw), F32),
            pltpu.VMEM((2, q, cw), F32),
            dma((2,)), dma((2, 2)), dma((2,)), dma((2,)), dma((8,)),
        ] + [dma((2, 3, RING))] * RING + [dma((2, 8))] * RING,
        compiler_params=pltpu.CompilerParams(collective_id=2, has_side_effects=True, vmem_limit_bytes=VMEM_LIMIT),
        cost_estimate=pl.CostEstimate(flops=flops, bytes_accessed=4 * tokens * d_model + 12 * f_loc * d_model, transcendentals=tokens * f_loc),
        name='ffn_ring',
    )(after_attn, wg_t, wu_t, w_down, gain, m_part)


def front_body(x_ref, wq, wk, wv, wo, eg, eu, ed, attn_gain, moe_gain, freq, ids, router,
               a_full, m_part, ctx_all, hid_all, ids_all, w_cols, og, ou, od,
               xn, ctxb, abuf, gate, idf, rope,
               lsem, rawsem, cls, als, cs, cr, cfs, cfr, as_, ar, afs, afr, hs, hr, hfs, hfr, ws, wr, wxs, wxr, wfs, wfr,
               wds, wdr, ins, inr, es, er, csem, xsem, usem, wsem, dsem, msem):
    t = lax.axis_index('tp')
    e = lax.axis_index('ep')
    core = odd(e)
    xc = e // 2
    tokens, d_model = xn.shape
    heads, hd = wq.shape[1], wq.shape[2]
    q = tokens // RING
    half = q // 2
    width = d_model // RING
    kblk = min(256, d_model)
    nk = d_model // kblk
    pair = 2 * hd
    pairs = heads // 2
    local, fe = eg.shape[0], eg.shape[1]
    top_k = ids.shape[0]
    partner = {'ep': xc * 2 + 1 - core}

    def ring(k):
        return lax.rem(k + RING, RING)

    def y_dev(k):
        return {'tp': ring(t + k)}

    def x_id(k):
        return ring(xc + k) * 2 + core

    def x_dev(k):
        return {'ep': x_id(k)}

    def w_swap(k):
        return rcopy(wo.at[window(e, hd), window(ring(t + k), width)], w_cols.at[e, t], ws.at[k - 1], wr.at[k - 1], y_dev(k))

    def w_round(side):
        return rcopy(w_cols.at[e], w_cols.at[e], wxs.at[side], wxr.at[side], x_dev(turn(side)))

    def w_forward(side):
        ref = w_cols.at[x_id(2 * side - 1), pl.ds(2 * side, 2)]
        return rcopy(ref, ref, wfs.at[side], wfr.at[side], x_dev(turn(side)))

    def w_core(k):
        return rcopy(w_cols.at[x_id(k)], w_cols.at[x_id(k)], wds.at[k], wdr.at[k], partner)

    def hid_send(part, side):
        rows = pl.ds(pl.multiple_of(t * q + part * half, half), half)
        return rcopy(x_ref.at[rows], hid_all.at[xc, part], hs.at[part, side], hr.at[part, side], x_dev(turn(side)))

    def hid_forward(part, side):
        ref = hid_all.at[ring(xc + 2 * side - 1), part, pl.ds(side * (half // 2), half // 2)]
        return rcopy(ref, ref, hfs.at[part, side], hfr.at[part, side], x_dev(turn(side)))

    def ids_send(k):
        return rcopy(ids.at[:, window(t, q)], ids_all.at[xc], ins.at[k - 1], inr.at[k - 1], x_dev(k))

    mats = ((eg, og), (eu, ou), (ed, od))

    def swap_mat(k, i):
        return rcopy(mats[i][0].at[k], mats[i][1].at[k], es.at[k, i], er.at[k, i], partner)

    def ctx_local(g):
        return pltpu.make_async_copy(ctxb.at[g], ctx_all.at[t, :, window(g, pair)], cls.at[g])

    def ctx_send(g, side):
        return rcopy(ctxb.at[g], ctx_all.at[t, :, window(g, pair)], cs.at[side, g], cr.at[side, g], y_dev(turn(side)))

    def ctx_forward(g, side):
        ref = ctx_all.at[ring(t + 2 * side - 1), pl.ds(side * (tokens // 2), tokens // 2), window(g, pair)]
        return rcopy(ref, ref, cfs.at[side, g], cfr.at[side, g], y_dev(turn(side)))

    def ctx_pass(g):
        for side in SIDES:
            ctx_send(g, side).wait_recv()
            ctx_forward(g, side).start()

    def a_local(c):
        return pltpu.make_async_copy(abuf.at[c], a_full.at[window(c, q), window(t, width)], als.at[c])

    def a_send(c, side):
        return rcopy(abuf.at[c], a_full.at[window(c, q), window(t, width)], as_.at[side, c], ar.at[side, c], y_dev(turn(side)))

    def a_forward(c, side):
        rows = pl.ds(pl.multiple_of(c * q + side * half, half), half)
        ref = a_full.at[rows, window(ring(t + 2 * side - 1), width)]
        return rcopy(ref, ref, afs.at[side, c], afr.at[side, c], y_dev(turn(side)))

    def a_pass(c):
        for side in SIDES:
            a_send(c, side).wait_recv()
            a_forward(c, side).start()

    load_x = [pltpu.make_async_copy(x_ref.at[pl.ds(k * q, q)], xn.at[pl.ds(k * q, q)], lsem.at[k]) for k in range(RING)]
    for c in load_x:
        c.start()
    w_own = pltpu.make_async_copy(wo.at[window(e, hd), window(t, width)], w_cols.at[e, t], lsem.at[RING])
    ids_own = pltpu.make_async_copy(ids.at[:, window(t, q)], ids_all.at[xc], lsem.at[RING + 1])

    def attention(raw, wide, wb, qb, kb, vb):
        proj = (wq, wk, wv)

        def raw_load(m, k):
            return pltpu.make_async_copy(proj[m].at[window(k, kblk)], raw.at[odd(k)], rawsem.at[odd(k)])
        for k in SIDES:
            raw_load(0, k).start()
        entry_barrier((y_dev(1), y_dev(-1), y_dev(2), x_dev(1), x_dev(-1), x_dev(2), partner))
        w_own.start()
        ids_own.start()
        for k in range(1, RING):
            w_swap(k).start()
            ids_send(k).start()
        for side in SIDES:
            hid_send(0, side).start()
        for i in range(len(mats)):
            swap_mat(0, i).start()

        sign = jnp.where(lax.broadcasted_iota(jnp.int32, (1, hd), 1) < hd // 2, -1.0, 1.0)
        steps = min(128, tokens)

        def angles(k):
            angle = (lax.broadcasted_iota(jnp.int32, (steps, 1), 0) + k * steps).astype(F32) * freq[...]
            rope[0, window(k, steps)] = jnp.cos(angle)
            rope[1, window(k, steps)] = jnp.sin(angle) * sign
        loop(tokens // steps, angles)

        for k in range(RING):
            load_x[k].wait()
            norm_rows(xn.at[pl.ds(k * q, q)], xn.at[pl.ds(k * q, q)], attn_gain, q, 16)

        for m in range(len(proj)):
            def one(k, m=m):
                raw_load(m, k).wait()
                wide[...] = raw[odd(k)].astype(F32).reshape(kblk * heads, hd)

                @pl.when(k + 2 < nk)
                def _():
                    raw_load(m, k + 2).start()
                for h in range(heads):
                    wb[m, window(k, kblk), h * hd:(h + 1) * hd] = wide[pl.ds(h, kblk, stride=heads), :].astype(BF16)
            loop(nk, one)
            if m + 1 < len(proj):
                for k in SIDES:
                    raw_load(m + 1, k).start()

        w_own.wait()
        for k in range(1, RING):
            w_swap(k).wait_recv()
        for side in SIDES:
            w_round(side).start()
        w_core(0).start()

        scale = hd ** -0.5
        tri = lax.broadcasted_iota(jnp.int32, (q, q), 0) >= lax.broadcasted_iota(jnp.int32, (q, q), 1)

        def heads_of(g):
            for m, dst in enumerate((qb, kb, vb)):
                r = jnp.dot(xn[...], wb[m, :, window(g, pair)], preferred_element_type=F32)
                if dst is vb:
                    dst[...] = r.astype(BF16)
                else:
                    for h in SIDES:
                        part = r[:, h * hd:(h + 1) * hd]
                        turned = part * rope[0] + pltpu.roll(part, hd // 2, 1) * rope[1]
                        dst[:, h * hd:(h + 1) * hd] = turned.astype(BF16)
            for h in SIDES:
                hc = slice(h * hd, (h + 1) * hd)
                for b in range(RING):
                    s = lax.dot_general(qb[b * q:(b + 1) * q, hc], kb[0:(b + 1) * q, hc], NT, preferred_element_type=F32) * scale
                    diag = jnp.where(tri, s[:, b * q:], -1e30)
                    s = diag if b == 0 else jnp.concatenate([s[:, :b * q], diag], axis=1)
                    w = jnp.exp(s - jnp.max(s, axis=-1, keepdims=True))
                    prob = (w * (1.0 / jnp.sum(w, axis=-1, keepdims=True))).astype(BF16)
                    ctxb[g, b * q:(b + 1) * q, hc] = jnp.dot(prob, vb[0:(b + 1) * q, hc], preferred_element_type=F32).astype(BF16)
            ctx_local(g).start()
            for side in SIDES:
                ctx_send(g, side).start()

            @pl.when(g == 0)
            def _():
                for side in SIDES:
                    hid_send(0, side).wait_recv()
                    hid_forward(0, side).start()

            @pl.when(g >= 2)
            def _():
                ctx_pass(g - 2)

            @pl.when(g == 2)
            def _():
                for side in SIDES:
                    w_round(side).wait_recv()
                    w_forward(side).start()
                w_core(1).start()
                w_core(RING - 1).start()

            @pl.when(g == pairs - 1)
            def _():
                for side in SIDES:
                    hid_send(1, side).start()
        loop(pairs, heads_of)

    pl.run_scoped(attention, pltpu.VMEM((2, kblk, heads, hd), BF16), pltpu.VMEM((kblk * heads, hd), F32),
                  pltpu.VMEM((len(SIDES) + 1, d_model, heads * hd), BF16), *[pltpu.VMEM((tokens, pair), BF16)] * (len(SIDES) + 1))

    def experts(wcv, cbuf, xbuf, mv, act, wbuf, dbuf):
        fb = wbuf.shape[2]
        sizes = [fb] * (fe // fb) + [fe % fb]
        nb = len(sizes)
        cw = dbuf.shape[2]
        nn = d_model // cw
        passes = 4 * local
        last = passes - 2

        def expert_of(p):
            late = p // last
            return (1 - late) * lax.rem(p, 3) + late * 3

        def half_of(p):
            late = p // last
            return (1 - late) * (p // 3) + late * (p - last)

        def w_load(k, b, slot, own):
            k = k if own else k - local
            rows = pl.ds(b * fb, sizes[b])
            return [pltpu.make_async_copy(ref.at[k, rows], wbuf.at[slot, i, pl.ds(0, sizes[b])], wsem.at[slot, i])
                    for i, ref in enumerate((eg, eu) if own else (og, ou))]

        def d_load(k, n, own):
            return pltpu.make_async_copy((ed if own else od).at[k if own else k - local, :, window(n, cw)], dbuf.at[odd(n)], dsem.at[odd(n)])

        def either(p, start):
            k = expert_of(p)

            @pl.when(jnp.logical_and(p < passes, k < local))
            def _():
                start(k, True)

            @pl.when(jnp.logical_and(p < passes, k >= local))
            def _():
                start(k, False)

        def w_start(p, b):
            def go(k, own):
                for c in w_load(k, b, odd(p * nb + b), own):
                    c.start()
            either(p, go)

        def d_start(p, n):
            either(p, lambda k, own: d_load(k, n, own).start())

        def u_rows(part, k):
            return xn.at[pl.ds(pl.multiple_of((part * RING + k) * half, half), half)]

        def u_ready(part):
            for k in range(RING):
                @pl.when(k == xc)
                def _():
                    rows = pl.ds(pl.multiple_of(t * q + part * half, half), half)
                    pltpu.make_async_copy(x_ref.at[rows], u_rows(part, k), usem.at[k]).start()

                @pl.when(k != xc)
                def _():
                    pltpu.make_async_copy(hid_all.at[k, part], u_rows(part, k), usem.at[k]).start()
            for k in range(RING):
                pltpu.make_async_copy(hid_all.at[k, part], u_rows(part, k), usem.at[k]).wait()
            rows = RING * half
            u = xn.at[pl.ds(part * rows, rows)]
            norm_rows(u, u, moe_gain, rows, 16)
            logits = lax.dot_general(u[...], router[...], NT, preferred_element_type=F32)
            lane = lax.broadcasted_iota(jnp.int32, logits.shape, 1).astype(F32)
            picks = jnp.concatenate([idf[k, :, part * half:(part + 1) * half].astype(F32) for k in range(RING)], axis=1).T
            chosen = lane == picks[:, 0:1]
            for j in range(1, top_k):
                chosen = jnp.logical_or(chosen, lane == picks[:, j:j + 1])
            top = jnp.max(jnp.where(chosen, logits, -jnp.inf), axis=-1, keepdims=True)
            w = jnp.where(chosen, jnp.exp(jnp.where(chosen, logits - top, 0.0)), 0.0)
            gate[part] = w / jnp.sum(w, axis=-1, keepdims=True)

        def ctx_load(c):
            return [pltpu.make_async_copy(ctx_all.at[k, window(c, q)], cbuf.at[odd(c), :, pl.ds(k * heads * hd, heads * hd)], csem.at[odd(c), k]) for k in range(RING)]

        def x_load(c):
            return pltpu.make_async_copy(x_ref.at[window(c, q), window(t, width)], xbuf.at[odd(c)], xsem.at[odd(c)])

        load_w = [pltpu.make_async_copy(w_cols.at[:, k], wcv.at[k], lsem.at[k]) for k in range(RING)]

        def attention_out():
            for side in SIDES:
                for g in range(pairs):
                    ctx_forward(g, side).wait_recv()
            for g in range(pairs):
                ctx_local(g).wait()
            for c in ctx_load(jnp.int32(0)):
                c.start()
            x_load(jnp.int32(0)).start()
            for c in load_w:
                c.wait()

            def chunk(c):
                @pl.when(c + 1 < RING)
                def _():
                    for d in ctx_load(c + 1):
                        d.start()
                    x_load(c + 1).start()
                for d in ctx_load(c):
                    d.wait()
                x_load(c).wait()
                o = jnp.dot(cbuf[odd(c)], wcv[...].reshape(RING * heads * hd, width), preferred_element_type=F32)
                abuf[c] = (xbuf[odd(c)].astype(F32) + o).astype(BF16)
                a_local(c).start()
                for side in SIDES:
                    a_send(c, side).start()
            loop(RING, chunk)

        def m_out(part, n):
            return pltpu.make_async_copy(mv.at[part, n], m_part.at[:, part, :, window(n, cw)], msem.at[part, n])

        for b in SIDES:
            w_start(jnp.int32(0), b)
            d_start(jnp.int32(0), jnp.int32(b))
        ids_own.wait()
        for k in range(1, RING):
            ids_send(k).wait_recv()
        load_i = pltpu.make_async_copy(ids_all, idf.at[:, pl.ds(0, top_k)], lsem.at[RING + 1])
        load_i.start()
        for side in SIDES:
            hid_forward(0, side).wait_recv()
        load_i.wait()
        u_ready(0)

        def one_pass(p):
            @pl.when(p == 1)
            def _():
                ctx_pass(pairs - 2)
                for side in SIDES:
                    w_forward(side).wait_recv()
                w_core(2).start()
                for i in range(len(mats)):
                    swap_mat(1, i).start()

            @pl.when(p == 2)
            def _():
                for k in range(RING):
                    w_core(k).wait_recv()
                for c in load_w:
                    c.start()

            @pl.when(p == 3)
            def _():
                ctx_pass(pairs - 1)
                for side in SIDES:
                    hid_send(1, side).wait_recv()
                    hid_forward(1, side).start()
                attention_out()
                for side in SIDES:
                    hid_forward(1, side).wait_recv()
                u_ready(1)

            @pl.when(p >= RING)
            def _():
                a_pass(p - RING)
            k, part = expert_of(p), half_of(p)
            which = (k // local) * ((e + 1 - 2 * core) * local + k - local) + (1 - k // local) * (e * local + k)
            rows = RING * half
            u = xn.at[pl.ds(pl.multiple_of(part * rows, rows), rows)]
            lane = lax.broadcasted_iota(jnp.int32, gate.shape[1:], 1)
            weight = jnp.sum(jnp.where(lane == which, gate[part], 0.0), axis=1, keepdims=True)

            def arrived(which_mats):
                for late, when in enumerate((1, last - 1)):
                    @pl.when(p == when)
                    def _():
                        for i in which_mats:
                            swap_mat(late, i).wait_recv()
            for b, size in enumerate(sizes):
                slot = odd(p * nb + b)
                for c in w_load(0, b, slot, True):
                    c.wait()
                g = lax.dot_general(u[...], wbuf[slot, 0, 0:size], NT, preferred_element_type=F32)
                v = lax.dot_general(u[...], wbuf[slot, 1, 0:size], NT, preferred_element_type=F32)
                act[:, b * fb:b * fb + size] = (jax.nn.silu(g) * v).astype(BF16)
                nxt = b + 2
                if nxt == nb:
                    arrived(SIDES)
                w_start(p + nxt // nb, nxt % nb)

            def block(n):
                d_load(0, n, True).wait()
                y = jnp.dot(act[...], dbuf[odd(n)], preferred_element_type=F32).astype(BF16)
                term = jnp.where(weight > 0.0, weight * y.astype(F32), 0.0).reshape(mv.shape[2:])

                @pl.when(n + 2 < nn)
                def _():
                    d_start(p, n + 2)

                @pl.when(n + 2 == nn)
                def _():
                    arrived((2,))

                @pl.when(n + 2 >= nn)
                def _():
                    d_start(p + 1, n + 2 - nn)

                @pl.when(k == 0)
                def _():
                    mv[part, n] = term

                @pl.when(k > 0)
                def _():
                    mv[part, n] = mv[part, n] + term

                @pl.when(p >= last)
                def _():
                    m_out(part, n).start()
            loop(nn, block)
        loop(passes, one_pass)

        def finish(n):
            for part in SIDES:
                m_out(part, n).wait()
        loop(nn, finish)

    fb = 256 if fe > 512 else 128
    cw = min(512, d_model // 4)
    pl.run_scoped(experts, pltpu.VMEM((RING, 8, hd, width), BF16), pltpu.VMEM((2, q, RING * heads * hd), BF16), pltpu.VMEM((2, q, width), BF16),
                  pltpu.VMEM((2, d_model // cw, RING, half, cw), F32), pltpu.VMEM((RING * half, fe), BF16),
                  pltpu.VMEM((2, 2, fb, d_model), BF16), pltpu.VMEM((2, fe, cw), BF16))

    for side in SIDES:
        w_round(side).wait_send()
        w_forward(side).wait_send()
        for part in SIDES:
            hid_send(part, side).wait_send()
            hid_forward(part, side).wait_send()
        for g in range(pairs):
            ctx_send(g, side).wait_send()
            ctx_forward(g, side).wait_send()
        for c in range(RING):
            a_send(c, side).wait_send()
            a_forward(c, side).wait()
    for k in range(1, RING):
        w_swap(k).wait_send()
        ids_send(k).wait_send()
    for k in SIDES:
        for i in range(len(mats)):
            swap_mat(k, i).wait_send()
    for k in range(RING):
        w_core(k).wait_send()
        a_local(k).wait()


def front_call(x, wq, wk, wv, wo, eg, eu, ed, attn_gain, moe_gain, ids, router):
    tokens, d_model = x.shape
    heads, hd = wq.shape[1], wq.shape[2]
    q = tokens // RING
    local, fe = eg.shape[0], eg.shape[1]
    experts = router.shape[0]
    pairs = heads // 2
    hbm = pl.BlockSpec(memory_space=pl.ANY)
    vmem = pl.BlockSpec(memory_space=pltpu.VMEM)
    dma = pltpu.SemaphoreType.DMA
    sds = jax.ShapeDtypeStruct
    freq = ROPE_BASE ** (np.arange(hd) % (hd // 2) * (-2.0 / hd))
    freq = jnp.asarray(freq.astype(np.float32).reshape(1, hd))
    two, three, four = dma((2,)), dma((3,)), dma((RING,))
    by_pair, by_chunk, square = dma((2, pairs)), dma((2, RING)), dma((2, 2))
    outs = pl.pallas_call(
        front_body,
        out_shape=(sds((tokens, d_model), BF16), sds((RING, 2, q // 2, d_model), F32), sds((RING, tokens, heads * hd), BF16),
                   sds((RING, 2, q // 2, d_model), BF16), sds((RING, ids.shape[0], q), ids.dtype), sds((8, RING, hd, d_model // RING), BF16),
                   sds(eg.shape, BF16), sds(eu.shape, BF16), sds(ed.shape, BF16)),
        in_specs=[hbm] * 8 + [vmem] * 3 + [hbm, vmem],
        out_specs=(hbm,) * 9,
        scratch_shapes=[
            pltpu.VMEM((tokens, d_model), BF16), pltpu.VMEM((pairs, tokens, 2 * hd), BF16), pltpu.VMEM((RING, q, d_model // RING), BF16),
            pltpu.VMEM((2, tokens // 2, experts), F32), pltpu.VMEM((RING, 8, q), ids.dtype),
            pltpu.VMEM((2, tokens, hd), F32),
            dma((RING + 2,)), two, dma((pairs,)), four,
        ] + [by_pair] * RING + [by_chunk] * RING + [square] * RING + [three] * 2 + [two] * RING + [four] * 2 + [three] * 2
          + [dma((2, 3))] * 2 + [by_chunk, two, four, square, two, dma((2, 8))],
        compiler_params=pltpu.CompilerParams(collective_id=0, has_side_effects=True, vmem_limit_bytes=VMEM_LIMIT),
        cost_estimate=pl.CostEstimate(flops=2 * tokens * d_model * (heads * hd * RING + 12 * fe), bytes_accessed=24 * fe * d_model, transcendentals=heads * tokens * tokens),
        name='attn_moe',
    )(x, wq, wk, wv, wo, eg, eu, ed, attn_gain, moe_gain, freq, ids, router)
    return outs[0], outs[1]


def solution(mesh):
    tok_spec = P(('dp', 'ep'))
    col_spec = P(None, 'tp')
    in_specs = (tok_spec,) * 3 + (P(),) + (col_spec,) * 3 + (P('tp'), P(), col_spec, col_spec, P('tp'), P(), P()) + (P('ep'),) * 3

    def layer_local(hidden_in, expert_ids, slot_ids, attn_gain, w_query, w_key, w_value, w_out, ffn_gain, w_gate, w_up, w_down, moe_gain, w_router, exp_gate, exp_up, exp_down):
        num_seqs, seq_len, d_model = hidden_in.shape
        tokens = num_seqs * seq_len
        heads, head_dim = w_out.shape[0], w_out.shape[1]
        x = hidden_in.reshape(tokens, d_model)
        ids = jnp.swapaxes(expert_ids, 1, 2).reshape(expert_ids.shape[2], tokens)
        after_attn, m_part = front_call(
            x, w_query, w_key, w_value, w_out.reshape(heads * head_dim, d_model), jnp.swapaxes(exp_gate, 1, 2), jnp.swapaxes(exp_up, 1, 2), exp_down,
            attn_gain, moe_gain, ids, w_router.T)
        out = ffn_call(after_attn, w_gate.T, w_up.T, w_down, ffn_gain, m_part.reshape(-1, tokens // 4, d_model))
        return out.reshape(hidden_in.shape)

    return jax.shard_map(layer_local, mesh=mesh, in_specs=in_specs, out_specs=tok_spec, check_vma=False)
```

time: 777 us -> 516 us (0.66)
  Pallas kernels: 249 us -> 506 us
  matrix products: 221 us -> 0 us
  waiting for transfers between devices: 109 us -> 0 us
  blocking collectives: 86.3 us -> 0 us
  other arithmetic: 37 us -> 0 us
  local copies, waits for them, and re-layouts: 44.1 us -> 7.89 us
  between operations: 13.9 us -> 0.02 us
    pallas_call x0 -> x1, Pallas kernels: none -> 260 us  [front_call(): pl.pallas_call(front_body, out_shape=(sds((tokens, d_model), BF16), sds((...]
    dot_general x16 -> x0, matrix products: 181 us -> none  [the longest x4 61.4 us: moe_partial(): y_out = jnp.dot(act, exp_down[k], preferred_element_type=F32).astype(BF16)]
    all_gather x4 -> x0, waiting for transfers between devices: 109 us -> none  [the longest x1 69.1 us: layer_local(): lax.all_gather(own, 'ep', axis=0, tiled=False)]
    all_gather x1 -> x0, blocking collectives: 61.3 us -> none  [layer_local(): lax.all_gather(own_ids, 'ep', axis=0, tiled=False)]
    unnamed x2 -> x0, matrix products: 26.2 us -> none
    unnamed x35 -> x1, local copies, waits for them, and re-layouts: 34.1 us -> 7.89 us
    all_to_all x1 -> x0, blocking collectives: 25 us -> none  [layer_local(): cols = lax.all_to_all(rows, 'tp', 1, 0, tiled=True)]
    convert_element_type x4 -> x0, other arithmetic: 21.1 us -> none  [rms_norm(): return (x_f32 * inv_rms * gain.astype(F32)).astype(BF16)]
  transfers between devices with their start and end apart: 7 -> 0, of which waited for: 2 -> 0; matrix products, arithmetic and copies ran while one was open for 24% -> 0% of each run, Pallas kernels for 0% -> 0%
where the time goes in v4:
time: 516 us; the launch traced here: 514 us
  Pallas kernels  506 us (98%)
  local copies, waits for them, and re-layouts  7.89 us (2%)
    pallas_call x1, Pallas kernels, front_call(): pl.pallas_call(front_body, out_shape=(sds((tokens, d_model), BF16), sds((...  260 us
    pallas_call x1, Pallas kernels, ffn_call(): pl.pallas_call(functools.partial(ffn_body, fb), out_shape=jax.ShapeDtypeS...  246 us

profile of v4, /device:TPU:97, one launch (start us, length us, event | category | flops | bytes accessed | tf_op | source)
XLA Modules:
  0.0 513.7 jit_solution(7942525110592348899)
XLA Ops:
  0.0 259.6 %attn_moe.1 = (bf16[1024,4096]{1,0:T(8,128)(2,1)}, f32[4,2,128,4096]{3,2,1,0:T(8,128)}, bf16[4,1024,1024]{2,1,0:T(8,128)(2,1)}, bf16[4,2,128,4096]{3,2,1,0:T(8,1...) custom-call(bf16[1024,4096]{1,0:T(8,128)(2,1)} %bitcast.17, ...), custom_call_target="tpu_custom_call" | custom-call | flops 103616086016 | bytes 67633152 | tf_op jit(solution)/shard_map/attn_moe/pallas_call | solution.py:810
  259.6 246.3 %ffn_ring.1 = bf16[1024,4096]{1,0:T(8,128)(2,1)} custom-call(bf16[1024,4096]{1,0:T(8,128)(2,1)} %get-tuple-element.7.a_ref, bf16[2752,4096]{1,0:T(8,128)(2,1)} %bitcast.13, bf16[2752,4096]{1,0:T(8,128)(2,1)} %bitcast.14, bf16[2752,4096]{1,0:T(8,128)(2,1)} %wd.1, bf16[4096]{0:T(1024)(128)(2,1)} %gain.1, f32[4,256,4096]{2,1,0:T(8,128)} %bitcast.21), custom_call_target="tpu_custom_call" | custom-call | flops 69256347648 | bytes 152043520 | tf_op jit(solution)/shard_map/ffn_ring/pallas_call | solution.py:318
  505.8 7.9 %copy.19 = bf16[1,1024,4096]{2,1,0:T(8,128)(2,1)} copy(bf16[1,1024,4096]{2,1,0:T(8,128)(2,1)} %bitcast.12) | data formatting | bytes 16777216

commit v5 on v4

--- a/solution.py
+++ b/solution.py
@@ -61,14 +61,14 @@
 
 
 def ffn_body(fb, a_ref, wg, wu, wd, gain, m_ref, out_ref,
-             a_buf, n2, h, wbuf, dbuf, p1, p2, yrecv, xrecv, mbuf,
+             a_own, n2, h, wbuf, dbuf, p1, yrecv, xrecv, mbuf,
              asem, wsem, dsem, msem, osem, ys, yr, xs, xr, gs, gr, fs, fr):
     t = lax.axis_index('tp')
     e = lax.axis_index('ep')
     big = odd(e)
     xc = e // 2
-    q = a_buf.shape[1]
-    d_model = a_buf.shape[2]
+    q = a_own.shape[0]
+    d_model = a_own.shape[1]
     f_loc = wg.shape[0]
     cw = d_model // 8
     hw = cw // 2
@@ -87,7 +87,8 @@
         return window(chunk(c), q)
 
     def a_load(c, slot):
-        return pltpu.make_async_copy(a_ref.at[rows(c)], a_buf.at[slot], asem.at[slot])
+        return pltpu.make_async_copy(a_ref.at[rows(c)], n2.at[pl.ds(slot * q, q)], asem.at[slot])
+    load_own = pltpu.make_async_copy(a_ref.at[rows(t)], a_own, asem.at[2])
 
     def w_load(i, slot, size):
         sl = pl.ds(pl.multiple_of(i * fb, fb), size)
@@ -95,7 +96,7 @@
                 pltpu.make_async_copy(wu.at[sl], wbuf.at[slot, 1, pl.ds(0, size)], wsem.at[slot, 1]))
 
     def w_start(i):
-        slot = odd(i)
+        slot = lax.rem(i, wbuf.shape[0])
 
         @pl.when(i < nf)
         def _():
@@ -111,8 +112,8 @@
         return odd(j) * 4 + j // 2
 
     def d_load(jj):
-        slot = odd(jj)
-        start = pl.multiple_of(col_of(jj // 2) * cw + slot * hw, hw)
+        slot = lax.rem(jj, RING)
+        start = pl.multiple_of(col_of(jj // 2) * cw + odd(jj) * hw, hw)
         return pltpu.make_async_copy(wd.at[:, pl.ds(start, hw)], dbuf.at[slot], dsem.at[slot])
 
     def m_load(k):
@@ -154,7 +155,8 @@
 
     def gate_up(serve):
         def block(i, size):
-            slot = odd(i)
+            slot = lax.rem(i, wbuf.shape[0])
+            w_start(i + 2)
             for c in w_load(i, slot, size):
                 c.wait()
             g = lax.dot_general(n2[...], wbuf[slot, 0, pl.ds(0, size)], NT, preferred_element_type=F32)
@@ -163,22 +165,29 @@
 
         def one(i):
             block(i, fb)
-            w_start(i + 2)
             serve(i)
         loop(nf, one)
         block(nf, tail)
 
-    def down(use):
+    def down(ready, use):
         def one(jj):
             sub = odd(jj)
+
+            @pl.when(jj + RING - 1 < 16)
+            def _():
+                d_load(jj + RING - 1).start()
+
+            @pl.when(sub == 0)
+            def _():
+                ready(jj // 2)
             d_load(jj).wait()
-            r = jnp.dot(h[...], dbuf[sub], preferred_element_type=F32)
-
-            @pl.when(jj + 2 < 16)
-            def _():
-                d_load(jj + 2).start()
-            use(jj // 2, sub, window(sub, hw), r)
+            r = jnp.dot(h[...], dbuf[lax.rem(jj, RING)], preferred_element_type=F32)
+            use(jj // 2, sub, pl.ds(pl.multiple_of(sub * hw, hw), hw), r)
         loop(16, one)
+
+    def d_first():
+        for k in range(RING - 1):
+            d_load(jnp.int32(k)).start()
 
     a_load(t - 1, 0).start()
     a_load(t + 1, 1).start()
@@ -190,16 +199,16 @@
         xsend(m_ref.at[chunk(xc - 1), :, cols(i)], 0, 0, i)
         xsend(m_ref.at[chunk(xc + 1), :, cols(4 + i)], 1, 0, i)
     loop(4, x_first)
-    d_load(0).start()
-    d_load(1).start()
+    d_first()
     m_load(0).start()
+    load_own.start()
 
     for slot in SIDES:
         a_load(t, slot).wait()
-        norm_rows(a_buf.at[slot], n2.at[pl.ds(slot * q, q)], gain, q, 16)
+        norm_rows(n2.at[pl.ds(slot * q, q)], n2.at[pl.ds(slot * q, q)], gain, q, 16)
+    gate_up(lambda i: None)
     a_load(t + 2, 0).start()
     a_load(t, 1).start()
-    gate_up(lambda i: None)
     w_start(0)
     w_start(1)
 
@@ -210,13 +219,12 @@
         @pl.when(sub == 1)
         def _():
             ysend(p1.at[col_of(j), window(side, q)], side, 0, i)
-    down(use1)
-    d_load(0).start()
-    d_load(1).start()
+    down(lambda j: None, use1)
+    d_first()
 
     for slot in SIDES:
         a_load(t, slot).wait()
-        norm_rows(a_buf.at[slot], n2.at[pl.ds(slot * q, q)], gain, q, 16)
+        norm_rows(n2.at[pl.ds(slot * q, q)], n2.at[pl.ds(slot * q, q)], gain, q, 16)
 
     def serve2(i):
         @pl.when(i < 8)
@@ -226,19 +234,22 @@
     for k in range(min(nf, 8), 8):
         xserve(k)
 
+    def sent_rows(j):
+        return pl.ds(pl.multiple_of(odd(j) * q, q), q)
+
+    def ready2(j):
+        arrived(yrecv, ys, yr, odd(j), 0, j // 2, yright)
+        sent(yrecv, ys, yr, odd(j), 0, j // 2, yright)
+
     def use2(j, sub, part, r):
         side, i = odd(j), j // 2
-        p2[col_of(j), :, part] = r[q:]
-
-        @pl.when(sub == 0)
-        def _():
-            arrived(yrecv, ys, yr, side, 0, i, yright)
+        p1[col_of(j), sent_rows(j), part] = r[q:]
         yrecv[side, 0, i, :, part] = yrecv[side, 0, i, :, part] + r[:q]
 
         @pl.when(sub == 1)
         def _():
             ysend(yrecv.at[side, 0, i], side, 1, i)
-    down(use2)
+    down(ready2, use2)
 
     def third(j):
         side, i = odd(j), j // 2
@@ -254,6 +265,8 @@
     def gather(cb, side, dev):
         return rcopy(n2.at[pl.ds(0, q), cols(cb)], out_ref.at[rows(t), cols(cb)], gs.at[side, cb], gr.at[side, cb], dev)
 
+    load_own.wait()
+
     def last(j):
         side, i = odd(j), j // 2
         cb = col_of(j)
@@ -265,7 +278,7 @@
         m_load(k).wait()
         arrived(xrecv, xs, xr, side, 2, i, xright)
         arrived(yrecv, ys, yr, side, 2, i, yright)
-        b_val = a_buf[1, :, cols(cb)].astype(F32) + (yrecv[side, 2, i] + p2[cb])
+        b_val = a_own[:, cols(cb)].astype(F32) + (yrecv[side, 2, i] + p1[cb, sent_rows(j)])
         n2[pl.ds(0, q), cols(cb)] = (b_val + (xrecv[side, 2, i] + mbuf[odd(k)])).astype(BF16)
         out_local(cb).start()
         gather(cb, 0, yright).start()
@@ -300,7 +313,10 @@
 
     def drain(k):
         step, j = k // 8, lax.rem(k, 8)
-        sent(yrecv, ys, yr, odd(j), step, j // 2, yright)
+
+        @pl.when(step > 0)
+        def _():
+            sent(yrecv, ys, yr, odd(j), step, j // 2, yright)
         sent(xrecv, xs, xr, odd(j), step, j // 2, yright)
     loop(24, drain)
 
@@ -321,17 +337,16 @@
         in_specs=[hbm, hbm, hbm, hbm, vmem, hbm],
         out_specs=hbm,
         scratch_shapes=[
-            pltpu.VMEM((2, q, d_model), BF16),
+            pltpu.VMEM((q, d_model), BF16),
             pltpu.VMEM((2 * q, d_model), BF16),
             pltpu.VMEM((2 * q, f_loc), BF16),
-            pltpu.VMEM((2, 2, fb, d_model), BF16),
-            pltpu.VMEM((2, f_loc, cw // 2), BF16),
+            pltpu.VMEM((3, 2, fb, d_model), BF16),
+            pltpu.VMEM((RING, f_loc, cw // 2), BF16),
             pltpu.VMEM((8, 2 * q, cw), F32),
-            pltpu.VMEM((8, q, cw), F32),
             pltpu.VMEM((2, 3, RING, q, cw), F32),
             pltpu.VMEM((2, 3, RING, q, cw), F32),
             pltpu.VMEM((2, q, cw), F32),
-            dma((2,)), dma((2, 2)), dma((2,)), dma((2,)), dma((8,)),
+            dma((3,)), dma((3, 2)), dma((RING,)), dma((2,)), dma((8,)),
         ] + [dma((2, 3, RING))] * RING + [dma((2, 8))] * RING,
         compiler_params=pltpu.CompilerParams(collective_id=2, has_side_effects=True, vmem_limit_bytes=VMEM_LIMIT),
         cost_estimate=pl.CostEstimate(flops=flops, bytes_accessed=4 * tokens * d_model + 12 * f_loc * d_model, transcendentals=tokens * f_loc),
@@ -442,9 +457,12 @@
     def attention(raw, wide, wb, qb, kb, vb):
         proj = (wq, wk, wv)
 
+        deep = raw.shape[0]
+
         def raw_load(m, k):
-            return pltpu.make_async_copy(proj[m].at[window(k, kblk)], raw.at[odd(k)], rawsem.at[odd(k)])
-        for k in SIDES:
+            slot = lax.rem(k, deep)
+            return pltpu.make_async_copy(proj[m].at[window(k, kblk)], raw.at[slot], rawsem.at[slot])
+        for k in range(deep):
             raw_load(0, k).start()
         entry_barrier((y_dev(1), y_dev(-1), y_dev(2), x_dev(1), x_dev(-1), x_dev(2), partner))
         w_own.start()
@@ -473,17 +491,19 @@
         for m in range(len(proj)):
             def one(k, m=m):
                 raw_load(m, k).wait()
-                wide[...] = raw[odd(k)].astype(F32).reshape(kblk * heads, hd)
-
-                @pl.when(k + 2 < nk)
+                wide[...] = raw[lax.rem(k, deep)].astype(F32).reshape(kblk * heads, hd)
+
+                @pl.when(k + deep < nk)
                 def _():
-                    raw_load(m, k + 2).start()
+                    raw_load(m, k + deep).start()
+
+                if m + 1 < len(proj):
+                    @pl.when(k + deep >= nk)
+                    def _():
+                        raw_load(m + 1, k + deep - nk).start()
                 for h in range(heads):
                     wb[m, window(k, kblk), h * hd:(h + 1) * hd] = wide[pl.ds(h, kblk, stride=heads), :].astype(BF16)
             loop(nk, one)
-            if m + 1 < len(proj):
-                for k in SIDES:
-                    raw_load(m + 1, k).start()
 
         w_own.wait()
         for k in range(1, RING):
@@ -542,7 +562,7 @@
                     hid_send(1, side).start()
         loop(pairs, heads_of)
 
-    pl.run_scoped(attention, pltpu.VMEM((2, kblk, heads, hd), BF16), pltpu.VMEM((kblk * heads, hd), F32),
+    pl.run_scoped(attention, pltpu.VMEM((8, kblk, heads, hd), BF16), pltpu.VMEM((kblk * heads, hd), F32),
                   pltpu.VMEM((len(SIDES) + 1, d_model, heads * hd), BF16), *[pltpu.VMEM((tokens, pair), BF16)] * (len(SIDES) + 1))
 
     def experts(wcv, cbuf, xbuf, mv, act, wbuf, dbuf):
@@ -569,7 +589,7 @@
                     for i, ref in enumerate((eg, eu) if own else (og, ou))]
 
         def d_load(k, n, own):
-            return pltpu.make_async_copy((ed if own else od).at[k if own else k - local, :, window(n, cw)], dbuf.at[odd(n)], dsem.at[odd(n)])
+            return pltpu.make_async_copy((ed if own else od).at[k if own else k - local, :, window(n, cw)], dbuf.at[lax.rem(n, RING)], dsem.at[lax.rem(n, RING)])
 
         def either(p, start):
             k = expert_of(p)
@@ -584,7 +604,7 @@
 
         def w_start(p, b):
             def go(k, own):
-                for c in w_load(k, b, odd(p * nb + b), own):
+                for c in w_load(k, b, b, own):
                     c.start()
             either(p, go)
 
@@ -658,9 +678,10 @@
         def m_out(part, n):
             return pltpu.make_async_copy(mv.at[part, n], m_part.at[:, part, :, window(n, cw)], msem.at[part, n])
 
-        for b in SIDES:
+        for b in range(nb - 1):
             w_start(jnp.int32(0), b)
-            d_start(jnp.int32(0), jnp.int32(b))
+        for n in range(RING - 1):
+            d_start(jnp.int32(0), jnp.int32(n))
         ids_own.wait()
         for k in range(1, RING):
             ids_send(k).wait_recv()
@@ -716,41 +737,34 @@
                         for i in which_mats:
                             swap_mat(late, i).wait_recv()
             for b, size in enumerate(sizes):
-                slot = odd(p * nb + b)
-                for c in w_load(0, b, slot, True):
-                    c.wait()
-                g = lax.dot_general(u[...], wbuf[slot, 0, 0:size], NT, preferred_element_type=F32)
-                v = lax.dot_general(u[...], wbuf[slot, 1, 0:size], NT, preferred_element_type=F32)
-                act[:, b * fb:b * fb + size] = (jax.nn.silu(g) * v).astype(BF16)
-                nxt = b + 2
+                nxt = b + nb - 1
                 if nxt == nb:
                     arrived(SIDES)
                 w_start(p + nxt // nb, nxt % nb)
+                for c in w_load(0, b, b, True):
+                    c.wait()
+                g = lax.dot_general(u[...], wbuf[b, 0, 0:size], NT, preferred_element_type=F32)
+                v = lax.dot_general(u[...], wbuf[b, 1, 0:size], NT, preferred_element_type=F32)
+                act[:, b * fb:b * fb + size] = (jax.nn.silu(g) * v).astype(BF16)
 
             def block(n):
-                d_load(0, n, True).wait()
-                y = jnp.dot(act[...], dbuf[odd(n)], preferred_element_type=F32).astype(BF16)
-                term = jnp.where(weight > 0.0, weight * y.astype(F32), 0.0).reshape(mv.shape[2:])
-
-                @pl.when(n + 2 < nn)
+                ahead = n + RING - 1
+
+                @pl.when(ahead < nn)
                 def _():
-                    d_start(p, n + 2)
-
-                @pl.when(n + 2 == nn)
+                    d_start(p, ahead)
+
+                @pl.when(ahead == nn)
                 def _():
                     arrived((2,))
 
-                @pl.when(n + 2 >= nn)
+                @pl.when(ahead >= nn)
                 def _():
-                    d_start(p + 1, n + 2 - nn)
-
-                @pl.when(k == 0)
-                def _():
-                    mv[part, n] = term
-
-                @pl.when(k > 0)
-                def _():
-                    mv[part, n] = mv[part, n] + term
+                    d_start(p + 1, ahead - nn)
+                d_load(0, n, True).wait()
+                y = jnp.dot(act[...], dbuf[lax.rem(n, RING)], preferred_element_type=F32).astype(BF16)
+                term = jnp.where(weight > 0.0, weight * y.astype(F32), 0.0).reshape(mv.shape[2:])
+                mv[part, n] = jnp.where(k == 0, term, mv[part, n] + term)
 
                 @pl.when(p >= last)
                 def _():
@@ -767,7 +781,7 @@
     cw = min(512, d_model // 4)
     pl.run_scoped(experts, pltpu.VMEM((RING, 8, hd, width), BF16), pltpu.VMEM((2, q, RING * heads * hd), BF16), pltpu.VMEM((2, q, width), BF16),
                   pltpu.VMEM((2, d_model // cw, RING, half, cw), F32), pltpu.VMEM((RING * half, fe), BF16),
-                  pltpu.VMEM((2, 2, fb, d_model), BF16), pltpu.VMEM((2, fe, cw), BF16))
+                  pltpu.VMEM((fe // fb + 1, 2, fb, d_model), BF16), pltpu.VMEM((RING, fe, cw), BF16))
 
     for side in SIDES:
         w_round(side).wait_send()
@@ -818,9 +832,9 @@
             pltpu.VMEM((tokens, d_model), BF16), pltpu.VMEM((pairs, tokens, 2 * hd), BF16), pltpu.VMEM((RING, q, d_model // RING), BF16),
             pltpu.VMEM((2, tokens // 2, experts), F32), pltpu.VMEM((RING, 8, q), ids.dtype),
             pltpu.VMEM((2, tokens, hd), F32),
-            dma((RING + 2,)), two, dma((pairs,)), four,
+            dma((RING + 2,)), dma((8,)), dma((pairs,)), four,
         ] + [by_pair] * RING + [by_chunk] * RING + [square] * RING + [three] * 2 + [two] * RING + [four] * 2 + [three] * 2
-          + [dma((2, 3))] * 2 + [by_chunk, two, four, square, two, dma((2, 8))],
+          + [dma((2, 3))] * 2 + [by_chunk, two, four, dma((fe // 256 + 1, 2)), four, dma((2, 8))],
         compiler_params=pltpu.CompilerParams(collective_id=0, has_side_effects=True, vmem_limit_bytes=VMEM_LIMIT),
         cost_estimate=pl.CostEstimate(flops=2 * tokens * d_model * (heads * hd * RING + 12 * fe), bytes_accessed=24 * fe * d_model, transcendentals=heads * tokens * tokens),
         name='attn_moe',

time: 516 us -> 481 us (0.932)
  Pallas kernels: 506 us -> 472 us
    pallas_call x1, Pallas kernels: 260 us -> 227 us  [front_call(): pl.pallas_call(front_body, out_shape=(sds((tokens, d_model), BF16), sds((...]
where the time goes in v5:
time: 481 us; the launch traced here: 480 us
  Pallas kernels  472 us (98%)
  local copies, waits for them, and re-layouts  7.89 us (2%)
    pallas_call x1, Pallas kernels, ffn_call(): pl.pallas_call(functools.partial(ffn_body, fb), out_shape=jax.ShapeDtypeS...  246 us
    pallas_call x1, Pallas kernels, front_call(): pl.pallas_call(front_body, out_shape=(sds((tokens, d_model), BF16), sds((...  227 us

profile of v5, /device:TPU:97, one launch (start us, length us, event | category | flops | bytes accessed | tf_op | source)
XLA Modules:
  0.0 480.3 jit_solution(9475707601692960434)
XLA Ops:
  0.0 226.9 %attn_moe.1 = (bf16[1024,4096]{1,0:T(8,128)(2,1)}, f32[4,2,128,4096]{3,2,1,0:T(8,128)}, bf16[4,1024,1024]{2,1,0:T(8,128)(2,1)}, bf16[4,2,128,4096]{3,2,1,0:T(8,1...) custom-call(bf16[1024,4096]{1,0:T(8,128)(2,1)} %bitcast.17, ...), custom_call_target="tpu_custom_call" | custom-call | flops 103616086016 | bytes 67633152 | tf_op jit(solution)/shard_map/attn_moe/pallas_call | solution.py:824
  226.9 245.5 %ffn_ring.1 = bf16[1024,4096]{1,0:T(8,128)(2,1)} custom-call(bf16[1024,4096]{1,0:T(8,128)(2,1)} %get-tuple-element.7.a_ref, bf16[2752,4096]{1,0:T(8,128)(2,1)} %bitcast.13, bf16[2752,4096]{1,0:T(8,128)(2,1)} %bitcast.14, bf16[2752,4096]{1,0:T(8,128)(2,1)} %wd.1, bf16[4096]{0:T(1024)(128)(2,1)} %gain.1, f32[4,256,4096]{2,1,0:T(8,128)} %bitcast.21), custom_call_target="tpu_custom_call" | custom-call | flops 69256347648 | bytes 152043520 | tf_op jit(solution)/shard_map/ffn_ring/pallas_call | solution.py:334
  472.4 7.9 %copy.19 = bf16[1,1024,4096]{2,1,0:T(8,128)(2,1)} copy(bf16[1,1024,4096]{2,1,0:T(8,128)(2,1)} %bitcast.12) | data formatting | bytes 16777216

commit v6 on v5

--- a/solution.py
+++ b/solution.py
@@ -111,10 +111,9 @@
     def col_of(j):
         return odd(j) * 4 + j // 2
 
-    def d_load(jj):
-        slot = lax.rem(jj, RING)
-        start = pl.multiple_of(col_of(jj // 2) * cw + odd(jj) * hw, hw)
-        return pltpu.make_async_copy(wd.at[:, pl.ds(start, hw)], dbuf.at[slot], dsem.at[slot])
+    def d_load(j):
+        start = col_of(j) * cw
+        return [pltpu.make_async_copy(wd.at[:, pl.ds(pl.multiple_of(start + sub * hw, hw), hw)], dbuf.at[odd(j), sub], dsem.at[odd(j), sub]) for sub in SIDES]
 
     def m_load(k):
         s, j = k // 8 + 1, lax.rem(k, 8)
@@ -169,25 +168,23 @@
         loop(nf, one)
         block(nf, tail)
 
-    def down(ready, use):
-        def one(jj):
-            sub = odd(jj)
-
-            @pl.when(jj + RING - 1 < 16)
-            def _():
-                d_load(jj + RING - 1).start()
-
-            @pl.when(sub == 0)
-            def _():
-                ready(jj // 2)
-            d_load(jj).wait()
-            r = jnp.dot(h[...], dbuf[lax.rem(jj, RING)], preferred_element_type=F32)
-            use(jj // 2, sub, pl.ds(pl.multiple_of(sub * hw, hw), hw), r)
-        loop(16, one)
-
-    def d_first():
-        for k in range(RING - 1):
-            d_load(jnp.int32(k)).start()
+    def d_start(j):
+        for c in d_load(j):
+            c.start()
+
+    def down(ready, use, done):
+        def one(j):
+            @pl.when(j + 1 < 8)
+            def _():
+                d_start(j + 1)
+            ready(j)
+            for c in d_load(j):
+                c.wait()
+            for sub in SIDES:
+                r = jnp.dot(h[...], dbuf[odd(j), sub], preferred_element_type=F32)
+                use(j, slice(sub * hw, (sub + 1) * hw), r)
+            done(j)
+        loop(8, one)
 
     a_load(t - 1, 0).start()
     a_load(t + 1, 1).start()
@@ -199,7 +196,7 @@
         xsend(m_ref.at[chunk(xc - 1), :, cols(i)], 0, 0, i)
         xsend(m_ref.at[chunk(xc + 1), :, cols(4 + i)], 1, 0, i)
     loop(4, x_first)
-    d_first()
+    d_start(jnp.int32(0))
     m_load(0).start()
     load_own.start()
 
@@ -212,15 +209,14 @@
     w_start(0)
     w_start(1)
 
-    def use1(j, sub, part, r):
+    def use1(j, part, r):
         p1[col_of(j), :, part] = r
-        side, i = odd(j), j // 2
-
-        @pl.when(sub == 1)
-        def _():
-            ysend(p1.at[col_of(j), window(side, q)], side, 0, i)
-    down(lambda j: None, use1)
-    d_first()
+
+    def done1(j):
+        side = odd(j)
+        ysend(p1.at[col_of(j), pl.ds(pl.multiple_of(side * q, q), q)], side, 0, j // 2)
+    down(lambda j: None, use1, done1)
+    d_start(jnp.int32(0))
 
     for slot in SIDES:
         a_load(t, slot).wait()
@@ -241,15 +237,13 @@
         arrived(yrecv, ys, yr, odd(j), 0, j // 2, yright)
         sent(yrecv, ys, yr, odd(j), 0, j // 2, yright)
 
-    def use2(j, sub, part, r):
-        side, i = odd(j), j // 2
+    def use2(j, part, r):
         p1[col_of(j), sent_rows(j), part] = r[q:]
-        yrecv[side, 0, i, :, part] = yrecv[side, 0, i, :, part] + r[:q]
-
-        @pl.when(sub == 1)
-        def _():
-            ysend(yrecv.at[side, 0, i], side, 1, i)
-    down(ready2, use2)
+        yrecv[odd(j), 0, j // 2, :, part] = yrecv[odd(j), 0, j // 2, :, part] + r[:q]
+
+    def done2(j):
+        ysend(yrecv.at[odd(j), 0, j // 2], odd(j), 1, j // 2)
+    down(ready2, use2, done2)
 
     def third(j):
         side, i = odd(j), j // 2
@@ -341,12 +335,12 @@
             pltpu.VMEM((2 * q, d_model), BF16),
             pltpu.VMEM((2 * q, f_loc), BF16),
             pltpu.VMEM((3, 2, fb, d_model), BF16),
-            pltpu.VMEM((RING, f_loc, cw // 2), BF16),
+            pltpu.VMEM((2, 2, f_loc, cw // 2), BF16),
             pltpu.VMEM((8, 2 * q, cw), F32),
             pltpu.VMEM((2, 3, RING, q, cw), F32),
             pltpu.VMEM((2, 3, RING, q, cw), F32),
             pltpu.VMEM((2, q, cw), F32),
-            dma((3,)), dma((3, 2)), dma((RING,)), dma((2,)), dma((8,)),
+            dma((3,)), dma((3, 2)), dma((2, 2)), dma((2,)), dma((8,)),
         ] + [dma((2, 3, RING))] * RING + [dma((2, 8))] * RING,
         compiler_params=pltpu.CompilerParams(collective_id=2, has_side_effects=True, vmem_limit_bytes=VMEM_LIMIT),
         cost_estimate=pl.CostEstimate(flops=flops, bytes_accessed=4 * tokens * d_model + 12 * f_loc * d_model, transcendentals=tokens * f_loc),
@@ -356,7 +350,7 @@
 
 def front_body(x_ref, wq, wk, wv, wo, eg, eu, ed, attn_gain, moe_gain, freq, ids, router,
                a_full, m_part, ctx_all, hid_all, ids_all, w_cols, og, ou, od,
-               xn, ctxb, abuf, gate, idf, rope,
+               xn, ctxb, abuf, gate, idf,
                lsem, rawsem, cls, als, cs, cr, cfs, cfr, as_, ar, afs, afr, hs, hr, hfs, hfr, ws, wr, wxs, wxr, wfs, wfr,
                wds, wdr, ins, inr, es, er, csem, xsem, usem, wsem, dsem, msem):
     t = lax.axis_index('tp')
@@ -368,7 +362,7 @@
     q = tokens // RING
     half = q // 2
     width = d_model // RING
-    kblk = min(256, d_model)
+    kblk = min(512, d_model // RING)
     nk = d_model // kblk
     pair = 2 * hd
     pairs = heads // 2
@@ -454,7 +448,7 @@
     w_own = pltpu.make_async_copy(wo.at[window(e, hd), window(t, width)], w_cols.at[e, t], lsem.at[RING])
     ids_own = pltpu.make_async_copy(ids.at[:, window(t, q)], ids_all.at[xc], lsem.at[RING + 1])
 
-    def attention(raw, wide, wb, qb, kb, vb):
+    def attention(rope, raw, wide, wb, qb, kb, vb):
         proj = (wq, wk, wv)
 
         deep = raw.shape[0]
@@ -562,14 +556,15 @@
                     hid_send(1, side).start()
         loop(pairs, heads_of)
 
-    pl.run_scoped(attention, pltpu.VMEM((8, kblk, heads, hd), BF16), pltpu.VMEM((kblk * heads, hd), F32),
+    pl.run_scoped(attention, pltpu.VMEM((2, tokens, hd), F32), pltpu.VMEM((RING, kblk, heads, hd), BF16), pltpu.VMEM((kblk * heads, hd), F32),
                   pltpu.VMEM((len(SIDES) + 1, d_model, heads * hd), BF16), *[pltpu.VMEM((tokens, pair), BF16)] * (len(SIDES) + 1))
 
-    def experts(wcv, cbuf, xbuf, mv, act, wbuf, dbuf):
-        fb = wbuf.shape[2]
+    fb = 256 if fe > 512 else 128
+    cw = min(512, d_model // 4)
+
+    def experts(wcv, cbuf, mv, act, wbuf, dbuf):
         sizes = [fb] * (fe // fb) + [fe % fb]
-        nb = len(sizes)
-        cw = dbuf.shape[2]
+        cw = mv.shape[-1]
         nn = d_model // cw
         passes = 4 * local
         last = passes - 2
@@ -582,34 +577,25 @@
             late = p // last
             return (1 - late) * (p // 3) + late * (p - last)
 
-        def w_load(k, b, slot, own):
+        def w_load(k, own):
             k = k if own else k - local
-            rows = pl.ds(b * fb, sizes[b])
-            return [pltpu.make_async_copy(ref.at[k, rows], wbuf.at[slot, i, pl.ds(0, sizes[b])], wsem.at[slot, i])
-                    for i, ref in enumerate((eg, eu) if own else (og, ou))]
-
-        def d_load(k, n, own):
-            return pltpu.make_async_copy((ed if own else od).at[k if own else k - local, :, window(n, cw)], dbuf.at[lax.rem(n, RING)], dsem.at[lax.rem(n, RING)])
-
-        def either(p, start):
+            return [pltpu.make_async_copy(ref.at[k], wbuf.at[i], wsem.at[i]) for i, ref in enumerate((eg, eu) if own else (og, ou))]
+
+        def d_load(k, own):
+            return [pltpu.make_async_copy((ed if own else od).at[k if own else k - local], dbuf, dsem.at[0])]
+
+        def start(p, load):
             k = expert_of(p)
 
             @pl.when(jnp.logical_and(p < passes, k < local))
             def _():
-                start(k, True)
+                for c in load(k, True):
+                    c.start()
 
             @pl.when(jnp.logical_and(p < passes, k >= local))
             def _():
-                start(k, False)
-
-        def w_start(p, b):
-            def go(k, own):
-                for c in w_load(k, b, b, own):
+                for c in load(k, False):
                     c.start()
-            either(p, go)
-
-        def d_start(p, n):
-            either(p, lambda k, own: d_load(k, n, own).start())
 
         def u_rows(part, k):
             return xn.at[pl.ds(pl.multiple_of((part * RING + k) * half, half), half)]
@@ -643,7 +629,7 @@
             return [pltpu.make_async_copy(ctx_all.at[k, window(c, q)], cbuf.at[odd(c), :, pl.ds(k * heads * hd, heads * hd)], csem.at[odd(c), k]) for k in range(RING)]
 
         def x_load(c):
-            return pltpu.make_async_copy(x_ref.at[window(c, q), window(t, width)], xbuf.at[odd(c)], xsem.at[odd(c)])
+            return pltpu.make_async_copy(x_ref.at[window(c, q), window(t, width)], abuf.at[c], xsem.at[odd(c)])
 
         load_w = [pltpu.make_async_copy(w_cols.at[:, k], wcv.at[k], lsem.at[k]) for k in range(RING)]
 
@@ -669,7 +655,7 @@
                     d.wait()
                 x_load(c).wait()
                 o = jnp.dot(cbuf[odd(c)], wcv[...].reshape(RING * heads * hd, width), preferred_element_type=F32)
-                abuf[c] = (xbuf[odd(c)].astype(F32) + o).astype(BF16)
+                abuf[c] = (abuf[c].astype(F32) + o).astype(BF16)
                 a_local(c).start()
                 for side in SIDES:
                     a_send(c, side).start()
@@ -678,10 +664,7 @@
         def m_out(part, n):
             return pltpu.make_async_copy(mv.at[part, n], m_part.at[:, part, :, window(n, cw)], msem.at[part, n])
 
-        for b in range(nb - 1):
-            w_start(jnp.int32(0), b)
-        for n in range(RING - 1):
-            d_start(jnp.int32(0), jnp.int32(n))
+        start(jnp.int32(0), w_load)
         ids_own.wait()
         for k in range(1, RING):
             ids_send(k).wait_recv()
@@ -730,46 +713,33 @@
             lane = lax.broadcasted_iota(jnp.int32, gate.shape[1:], 1)
             weight = jnp.sum(jnp.where(lane == which, gate[part], 0.0), axis=1, keepdims=True)
 
-            def arrived(which_mats):
-                for late, when in enumerate((1, last - 1)):
-                    @pl.when(p == when)
+            def if_new(ahead, which_mats):
+                for late, when in enumerate((3, last + 1)):
+                    @pl.when(ahead == when)
                     def _():
                         for i in which_mats:
                             swap_mat(late, i).wait_recv()
+            if_new(p + 1, (2,))
+            start(p, d_load)
+            for c in w_load(0, True):
+                c.wait()
             for b, size in enumerate(sizes):
-                nxt = b + nb - 1
-                if nxt == nb:
-                    arrived(SIDES)
-                w_start(p + nxt // nb, nxt % nb)
-                for c in w_load(0, b, b, True):
-                    c.wait()
-                g = lax.dot_general(u[...], wbuf[b, 0, 0:size], NT, preferred_element_type=F32)
-                v = lax.dot_general(u[...], wbuf[b, 1, 0:size], NT, preferred_element_type=F32)
-                act[:, b * fb:b * fb + size] = (jax.nn.silu(g) * v).astype(BF16)
-
-            def block(n):
-                ahead = n + RING - 1
-
-                @pl.when(ahead < nn)
-                def _():
-                    d_start(p, ahead)
-
-                @pl.when(ahead == nn)
-                def _():
-                    arrived((2,))
-
-                @pl.when(ahead >= nn)
-                def _():
-                    d_start(p + 1, ahead - nn)
-                d_load(0, n, True).wait()
-                y = jnp.dot(act[...], dbuf[lax.rem(n, RING)], preferred_element_type=F32).astype(BF16)
+                cols = slice(b * fb, b * fb + size)
+                g = lax.dot_general(u[...], wbuf[0, cols], NT, preferred_element_type=F32)
+                v = lax.dot_general(u[...], wbuf[1, cols], NT, preferred_element_type=F32)
+                act[:, cols] = (jax.nn.silu(g) * v).astype(BF16)
+            if_new(p + 2, SIDES)
+            start(p + 1, w_load)
+            for c in d_load(0, True):
+                c.wait()
+            for n in range(nn):
+                y = jnp.dot(act[...], dbuf[:, n * cw:(n + 1) * cw], preferred_element_type=F32).astype(BF16)
                 term = jnp.where(weight > 0.0, weight * y.astype(F32), 0.0).reshape(mv.shape[2:])
                 mv[part, n] = jnp.where(k == 0, term, mv[part, n] + term)
 
-                @pl.when(p >= last)
-                def _():
-                    m_out(part, n).start()
-            loop(nn, block)
+            @pl.when(p >= last)
+            def _():
+                loop(nn, lambda n: m_out(part, n).start())
         loop(passes, one_pass)
 
         def finish(n):
@@ -777,11 +747,9 @@
                 m_out(part, n).wait()
         loop(nn, finish)
 
-    fb = 256 if fe > 512 else 128
-    cw = min(512, d_model // 4)
-    pl.run_scoped(experts, pltpu.VMEM((RING, 8, hd, width), BF16), pltpu.VMEM((2, q, RING * heads * hd), BF16), pltpu.VMEM((2, q, width), BF16),
+    pl.run_scoped(experts, pltpu.VMEM((RING, 8, hd, width), BF16), pltpu.VMEM((2, q, RING * heads * hd), BF16),
                   pltpu.VMEM((2, d_model // cw, RING, half, cw), F32), pltpu.VMEM((RING * half, fe), BF16),
-                  pltpu.VMEM((fe // fb + 1, 2, fb, d_model), BF16), pltpu.VMEM((RING, fe, cw), BF16))
+                  pltpu.VMEM((2, fe, d_model), BF16), pltpu.VMEM((fe, d_model), BF16))
 
     for side in SIDES:
         w_round(side).wait_send()
@@ -831,10 +799,9 @@
         scratch_shapes=[
             pltpu.VMEM((tokens, d_model), BF16), pltpu.VMEM((pairs, tokens, 2 * hd), BF16), pltpu.VMEM((RING, q, d_model // RING), BF16),
             pltpu.VMEM((2, tokens // 2, experts), F32), pltpu.VMEM((RING, 8, q), ids.dtype),
-            pltpu.VMEM((2, tokens, hd), F32),
-            dma((RING + 2,)), dma((8,)), dma((pairs,)), four,
+            dma((RING + 2,)), four, dma((pairs,)), four,
         ] + [by_pair] * RING + [by_chunk] * RING + [square] * RING + [three] * 2 + [two] * RING + [four] * 2 + [three] * 2
-          + [dma((2, 3))] * 2 + [by_chunk, two, four, dma((fe // 256 + 1, 2)), four, dma((2, 8))],
+          + [dma((2, 3))] * 2 + [by_chunk, two, four, two, two, dma((2, 8))],
         compiler_params=pltpu.CompilerParams(collective_id=0, has_side_effects=True, vmem_limit_bytes=VMEM_LIMIT),
         cost_estimate=pl.CostEstimate(flops=2 * tokens * d_model * (heads * hd * RING + 12 * fe), bytes_accessed=24 * fe * d_model, transcendentals=heads * tokens * tokens),
         name='attn_moe',

time: 481 us -> 471 us (0.979)
  Pallas kernels: 472 us -> 462 us
    pallas_call x1, Pallas kernels: 227 us -> 216 us  [front_call(): pl.pallas_call(front_body, out_shape=(sds((tokens, d_model), BF16), sds((...]
where the time goes in v6:
time: 471 us; the launch traced here: 470 us
  Pallas kernels  462 us (98%)
  local copies, waits for them, and re-layouts  7.89 us (2%)
    pallas_call x1, Pallas kernels, ffn_call(): pl.pallas_call(functools.partial(ffn_body, fb), out_shape=jax.ShapeDtypeS...  245 us
    pallas_call x1, Pallas kernels, front_call(): pl.pallas_call(front_body, out_shape=(sds((tokens, d_model), BF16), sds((...  216 us

profile of v6, /device:TPU:97, one launch (start us, length us, event | category | flops | bytes accessed | tf_op | source)
XLA Modules:
  0.0 469.8 jit_solution(17363120968070730369)
XLA Ops:
  0.0 216.4 %attn_moe.1 = (bf16[1024,4096]{1,0:T(8,128)(2,1)}, f32[4,2,128,4096]{3,2,1,0:T(8,128)}, bf16[4,1024,1024]{2,1,0:T(8,128)(2,1)}, bf16[4,2,128,4096]{3,2,1,0:T(8,1...) custom-call(bf16[1024,4096]{1,0:T(8,128)(2,1)} %bitcast.17, ...), custom_call_target="tpu_custom_call" | custom-call | flops 103616086016 | bytes 67633152 | tf_op jit(solution)/shard_map/attn_moe/pallas_call | solution.py:792
  216.4 245.5 %ffn_ring.1 = bf16[1024,4096]{1,0:T(8,128)(2,1)} custom-call(bf16[1024,4096]{1,0:T(8,128)(2,1)} %get-tuple-element.7.a_ref, bf16[2752,4096]{1,0:T(8,128)(2,1)} %bitcast.13, bf16[2752,4096]{1,0:T(8,128)(2,1)} %bitcast.14, bf16[2752,4096]{1,0:T(8,128)(2,1)} %wd.1, bf16[4096]{0:T(1024)(128)(2,1)} %gain.1, f32[4,256,4096]{2,1,0:T(8,128)} %bitcast.21), custom_call_target="tpu_custom_call" | custom-call | flops 69256347648 | bytes 152043520 | tf_op jit(solution)/shard_map/ffn_ring/pallas_call | solution.py:328
  461.9 7.9 %copy.19 = bf16[1,1024,4096]{2,1,0:T(8,128)(2,1)} copy(bf16[1,1024,4096]{2,1,0:T(8,128)(2,1)} %bitcast.12) | data formatting | bytes 16777216

commit v7 on v6

--- a/solution.py
+++ b/solution.py
@@ -396,8 +396,7 @@
         return rcopy(w_cols.at[x_id(k)], w_cols.at[x_id(k)], wds.at[k], wdr.at[k], partner)
 
     def hid_send(part, side):
-        rows = pl.ds(pl.multiple_of(t * q + part * half, half), half)
-        return rcopy(x_ref.at[rows], hid_all.at[xc, part], hs.at[part, side], hr.at[part, side], x_dev(turn(side)))
+        return rcopy(hid_all.at[xc, part], hid_all.at[xc, part], hs.at[part, side], hr.at[part, side], x_dev(turn(side)))
 
     def hid_forward(part, side):
         ref = hid_all.at[ring(xc + 2 * side - 1), part, pl.ds(side * (half // 2), half // 2)]
@@ -448,14 +447,38 @@
     w_own = pltpu.make_async_copy(wo.at[window(e, hd), window(t, width)], w_cols.at[e, t], lsem.at[RING])
     ids_own = pltpu.make_async_copy(ids.at[:, window(t, q)], ids_all.at[xc], lsem.at[RING + 1])
 
-    def attention(rope, raw, wide, wb, qb, kb, vb):
+    def attention(rope, raw, wide, wide2, wb, qb, kb, vb, ub):
         proj = (wq, wk, wv)
-
         deep = raw.shape[0]
+        share = tokens // nk
+        step = min(16, share)
 
         def raw_load(m, k):
             slot = lax.rem(k, deep)
             return pltpu.make_async_copy(proj[m].at[window(k, kblk)], raw.at[slot], rawsem.at[slot])
+
+        def rows_of(m, k):
+            slot = lax.rem(k, deep)
+            part = kblk // 2
+            for i, buf in enumerate((wide, wide2)):
+                buf[...] = raw[slot, i * part:(i + 1) * part].astype(F32).reshape(part * heads, hd)
+            for i, buf in enumerate((wide, wide2)):
+                rows = pl.ds(pl.multiple_of(k * kblk + i * part, part), part)
+                for h in range(heads):
+                    wb[m, rows, h * hd:(h + 1) * hd] = buf[pl.ds(h, part, stride=heads), :].astype(BF16)
+
+        def raw_next(m, k):
+            @pl.when(k + deep < nk)
+            def _():
+                raw_load(m, k + deep).start()
+
+            if m + 1 < len(proj):
+                @pl.when(k + deep >= nk)
+                def _():
+                    raw_load(m + 1, k + deep - nk).start()
+
+        own = pltpu.make_async_copy(x_ref.at[window(t, q)], ub, lsem.at[RING + 2])
+        own.start()
         for k in range(deep):
             raw_load(0, k).start()
         entry_barrier((y_dev(1), y_dev(-1), y_dev(2), x_dev(1), x_dev(-1), x_dev(2), partner))
@@ -464,10 +487,14 @@
         for k in range(1, RING):
             w_swap(k).start()
             ids_send(k).start()
-        for side in SIDES:
-            hid_send(0, side).start()
         for i in range(len(mats)):
             swap_mat(0, i).start()
+
+        own.wait()
+        norm_rows(ub, ub, moe_gain, q, 16)
+        keep = [pltpu.make_async_copy(ub.at[pl.ds(part * half, half)], hid_all.at[xc, part], lsem.at[RING + 2 + part]) for part in SIDES]
+        for c in keep:
+            c.start()
 
         sign = jnp.where(lax.broadcasted_iota(jnp.int32, (1, hd), 1) < hd // 2, -1.0, 1.0)
         steps = min(128, tokens)
@@ -477,27 +504,33 @@
             rope[0, window(k, steps)] = jnp.cos(angle)
             rope[1, window(k, steps)] = jnp.sin(angle) * sign
         loop(tokens // steps, angles)
-
+        for c in keep:
+            c.wait()
+        for side in SIDES:
+            hid_send(0, side).start()
         for k in range(RING):
             load_x[k].wait()
-            norm_rows(xn.at[pl.ds(k * q, q)], xn.at[pl.ds(k * q, q)], attn_gain, q, 16)
 
         for m in range(len(proj)):
             def one(k, m=m):
                 raw_load(m, k).wait()
-                wide[...] = raw[lax.rem(k, deep)].astype(F32).reshape(kblk * heads, hd)
-
-                @pl.when(k + deep < nk)
-                def _():
-                    raw_load(m, k + deep).start()
-
-                if m + 1 < len(proj):
-                    @pl.when(k + deep >= nk)
-                    def _():
-                        raw_load(m + 1, k + deep - nk).start()
-                for h in range(heads):
-                    wb[m, window(k, kblk), h * hd:(h + 1) * hd] = wide[pl.ds(h, kblk, stride=heads), :].astype(BF16)
+                rows_of(m, k)
+                if m == 0:
+                    for i in range(0, share, step):
+                        rows = pl.ds(pl.multiple_of(k * share + i, step), step)
+                        x = xn[rows, :].astype(F32)
+                        inv = lax.rsqrt(jnp.mean(x * x, axis=-1, keepdims=True) + EPS)
+                        xn[rows, :] = (x * inv * attn_gain[...].astype(F32).reshape(1, -1)).astype(BF16)
+                raw_next(m, k)
             loop(nk, one)
+
+        def turned(r):
+            for h in SIDES:
+                part = r[:, h * hd:(h + 1) * hd]
+                yield (part * rope[0] + pltpu.roll(part, hd // 2, 1) * rope[1]).astype(BF16)
+
+        def project(m, g):
+            return jnp.dot(xn[...], wb[m, :, window(g, pair)], preferred_element_type=F32)
 
         w_own.wait()
         for k in range(1, RING):
@@ -510,15 +543,10 @@
         tri = lax.broadcasted_iota(jnp.int32, (q, q), 0) >= lax.broadcasted_iota(jnp.int32, (q, q), 1)
 
         def heads_of(g):
-            for m, dst in enumerate((qb, kb, vb)):
-                r = jnp.dot(xn[...], wb[m, :, window(g, pair)], preferred_element_type=F32)
-                if dst is vb:
-                    dst[...] = r.astype(BF16)
-                else:
-                    for h in SIDES:
-                        part = r[:, h * hd:(h + 1) * hd]
-                        turned = part * rope[0] + pltpu.roll(part, hd // 2, 1) * rope[1]
-                        dst[:, h * hd:(h + 1) * hd] = turned.astype(BF16)
+            for m, dst in enumerate((qb, kb)):
+                for h, part in enumerate(turned(project(m, g))):
+                    dst[:, h * hd:(h + 1) * hd] = part
+            vb[...] = project(2, g).astype(BF16)
             for h in SIDES:
                 hc = slice(h * hd, (h + 1) * hd)
                 for b in range(RING):
@@ -556,8 +584,8 @@
                     hid_send(1, side).start()
         loop(pairs, heads_of)
 
-    pl.run_scoped(attention, pltpu.VMEM((2, tokens, hd), F32), pltpu.VMEM((RING, kblk, heads, hd), BF16), pltpu.VMEM((kblk * heads, hd), F32),
-                  pltpu.VMEM((len(SIDES) + 1, d_model, heads * hd), BF16), *[pltpu.VMEM((tokens, pair), BF16)] * (len(SIDES) + 1))
+    pl.run_scoped(attention, pltpu.VMEM((2, tokens, hd), F32), pltpu.VMEM((RING, kblk, heads, hd), BF16), *[pltpu.VMEM((kblk // 2 * heads, hd), F32)] * 2,
+                  pltpu.VMEM((3, d_model, heads * hd), BF16), *[pltpu.VMEM((tokens, pair), BF16)] * 3, pltpu.VMEM((q, d_model), BF16))
 
     fb = 256 if fe > 512 else 128
     cw = min(512, d_model // 4)
@@ -602,19 +630,11 @@
 
         def u_ready(part):
             for k in range(RING):
-                @pl.when(k == xc)
-                def _():
-                    rows = pl.ds(pl.multiple_of(t * q + part * half, half), half)
-                    pltpu.make_async_copy(x_ref.at[rows], u_rows(part, k), usem.at[k]).start()
-
-                @pl.when(k != xc)
-                def _():
-                    pltpu.make_async_copy(hid_all.at[k, part], u_rows(part, k), usem.at[k]).start()
+                pltpu.make_async_copy(hid_all.at[k, part], u_rows(part, k), usem.at[k]).start()
             for k in range(RING):
                 pltpu.make_async_copy(hid_all.at[k, part], u_rows(part, k), usem.at[k]).wait()
             rows = RING * half
             u = xn.at[pl.ds(part * rows, rows)]
-            norm_rows(u, u, moe_gain, rows, 16)
             logits = lax.dot_general(u[...], router[...], NT, preferred_element_type=F32)
             lane = lax.broadcasted_iota(jnp.int32, logits.shape, 1).astype(F32)
             picks = jnp.concatenate([idf[k, :, part * half:(part + 1) * half].astype(F32) for k in range(RING)], axis=1).T
@@ -799,7 +819,7 @@
         scratch_shapes=[
             pltpu.VMEM((tokens, d_model), BF16), pltpu.VMEM((pairs, tokens, 2 * hd), BF16), pltpu.VMEM((RING, q, d_model // RING), BF16),
             pltpu.VMEM((2, tokens // 2, experts), F32), pltpu.VMEM((RING, 8, q), ids.dtype),
-            dma((RING + 2,)), four, dma((pairs,)), four,
+            dma((RING + RING,)), four, dma((pairs,)), four,
         ] + [by_pair] * RING + [by_chunk] * RING + [square] * RING + [three] * 2 + [two] * RING + [four] * 2 + [three] * 2
           + [dma((2, 3))] * 2 + [by_chunk, two, four, two, two, dma((2, 8))],
         compiler_params=pltpu.CompilerParams(collective_id=0, has_side_effects=True, vmem_limit_bytes=VMEM_LIMIT),
@@ -807,6 +827,16 @@
         name='attn_moe',
     )(x, wq, wk, wv, wo, eg, eu, ed, attn_gain, moe_gain, freq, ids, router)
     return outs[0], outs[1]
+
+
+def copy_body(src, dst):
+    dst[...] = src[...]
+
+
+def copy_out(x):
+    rows = x.shape[0] // 8
+    spec = pl.BlockSpec((rows, x.shape[1]), lambda i: (i, 0))
+    return pl.pallas_call(copy_body, out_shape=jax.ShapeDtypeStruct(x.shape, x.dtype), grid=(8,), in_specs=[spec], out_specs=spec, name='copy_out')(x)
 
 
 def solution(mesh):
@@ -824,6 +854,6 @@
             x, w_query, w_key, w_value, w_out.reshape(heads * head_dim, d_model), jnp.swapaxes(exp_gate, 1, 2), jnp.swapaxes(exp_up, 1, 2), exp_down,
             attn_gain, moe_gain, ids, w_router.T)
         out = ffn_call(after_attn, w_gate.T, w_up.T, w_down, ffn_gain, m_part.reshape(-1, tokens // 4, d_model))
-        return out.reshape(hidden_in.shape)
+        return copy_out(out).reshape(hidden_in.shape)
 
     return jax.shard_map(layer_local, mesh=mesh, in_specs=in_specs, out_specs=tok_spec, check_vma=False)

time: 471 us -> 464 us (0.985)
  local copies, waits for them, and re-layouts: 7.89 us -> 0 us
    pallas_call x1, Pallas kernels: 216 us -> 207 us  [front_call(): pl.pallas_call(front_body, out_shape=(sds((tokens, d_model), BF16), sds((...]
    pallas_call x0 -> x1, Pallas kernels: none -> 8.96 us  [copy_out(): pl.pallas_call(copy_body, out_shape=jax.ShapeDtypeStruct(x.shape, x.dtype...]
    unnamed x1 -> x0, local copies, waits for them, and re-layouts: 7.89 us -> none
where the time goes in v7:
time: 464 us; the launch traced here: 462 us
  Pallas kernels  462 us (100%)
    pallas_call x1, Pallas kernels, ffn_call(): pl.pallas_call(functools.partial(ffn_body, fb), out_shape=jax.ShapeDtypeS...  246 us
    pallas_call x1, Pallas kernels, front_call(): pl.pallas_call(front_body, out_shape=(sds((tokens, d_model), BF16), sds((...  207 us

profile of v7, /device:TPU:97, one launch (start us, length us, event | category | flops | bytes accessed | tf_op | source)
XLA Modules:
  0.0 461.9 jit_solution(11856718607768648720)
XLA Ops:
  0.0 206.8 %attn_moe.1 = (bf16[1024,4096]{1,0:T(8,128)(2,1)}, f32[4,2,128,4096]{3,2,1,0:T(8,128)}, bf16[4,1024,1024]{2,1,0:T(8,128)(2,1)}, bf16[4,2,128,4096]{3,2,1,0:T(8,1...) custom-call(bf16[1024,4096]{1,0:T(8,128)(2,1)} %bitcast.16, ...), custom_call_target="tpu_custom_call" | custom-call | flops 103616086016 | bytes 67633152 | tf_op jit(solution)/shard_map/attn_moe/pallas_call | solution.py:812
  206.9 246.0 %ffn_ring.1.src = bf16[1024,4096]{1,0:T(8,128)(2,1)} custom-call(bf16[1024,4096]{1,0:T(8,128)(2,1)} %get-tuple-element.7.a_ref, bf16[2752,4096]{1,0:T(8,128)(2,1)} %bitcast.12, bf16[2752,4096]{1,0:T(8,128)(2,1)} %bitcast.13, bf16[2752,4096]{1,0:T(8,128)(2,1)} %wd.1, bf16[4096]{0:T(1024)(128)(2,1)} %gain.1, f32[4,256,4096]{2,1,0:T(8,128)} %bitcast.20), custom_call_target="tpu_custom_call" | custom-call | flops 69256347648 | bytes 152043520 | tf_op jit(solution)/shard_map/ffn_ring/pallas_call | solution.py:328
  452.9 9.0 %copy_out.1 = bf16[1024,4096]{1,0:T(8,128)(2,1)} custom-call(bf16[1024,4096]{1,0:T(8,128)(2,1)} %ffn_ring.1.src), custom_call_target="tpu_custom_call" | custom-call | tf_op jit(solution)/shard_map/copy_out/pallas_call | solution.py:839

commit v8 on v7

--- a/solution.py
+++ b/solution.py
@@ -490,20 +490,20 @@
         for i in range(len(mats)):
             swap_mat(0, i).start()
 
+        sign = jnp.where(lax.broadcasted_iota(jnp.int32, (1, hd), 1) < hd // 2, -1.0, 1.0)
+        steps = min(128, tokens)
+
+        def angles(k):
+            angle = (lax.broadcasted_iota(jnp.int32, (steps, 1), 0) + k * steps).astype(F32) * freq[...]
+            rope[0, window(k, steps)] = jnp.cos(angle)
+            rope[1, window(k, steps)] = jnp.sin(angle) * sign
+        loop(tokens // steps, angles)
         own.wait()
         norm_rows(ub, ub, moe_gain, q, 16)
         keep = [pltpu.make_async_copy(ub.at[pl.ds(part * half, half)], hid_all.at[xc, part], lsem.at[RING + 2 + part]) for part in SIDES]
         for c in keep:
             c.start()
 
-        sign = jnp.where(lax.broadcasted_iota(jnp.int32, (1, hd), 1) < hd // 2, -1.0, 1.0)
-        steps = min(128, tokens)
-
-        def angles(k):
-            angle = (lax.broadcasted_iota(jnp.int32, (steps, 1), 0) + k * steps).astype(F32) * freq[...]
-            rope[0, window(k, steps)] = jnp.cos(angle)
-            rope[1, window(k, steps)] = jnp.sin(angle) * sign
-        loop(tokens // steps, angles)
         for c in keep:
             c.wait()
         for side in SIDES:
@@ -594,16 +594,11 @@
         sizes = [fb] * (fe // fb) + [fe % fb]
         cw = mv.shape[-1]
         nn = d_model // cw
-        passes = 4 * local
-        last = passes - 2
+        each = 2 * local
+        passes = 2 * each
 
         def expert_of(p):
-            late = p // last
-            return (1 - late) * lax.rem(p, 3) + late * 3
-
-        def half_of(p):
-            late = p // last
-            return (1 - late) * (p // 3) + late * (p - last)
+            return lax.rem(p, each)
 
         def w_load(k, own):
             k = k if own else k - local
@@ -628,11 +623,18 @@
         def u_rows(part, k):
             return xn.at[pl.ds(pl.multiple_of((part * RING + k) * half, half), half)]
 
+        def u_load(part, k):
+            return pltpu.make_async_copy(hid_all.at[k, part], u_rows(part, k), usem.at[k])
+
+        def u_start(part):
+            for side in SIDES:
+                hid_forward(part, side).wait_recv()
+            for k in range(RING):
+                u_load(part, k).start()
+
         def u_ready(part):
             for k in range(RING):
-                pltpu.make_async_copy(hid_all.at[k, part], u_rows(part, k), usem.at[k]).start()
-            for k in range(RING):
-                pltpu.make_async_copy(hid_all.at[k, part], u_rows(part, k), usem.at[k]).wait()
+                u_load(part, k).wait()
             rows = RING * half
             u = xn.at[pl.ds(part * rows, rows)]
             logits = lax.dot_general(u[...], router[...], NT, preferred_element_type=F32)
@@ -690,8 +692,9 @@
             ids_send(k).wait_recv()
         load_i = pltpu.make_async_copy(ids_all, idf.at[:, pl.ds(0, top_k)], lsem.at[RING + 1])
         load_i.start()
-        for side in SIDES:
-            hid_forward(0, side).wait_recv()
+        u_start(0)
+        for i in SIDES:
+            swap_mat(1, i).start()
         load_i.wait()
         u_ready(0)
 
@@ -702,8 +705,7 @@
                 for side in SIDES:
                     w_forward(side).wait_recv()
                 w_core(2).start()
-                for i in range(len(mats)):
-                    swap_mat(1, i).start()
+                swap_mat(1, 2).start()
 
             @pl.when(p == 2)
             def _():
@@ -719,14 +721,16 @@
                     hid_send(1, side).wait_recv()
                     hid_forward(1, side).start()
                 attention_out()
-                for side in SIDES:
-                    hid_forward(1, side).wait_recv()
+                u_start(1)
+
+            @pl.when(p == each)
+            def _():
                 u_ready(1)
 
             @pl.when(p >= RING)
             def _():
                 a_pass(p - RING)
-            k, part = expert_of(p), half_of(p)
+            k, part = expert_of(p), p // each
             which = (k // local) * ((e + 1 - 2 * core) * local + k - local) + (1 - k // local) * (e * local + k)
             rows = RING * half
             u = xn.at[pl.ds(pl.multiple_of(part * rows, rows), rows)]
@@ -734,7 +738,7 @@
             weight = jnp.sum(jnp.where(lane == which, gate[part], 0.0), axis=1, keepdims=True)
 
             def if_new(ahead, which_mats):
-                for late, when in enumerate((3, last + 1)):
+                for late, when in enumerate((3, 4)):
                     @pl.when(ahead == when)
                     def _():
                         for i in which_mats:
@@ -757,7 +761,7 @@
                 term = jnp.where(weight > 0.0, weight * y.astype(F32), 0.0).reshape(mv.shape[2:])
                 mv[part, n] = jnp.where(k == 0, term, mv[part, n] + term)
 
-            @pl.when(p >= last)
+            @pl.when(k == each - 1)
             def _():
                 loop(nn, lambda n: m_out(part, n).start())
         loop(passes, one_pass)
@@ -829,16 +833,6 @@
     return outs[0], outs[1]
 
 
-def copy_body(src, dst):
-    dst[...] = src[...]
-
-
-def copy_out(x):
-    rows = x.shape[0] // 8
-    spec = pl.BlockSpec((rows, x.shape[1]), lambda i: (i, 0))
-    return pl.pallas_call(copy_body, out_shape=jax.ShapeDtypeStruct(x.shape, x.dtype), grid=(8,), in_specs=[spec], out_specs=spec, name='copy_out')(x)
-
-
 def solution(mesh):
     tok_spec = P(('dp', 'ep'))
     col_spec = P(None, 'tp')
@@ -854,6 +848,6 @@
             x, w_query, w_key, w_value, w_out.reshape(heads * head_dim, d_model), jnp.swapaxes(exp_gate, 1, 2), jnp.swapaxes(exp_up, 1, 2), exp_down,
             attn_gain, moe_gain, ids, w_router.T)
         out = ffn_call(after_attn, w_gate.T, w_up.T, w_down, ffn_gain, m_part.reshape(-1, tokens // 4, d_model))
-        return copy_out(out).reshape(hidden_in.shape)
+        return out.reshape(hidden_in.shape)
 
     return jax.shard_map(layer_local, mesh=mesh, in_specs=in_specs, out_specs=tok_spec, check_vma=False)

time: 464 us -> 461 us (level)
  Pallas kernels: 462 us -> 452 us
  local copies, waits for them, and re-layouts: 0 us -> 7.89 us
    pallas_call x1 -> x0, Pallas kernels: 8.96 us -> none  [copy_out(): pl.pallas_call(copy_body, out_shape=jax.ShapeDtypeStruct(x.shape, x.dtype...]
    unnamed x0 -> x1, local copies, waits for them, and re-layouts: none -> 7.89 us
where the time goes in v8:
time: 461 us; the launch traced here: 460 us
  Pallas kernels  452 us (98%)
  local copies, waits for them, and re-layouts  7.89 us (2%)
    pallas_call x1, Pallas kernels, ffn_call(): pl.pallas_call(functools.partial(ffn_body, fb), out_shape=jax.ShapeDtypeS...  247 us
    pallas_call x1, Pallas kernels, front_call(): pl.pallas_call(front_body, out_shape=(sds((tokens, d_model), BF16), sds((...  205 us

profile of v8, /device:TPU:97, one launch (start us, length us, event | category | flops | bytes accessed | tf_op | source)
XLA Modules:
  0.0 459.6 jit_solution(6702482676989625514)
XLA Ops:
  0.0 204.5 %attn_moe.1 = (bf16[1024,4096]{1,0:T(8,128)(2,1)}, f32[4,2,128,4096]{3,2,1,0:T(8,128)}, bf16[4,1024,1024]{2,1,0:T(8,128)(2,1)}, bf16[4,2,128,4096]{3,2,1,0:T(8,1...) custom-call(bf16[1024,4096]{1,0:T(8,128)(2,1)} %bitcast.17, ...), custom_call_target="tpu_custom_call" | custom-call | flops 103616086016 | bytes 67633152 | tf_op jit(solution)/shard_map/attn_moe/pallas_call | solution.py:816
  204.5 247.2 %ffn_ring.1 = bf16[1024,4096]{1,0:T(8,128)(2,1)} custom-call(bf16[1024,4096]{1,0:T(8,128)(2,1)} %get-tuple-element.7.a_ref, bf16[2752,4096]{1,0:T(8,128)(2,1)} %bitcast.13, bf16[2752,4096]{1,0:T(8,128)(2,1)} %bitcast.14, bf16[2752,4096]{1,0:T(8,128)(2,1)} %wd.1, bf16[4096]{0:T(1024)(128)(2,1)} %gain.1, f32[4,256,4096]{2,1,0:T(8,128)} %bitcast.21), custom_call_target="tpu_custom_call" | custom-call | flops 69256347648 | bytes 152043520 | tf_op jit(solution)/shard_map/ffn_ring/pallas_call | solution.py:328
  451.8 7.9 %copy.19 = bf16[1,1024,4096]{2,1,0:T(8,128)(2,1)} copy(bf16[1,1024,4096]{2,1,0:T(8,128)(2,1)} %bitcast.12) | data formatting | bytes 16777216
